TPU v7x, 16 devices: a 4x2x1 block of a 4x4x8 slice. The times are simulated.
16 devices in a mesh: dp: 2 (over y, z), tp: 8 (over x, core).
Axes of the slice: x: 4, y: 2, z: 1, core: 2. Of those that a mesh axis runs over, the one named last changes fastest.
The devices are a block of a 4x4x8 slice.
Arguments:
- x: bfloat16 [64, 256, 1024], P('dp', 'tp'), parts along dimension 0
- d_out: bfloat16 [64, 256, 1024], P('dp', 'tp'), parts along dimension 0
- ln1_gain: float32 [1024], replicated
- ln1_bias: float32 [1024], replicated
- w_q: bfloat16 [1024, 16, 64], P(None, 'tp')
- b_q: bfloat16 [16, 64], P('tp')
- w_k: bfloat16 [1024, 16, 64], P(None, 'tp')
- w_v: bfloat16 [1024, 16, 64], P(None, 'tp')
- b_v: bfloat16 [16, 64], P('tp')
- w_o: bfloat16 [16, 64, 1024], P('tp')
- b_o: bfloat16 [1024], replicated
- ln2_gain: float32 [1024], replicated
- ln2_bias: float32 [1024], replicated
- w_1: bfloat16 [1024, 4096], P(None, 'tp')
- b_1: bfloat16 [4096], P('tp')
- w_2: bfloat16 [4096, 1024], P('tp')
- b_2: bfloat16 [1024], replicated
Outputs:
- output 1: bfloat16 [64, 256, 1024], P('dp', 'tp'), parts along dimension 0
- output 2: bfloat16 [64, 256, 1024], P('dp', 'tp'), parts along dimension 0
- output 3: float32 [2048], P('dp'), parts along dimension 0
- output 4: float32 [2048], P('dp'), parts along dimension 0
- output 5: bfloat16 [2048, 16, 64], P('dp', 'tp'), parts along dimension 0
- output 6: bfloat16 [32, 64], P(('dp', 'tp')), parts along dimension 0
- output 7: bfloat16 [2048, 16, 64], P('dp', 'tp'), parts along dimension 0
- output 8: bfloat16 [2048, 16, 64], P('dp', 'tp'), parts along dimension 0
- output 9: bfloat16 [32, 64], P(('dp', 'tp')), parts along dimension 0
- output 10: bfloat16 [32, 64, 1024], P(('dp', 'tp')), parts along dimension 0
- output 11: bfloat16 [2048], P('dp'), parts along dimension 0
- output 12: float32 [2048], P('dp'), parts along dimension 0
- output 13: float32 [2048], P('dp'), parts along dimension 0
- output 14: bfloat16 [2048, 4096], P('dp', 'tp'), parts along dimension 0
- output 15: bfloat16 [8192], P(('dp', 'tp')), parts along dimension 0
- output 16: bfloat16 [8192, 1024], P(('dp', 'tp')), parts along dimension 0
- output 17: bfloat16 [2048], P('dp'), parts along dimension 0
There are 2 independent parts. A program takes and returns all parts, laid end to end along the dimension named above; an argument that names none is the same for every part.
All inputs are finite; a program needn't handle non-finite values.
Results may differ from a plain program's by a relative error of at most 0.0185995.
Values are sent between devices in bfloat16 or wider.
A program may use at most 768 MiB of HBM per device.

v0:
```python
import math
import jax
import jax.numpy as jnp
from jax import lax
from jax.sharding import PartitionSpec as P

LN_EPS = 1e-6


def layer_norm(rows, ln_gain, ln_bias):
    row_mean = jnp.mean(rows, axis=-1, keepdims=True)
    centered = rows - row_mean
    variance = jnp.mean(centered * centered, axis=-1, keepdims=True)
    return centered * lax.rsqrt(variance + LN_EPS) * ln_gain + ln_bias


def gelu_tanh(pre_act):
    return jax.nn.gelu(pre_act, approximate=True)


def attention_core(queries, keys, values):
    att_scale = 1.0 / math.sqrt(queries.shape[-1])
    scores = jnp.einsum('bqhd,bkhd->bhqk', queries, keys, preferred_element_type=jnp.float32) * att_scale
    probs = jax.nn.softmax(scores, axis=-1).astype(jnp.bfloat16)
    mixed = jnp.einsum('bhqk,bkhd->bqhd', probs, values, preferred_element_type=jnp.float32)
    return mixed.astype(jnp.bfloat16)


def token_sum(grad_rows):
    return jnp.sum(grad_rows, axis=(0, 1), dtype=jnp.float32)


def solution(mesh):
    act_spec = P('dp', 'tp', None)
    replicated = P()
    head_w = P(None, 'tp', None)
    head_b = P('tp', None)
    grad_head_w = P('dp', 'tp', None)
    grad_head_b = P(('dp', 'tp'), None)
    grad_vec = P('dp')
    in_specs = (act_spec, act_spec, replicated, replicated, head_w, head_b, head_w, head_w, head_b,
                P('tp', None, None), replicated, replicated, replicated, P(None, 'tp'), P('tp'), P('tp', None), replicated)
    out_specs = (act_spec, act_spec, grad_vec, grad_vec, grad_head_w, grad_head_b, grad_head_w, grad_head_w, grad_head_b,
                 P(('dp', 'tp'), None, None), grad_vec, grad_vec, grad_vec, P('dp', 'tp'), P(('dp', 'tp')),
                 P(('dp', 'tp'), None), grad_vec)

    def gather_tokens(local_rows):
        return lax.all_gather(local_rows, 'tp', axis=1, tiled=True)

    def scatter_sum(part_sum):
        return lax.psum_scatter(part_sum, 'tp', scatter_dimension=1, tiled=True)

    def layer_step(x, d_out, ln1_gain, ln1_bias, w_q, b_q, w_k, w_v, b_v, w_o, b_o, ln2_gain, ln2_bias, w_1, b_1, w_2, b_2):
        x_f32 = x.astype(jnp.float32)
        h_one_f, ln1_pull = jax.vjp(layer_norm, x_f32, ln1_gain, ln1_bias)
        h_one = gather_tokens(h_one_f.astype(jnp.bfloat16))
        queries = (jnp.einsum('bnw,whd->bnhd', h_one, w_q, preferred_element_type=jnp.float32) + b_q).astype(jnp.bfloat16)
        keys = jnp.einsum('bnw,whd->bnhd', h_one, w_k, preferred_element_type=jnp.float32).astype(jnp.bfloat16)
        values = (jnp.einsum('bnw,whd->bnhd', h_one, w_v, preferred_element_type=jnp.float32) + b_v).astype(jnp.bfloat16)
        mixed, attn_pull = jax.vjp(attention_core, queries, keys, values)
        attn_out = scatter_sum(jnp.einsum('bnhd,hdw->bnw', mixed, w_o, preferred_element_type=jnp.float32))
        x_mid = (x_f32 + attn_out + b_o).astype(jnp.bfloat16)
        mid_f32 = x_mid.astype(jnp.float32)
        h_two_f, ln2_pull = jax.vjp(layer_norm, mid_f32, ln2_gain, ln2_bias)
        h_two = gather_tokens(h_two_f.astype(jnp.bfloat16))
        pre_act = (jnp.einsum('bnw,wf->bnf', h_two, w_1, preferred_element_type=jnp.float32) + b_1).astype(jnp.bfloat16)
        hidden_f, gelu_pull = jax.vjp(gelu_tanh, pre_act.astype(jnp.float32))
        hidden = hidden_f.astype(jnp.bfloat16)
        mlp_out = scatter_sum(jnp.einsum('bnf,fw->bnw', hidden, w_2, preferred_element_type=jnp.float32))
        y_out = (mid_f32 + mlp_out + b_2).astype(jnp.bfloat16)

        d_out_all = gather_tokens(d_out)
        d_hidden = jnp.einsum('bnw,fw->bnf', d_out_all, w_2, preferred_element_type=jnp.float32).astype(jnp.bfloat16)
        grad_w_2 = jnp.einsum('bnf,bnw->fw', hidden, d_out_all, preferred_element_type=jnp.float32).astype(jnp.bfloat16)
        (d_pre_f,) = gelu_pull(d_hidden.astype(jnp.float32))
        d_pre = d_pre_f.astype(jnp.bfloat16)
        grad_b_1 = token_sum(d_pre).astype(jnp.bfloat16)
        grad_w_1 = jnp.einsum('bnw,bnf->wf', h_two, d_pre, preferred_element_type=jnp.float32).astype(jnp.bfloat16)
        d_h_two = scatter_sum(jnp.einsum('bnf,wf->bnw', d_pre, w_1, preferred_element_type=jnp.float32)).astype(jnp.bfloat16)
        d_mid_ln, g_ln2_gain, g_ln2_bias = ln2_pull(d_h_two.astype(jnp.float32))
        d_mid = (d_out.astype(jnp.float32) + d_mid_ln).astype(jnp.bfloat16)
        d_mid_all = gather_tokens(d_mid)
        d_mixed = jnp.einsum('bnw,hdw->bnhd', d_mid_all, w_o, preferred_element_type=jnp.float32).astype(jnp.bfloat16)
        grad_w_o = jnp.einsum('bnhd,bnw->hdw', mixed, d_mid_all, preferred_element_type=jnp.float32).astype(jnp.bfloat16)
        d_query, d_key, d_value = attn_pull(d_mixed)
        grad_b_q = token_sum(d_query).astype(jnp.bfloat16)
        grad_b_v = token_sum(d_value).astype(jnp.bfloat16)
        grad_w_q = jnp.einsum('bnw,bnhd->whd', h_one, d_query, preferred_element_type=jnp.float32).astype(jnp.bfloat16)
        grad_w_k = jnp.einsum('bnw,bnhd->whd', h_one, d_key, preferred_element_type=jnp.float32).astype(jnp.bfloat16)
        grad_w_v = jnp.einsum('bnw,bnhd->whd', h_one, d_value, preferred_element_type=jnp.float32).astype(jnp.bfloat16)
        d_h_one_part = (jnp.einsum('bnhd,whd->bnw', d_query, w_q, preferred_element_type=jnp.float32)
                        + jnp.einsum('bnhd,whd->bnw', d_key, w_k, preferred_element_type=jnp.float32)
                        + jnp.einsum('bnhd,whd->bnw', d_value, w_v, preferred_element_type=jnp.float32))
        d_h_one = scatter_sum(d_h_one_part).astype(jnp.bfloat16)
        d_in_ln, g_ln1_gain, g_ln1_bias = ln1_pull(d_h_one.astype(jnp.float32))
        grad_x = (d_mid.astype(jnp.float32) + d_in_ln).astype(jnp.bfloat16)
        vec_sums = lax.psum(jnp.stack([g_ln1_gain, g_ln1_bias, token_sum(d_mid), g_ln2_gain, g_ln2_bias, token_sum(d_out)]), 'tp')
        return (y_out, grad_x, vec_sums[0], vec_sums[1], grad_w_q, grad_b_q, grad_w_k, grad_w_v, grad_b_v, grad_w_o,
                vec_sums[2].astype(jnp.bfloat16), vec_sums[3], vec_sums[4], grad_w_1, grad_b_1, grad_w_2,
                vec_sums[5].astype(jnp.bfloat16))

    return jax.shard_map(layer_step, mesh=mesh, in_specs=in_specs, out_specs=out_specs, check_vma=False)
```

profile of v0, /device:TPU:112, one launch (start us, length us, event | category | flops | bytes accessed | tf_op | source)
XLA Modules:
  0.0 1302.2 jit_solution(2280335901751584387)
XLA Ops:
  7.3 2.1 convert_reduce_fusion.3
  9.5 2.3 fusion.55
  11.8 0.6 copy-done.33
  12.4 0.6 copy-done.29
  13.0 2.1 fusion.52
  15.3 0.1 reduce-scatter.5.cloned.1.call-start
  15.4 84.0 %all-gather.5.cloned.1.call-done = bf16[32,256,1024]{2,1,0:T(8,128)(2,1)} async-done(((bf16[32,32,1024]{2,1,0:T(8,128)(2,1)}), bf16[32,256,1024]{2,1,0:T(8,128)(2,1)}) %all-gather.5.cloned.1.call-update) | async-done | bytes 16777232 | tf_op jit(solution)/shard_map/all_gather | solution.py:48
  99.4 12.9 fusion.87
  112.2 7.0 add_convert_fusion.1
  119.2 10.9 fusion.159
  130.1 6.8 divide_convert_fusion
  137.0 14.5 %add_convert_fusion.2 = bf16[32,256,2,64]{1,3,2,0:T(8,128)(2,1)S(1)} fusion(f32[2,64]{1,0:T(2,128)S(1)} %convert_element_type.161, bf16[32,256,1024]{2,1,0:T(8,128)(2,1)} %all-gather.5.cloned.1.call-done, bf16[1024,2,64]{0,2,1:T(8,128)(2,1)S(1)} %copy-done.27), kind=kOutput, calls=%fused_computation.98 | convolution fusion | flops 2149580800 | bytes 19137024 | tf_op jit(solution)/shard_map/bnw,whd->bnhd/dot_general | solution.py:59
  151.5 1.6 convolution_convert_fusion.3
  153.1 1.3 copy-done.7
  154.4 13.1 %convolution_bitcast_fusion = f32[32,256,1024]{2,1,0:T(8,128)} fusion(bf16[32,2,64,256]{3,2,1,0:T(8,128)(2,1)S(1)} %convolution_convert_fusion.3, bf16[2,64,1024]{2,1,0:T(8,128)(2,1)S(1)} %copy-done.21), kind=kOutput, calls=%fused_computation.48 | convolution fusion | flops 2147483648 | bytes 35913728 | tf_op jit(solution)/shard_map/bnhd,hdw->bnw/dot_general | solution.py:61
  167.6 0.5 all-gather.7.cloned.1.call-start
  168.1 0.1 copy-done.44
  168.2 166.5 %reduce-scatter.5.cloned.1.call-done = f32[32,32,1024]{2,1,0:T(8,128)} async-done(((f32[32,256,1024]{2,1,0:T(8,128)}), f32[32,32,1024]{2,1,0:T(8,128)}) %reduce-scatter.5.cloned.1.call-update) | async-done | bytes 4194320 | tf_op jit(solution)/shard_map/reduce_scatter | solution.py:51
  334.7 2.9 convert_reduce_fusion.2
  337.6 0.7 fusion.59
  338.3 0.6 copy-done.5
  338.9 2.1 fusion.50
  341.1 0.1 all-gather.9.cloned.1.call-start
  341.2 0.6 all-gather.9.cloned.1.call-update
  341.8 80.2 %all-gather.7.cloned.1.call-done = bf16[32,256,1024]{2,1,0:T(8,128)(2,1)} async-done(((bf16[32,32,1024]{2,1,0:T(8,128)(2,1)}), bf16[32,256,1024]{2,1,0:T(8,128)(2,1)}) %all-gather.7.cloned.1.call-update) | async-done | bytes 16777232 | tf_op jit(solution)/shard_map/all_gather | solution.py:48
  422.0 16.9 %add_convert_fusion = bf16[32,256,512]{2,1,0:T(8,128)(2,1)} fusion(f32[512]{0:T(512)S(1)} %convert_element_type.173, bf16[32,256,1024]{2,1,0:T(8,128)(2,1)} %all-gather.7.cloned.1.call-done, bf16[1024,512]{1,0:T(8,128)(2,1)S(1)} %copy-done.48), kind=kOutput, calls=%fused_computation.43 | convolution fusion | flops 8598323200 | bytes 26216448 | tf_op jit(solution)/shard_map/bnw,wf->bnf/dot_general | solution.py:66
  438.9 66.2 %all-gather.9.cloned.1.call-done = bf16[32,256,1024]{2,1,0:T(8,128)(2,1)} async-done(((bf16[32,32,1024]{2,1,0:T(8,128)(2,1)}), bf16[32,256,1024]{2,1,0:T(8,128)(2,1)}) %all-gather.9.cloned.1.call-update) | async-done | bytes 16777232 | tf_op jit(solution)/shard_map/all_gather | solution.py:48
  505.1 27.5 %fusion.160 = (bf16[512]{0:T(512)(128)(2,1)}, bf16[32,256,512]{2,1,0:T(8,128)(2,1)}) fusion(bf16[32,256,512]{2,1,0:T(8,128)(2,1)} %add_convert_fusion, bf16[32,256,1024]{2,1,0:T(8,128)(2,1)} %all-gather.9.cloned.1.call-done, bf16[512,1024]{1,0:T(8,128)(2,1)S(1)} %copy-done), kind=kOutput, calls=%fused_computation.163 | convolution fusion | flops 8690597888 | bytes 34604032 | tf_op jit(solution)/shard_map/bnw,fw->bnf/dot_general | solution.py:73
  532.6 19.0 %fusion.138 = f32[32,256,1024]{2,1,0:T(8,128)} fusion(bf16[32,256,512]{2,1,0:T(8,128)(2,1)} %get-tuple-element.48, bf16[1024,512]{1,0:T(8,128)(2,1)S(1)} %copy-done.48), kind=kOutput, calls=%fused_computation.136 | convolution fusion | flops 8589934592 | bytes 42991616 | tf_op jit(solution)/shard_map/bnf,wf->bnw/dot_general | solution.py:79
  551.7 0.1 reduce-scatter.7.cloned.1.call-start
  551.7 19.0 %fusion.136 = f32[32,256,1024]{2,1,0:T(8,128)} fusion(bf16[512,1024]{1,0:T(8,128)(2,1)S(1)} %copy-done, bf16[32,256,512]{2,1,0:T(8,128)(2,1)} %add_convert_fusion), kind=kOutput, calls=%fused_computation.134 | convolution fusion | flops 8631877632 | bytes 42991616 | tf_op jit(solution)/shard_map/bnf,fw->bnw/dot_general | solution.py:69
  570.8 0.1 all-gather.11.cloned.1.call-start
  570.9 0.5 copy-done.45
  571.5 147.3 %reduce-scatter.9.cloned.1.call-done = f32[32,32,1024]{2,1,0:T(8,128)} async-done(((f32[32,256,1024]{2,1,0:T(8,128)}), f32[32,32,1024]{2,1,0:T(8,128)}) %reduce-scatter.9.cloned.1.call-update) | async-done | bytes 4194320 | tf_op jit(solution)/shard_map/reduce_scatter | solution.py:51
  718.8 3.9 convert_reduce_fusion.1
  722.6 1.3 copy-done.10
  723.9 3.5 fusion.63
  727.5 159.6 %reduce-scatter.7.cloned.1.call-done = f32[32,32,1024]{2,1,0:T(8,128)} async-done(((f32[32,256,1024]{2,1,0:T(8,128)}), f32[32,32,1024]{2,1,0:T(8,128)}) %reduce-scatter.7.cloned.1.call-update) | async-done | bytes 4194320 | tf_op jit(solution)/shard_map/reduce_scatter | solution.py:51
  887.1 6.6 convert_reduce_fusion.4
  893.8 0.1 reduce-scatter.11.cloned.1.call-start
  893.9 80.8 %all-gather.11.cloned.1.call-done = bf16[32,256,1024]{2,1,0:T(8,128)(2,1)} async-done(((bf16[32,32,1024]{2,1,0:T(8,128)(2,1)}), bf16[32,256,1024]{2,1,0:T(8,128)(2,1)}) %all-gather.11.cloned.1.call-update) | async-done | bytes 16777232 | tf_op jit(solution)/shard_map/all_gather | solution.py:48
  974.7 11.3 fusion.90
  986.0 1.4 copy-done.14
  987.4 6.6 bitcast_reduce_fusion
  994.0 13.9 %fusion.9 = (f32[32,2,256]{2,1,0:T(2,128)S(1)}, bf16[32,2,256,256]{2,3,1,0:T(8,128)(2,1)}) fusion(f32[32,2,256,256]{2,3,1,0:T(8,128)} %get-tuple-element.40, f32[32,2,256]{2,1,0:T(2,128)S(1)} %multiply_divide_fusion, bf16[32,256,2,64]{1,3,2,0:T(8,128)(2,1)} %copy-done.13, bf16[32,256,2,64]{1,3,2,0:T(8,128)(2,1)} %copy-done.14), kind=kOutput, calls=%fused_computation.19 | convolution fusion | flops 557826048 | bytes 29491200 | tf_op jit(solution)/shard_map/transpose(jvp(bhqk,bkhd->bqhd))/dot_general | solution.py:25
  1008.0 11.2 convolution_convert_fusion.1
  1019.3 11.4 bitcast_reduce_fusion.1
  1030.6 13.1 %fusion.70 = f32[32,256,1024,1]{2,1,3,0:T(8,128)} fusion(bf16[32,2,256,64]{2,3,1,0:T(8,128)(2,1)S(1)} %convolution_convert_fusion.1, bf16[1024,2,64]{0,2,1:T(8,128)(2,1)S(1)} %copy-done.24), kind=kOutput, calls=%fused_computation.107 | convolution fusion | flops 2147483648 | bytes 35913728 | tf_op jit(solution)/shard_map/bnhd,whd->bnw/dot_general | solution.py:92
  1043.7 13.1 %fusion.73 = f32[32,256,1024,1]{2,1,3,0:T(8,128)} fusion(bf16[32,2,256,64]{2,3,1,0:T(8,128)(2,1)S(1)} %get-tuple-element.44, bf16[1024,2,64]{0,2,1:T(8,128)(2,1)S(1)} %copy-done.26), kind=kOutput, calls=%fused_computation.111 | convolution fusion | flops 2147483648 | bytes 35913728 | tf_op jit(solution)/shard_map/bnhd,whd->bnw/dot_general | solution.py:91
  1056.9 33.9 %bitcast_add_fusion = f32[32,256,1024]{2,1,0:T(8,128)} fusion(f32[32,256,1024,1]{2,1,3,0:T(8,128)} %fusion.70, f32[32,256,1024,1]{2,1,3,0:T(8,128)} %fusion.73, bf16[32,2,64,256]{3,2,1,0:T(8,128)(2,1)S(1)} %get-tuple-element.46, bf16[1024,2,64]{0,2,1:T(8,128)(2,1)S(1)} %copy-done.28), kind=kOutput, calls=%fused_computation.1 | convolution fusion | flops 2164260864 | bytes 103022592 | tf_op jit(solution)/shard_map/bnhd,whd->bnw/dot_general | solution.py:93
  1090.9 15.7 %bitcast_convert_fusion.1 = bf16[1024,512]{1,0:T(8,128)(2,1)} fusion(bf16[32,256,1024]{2,1,0:T(8,128)(2,1)} %all-gather.7.cloned.1.call-done, bf16[32,256,512]{2,1,0:T(8,128)(2,1)} %get-tuple-element.48), kind=kOutput, calls=%fused_computation.102 | convolution fusion | flops 8590458880 | bytes 26214400 | tf_op jit(solution)/shard_map/bnw,bnf->wf/dot_general | solution.py:78
  1106.6 18.0 %bitcast_convert_fusion = bf16[512,1024]{1,0:T(8,128)(2,1)} fusion(bf16[32,256,1024]{2,1,0:T(8,128)(2,1)} %all-gather.9.cloned.1.call-done, bf16[32,256,512]{2,1,0:T(8,128)(2,1)} %add_convert_fusion), kind=kOutput, calls=%fused_computation.101 | convolution fusion | flops 8632401920 | bytes 26214400 | tf_op jit(solution)/shard_map/bnf,bnw->fw/dot_general | solution.py:74
  1124.8 3.0 fusion.115
  1127.8 9.0 fusion.120
  1136.9 9.0 fusion.130
  1146.0 3.0 fusion.125
  1149.0 108.9 %reduce-scatter.11.cloned.1.call-done = f32[32,32,1024]{2,1,0:T(8,128)} async-done(((f32[32,256,1024]{2,1,0:T(8,128)}), f32[32,32,1024]{2,1,0:T(8,128)}) %reduce-scatter.11.cloned.1.call-update) | async-done | bytes 4194320 | tf_op jit(solution)/shard_map/reduce_scatter | solution.py:51
  1257.9 3.3 convert_reduce_fusion
  1261.3 1.2 copy-done.9
  1262.5 2.5 fusion.64
  1265.1 24.2 %psum.7 = f32[6,1024]{1,0:T(8,128)S(1)} all-reduce(f32[6,1024]{1,0:T(8,128)S(1)} %stack.27), channel_id=1, replica_groups=mesh['dp'=2,'tp'=8] {'tp'}, use_global_device_ids=true, to_apply=%region_21.0 | all-reduce | flops 6144 | bytes 49152 | tf_op jit(solution)/shard_map/psum | solution.py:97
  1289.3 0.6 fusion.158
  1289.9 0.6 slice_reduce_fusion
  1290.5 4.4 fusion.54
  (139 shorter events, 1.0 us)
Async XLA Ops:
  7.2 497.9 %copy-start = (bf16[512,1024]{1,0:T(8,128)(2,1)S(1)}, bf16[512,1024]{1,0:T(8,128)(2,1)}, u32[]{:S(2)}) copy-start(bf16[512,1024]{1,0:T(8,128)(2,1)} %param.32) | copy-start | bytes 3145732
  7.2 5.8 copy-start.3
  7.2 5.8 copy-start.36
  7.2 5.8 copy-start.42
  7.3 92.1 %all-gather.5.cloned.1.call-start = ((), (), s32[]{:S(2)}) async-start(), calls=%async_computation.4 | async-start | bytes 18874368 | tf_op jit(solution)/shard_map/all_gather | solution.py:48
  9.4 3.0 copy-start.19
  9.4 5.9 copy-start.49
  9.4 5.9 copy-start.50
  9.5 89.9 %copy-start.23 = (bf16[1024,2,64]{0,2,1:T(8,128)(2,1)S(1)}, bf16[1024,2,64]{0,2,1:T(8,128)(2,1)}, u32[]{:S(2)}) copy-start(bf16[1024,2,64]{0,2,1:T(8,128)(2,1)} %param.23) | copy-start | bytes 786436
  15.3 319.4 %reduce-scatter.5.cloned.1.call-start = ((), (), s32[]{:S(2)}) async-start(), calls=%async_computation.5 | async-start | bytes 37748736 | tf_op jit(solution)/shard_map/reduce_scatter | solution.py:51
  99.4 12.9 copy-start.25
  99.4 12.9 copy-start.47
  130.1 6.8 copy-start.31
  130.1 6.8 copy-start.27
  136.9 14.5 %copy-start.2 = (bf16[32,2,256,256]{2,3,1,0:T(8,128)(2,1)}, bf16[32,2,256,256]{2,3,1,0:T(8,128)(2,1)S(1)}, u32[]{:S(2)}) copy-start(bf16[32,2,256,256]{2,3,1,0:T(8,128)(2,1)S(1)} %divide_convert_fusion) | copy-start | bytes 25165828
  151.4 1.6 copy-start.13
  151.5 3.0 copy-start.21
  153.0 1.4 copy-start.7
  167.6 254.4 %all-gather.7.cloned.1.call-start = ((), (), s32[]{:S(2)}) async-start(), calls=%async_computation.6 | async-start | bytes 18874368 | tf_op jit(solution)/shard_map/all_gather | solution.py:48
  168.2 170.7 %copy-start.35 = (f32[1024]{0:T(1024)S(1)}, f32[1024]{0:T(1024)}, u32[]{:S(2)}) copy-start(f32[1024]{0:T(1024)} %param.28) | copy-start | bytes 12292
  168.2 170.7 %copy-start.43 = (f32[1024]{0:T(1024)S(1)}, f32[1024]{0:T(1024)}, u32[]{:S(2)}) copy-start(f32[1024]{0:T(1024)} %param.29) | copy-start | bytes 12292
  337.6 1.3 copy-start.5
  338.9 2.9 copy-start.46
  338.9 83.1 %copy-start.48 = (bf16[1024,512]{1,0:T(8,128)(2,1)S(1)}, bf16[1024,512]{1,0:T(8,128)(2,1)}, u32[]{:S(2)}) copy-start(bf16[1024,512]{1,0:T(8,128)(2,1)} %param.30) | copy-start | bytes 3145732
  341.1 164.0 %all-gather.9.cloned.1.call-start = ((), (), s32[]{:S(2)}) async-start(), calls=%async_computation.8 | async-start | bytes 18874368 | tf_op jit(solution)/shard_map/all_gather | solution.py:48
  341.7 377.0 %reduce-scatter.9.cloned.1.call-start = ((), (), s32[]{:S(2)}) async-start(), calls=%async_computation.9 | async-start | bytes 37748736 | tf_op jit(solution)/shard_map/reduce_scatter | solution.py:51
  551.7 335.4 %reduce-scatter.7.cloned.1.call-start = ((), (), s32[]{:S(2)}) async-start(), calls=%async_computation.7 | async-start | bytes 37748736 | tf_op jit(solution)/shard_map/reduce_scatter | solution.py:51
  570.8 148.0 %copy-start.6 = (bf16[32,32,1024]{2,1,0:T(8,128)(2,1)S(1)}, bf16[32,32,1024]{2,1,0:T(8,128)(2,1)}, u32[]{:S(2)}) copy-start(bf16[32,32,1024]{2,1,0:T(8,128)(2,1)} %copy-done.5) | copy-start | bytes 6291460
  570.8 403.8 %all-gather.11.cloned.1.call-start = ((), (), s32[]{:S(2)}) async-start(), calls=%async_computation.10 | async-start | bytes 18874368 | tf_op jit(solution)/shard_map/all_gather | solution.py:48
  722.6 1.3 copy-start.10
  727.5 166.4 %copy-start.32 = (f32[32,2,256]{2,1,0:T(2,128)S(1)}, f32[32,2,256]{2,1,0:T(2,128)}, u32[]{:S(2)}) copy-start(f32[32,2,256]{2,1,0:T(2,128)} %copy-done.31) | copy-start | bytes 196612
  727.5 247.2 %copy-start.22 = (bf16[2,64,1024]{2,1,0:T(8,128)(2,1)S(1)}, bf16[2,64,1024]{2,1,0:T(8,128)(2,1)}, u32[]{:S(2)}) copy-start(bf16[2,64,1024]{2,1,0:T(8,128)(2,1)} %param.26) | copy-start | bytes 786436
  893.8 364.2 %reduce-scatter.11.cloned.1.call-start = ((), (), s32[]{:S(2)}) async-start(), calls=%async_computation.11 | async-start | bytes 37748736 | tf_op jit(solution)/shard_map/reduce_scatter | solution.py:51
  986.0 1.4 copy-start.14
  994.0 62.9 %copy-start.11 = (bf16[32,2,64,256]{3,2,1,0:T(8,128)(2,1)}, bf16[32,2,64,256]{3,2,1,0:T(8,128)(2,1)S(1)}, u32[]{:S(2)}) copy-start(bf16[32,2,64,256]{3,2,1,0:T(8,128)(2,1)S(1)} %get-tuple-element.46) | copy-start | bytes 6291460
  1008.0 11.2 copy-start.51
  1019.2 11.4 copy-start.15
  1019.2 11.4 copy-start.24
  1030.6 13.1 %copy-start.17 = (bf16[32,2,256,64]{2,3,1,0:T(8,128)(2,1)}, bf16[32,2,256,64]{2,3,1,0:T(8,128)(2,1)S(1)}, u32[]{:S(2)}) copy-start(bf16[32,2,256,64]{2,3,1,0:T(8,128)(2,1)S(1)} %get-tuple-element.44) | copy-start | bytes 6291460
  1030.6 13.1 %copy-start.26 = (bf16[1024,2,64]{0,2,1:T(8,128)(2,1)S(1)}, bf16[1024,2,64]{0,2,1:T(8,128)(2,1)}, u32[]{:S(2)}) copy-start(bf16[1024,2,64]{0,2,1:T(8,128)(2,1)} %param.21) | copy-start | bytes 786436
  1043.7 13.1 %copy-start.28 = (bf16[1024,2,64]{0,2,1:T(8,128)(2,1)S(1)}, bf16[1024,2,64]{0,2,1:T(8,128)(2,1)}, u32[]{:S(2)}) copy-start(bf16[1024,2,64]{0,2,1:T(8,128)(2,1)} %param.24) | copy-start | bytes 786436
  1090.9 33.8 %slice-start = ((s8[16777216]{0:T(1024)(128)(4,1)}), s8[4194304]{0:T(1024)(128)(4,1)S(1)}, s32[]{:S(2)}) async-start(s8[16777216]{0:T(1024)(128)(4,1)} %bitcast.200), calls=%async_computation.12 | async-start | bytes 8388608
  1090.9 33.8 %slice-start.1 = ((s8[16777216]{0:T(1024)(128)(4,1)}), s8[4194304]{0:T(1024)(128)(4,1)S(1)}, s32[]{:S(2)}) async-start(s8[16777216]{0:T(1024)(128)(4,1)} %bitcast.200), calls=%async_computation.13 | async-start | bytes 8388608
  1106.6 18.1 %copy-start.8 = (bf16[32,2,64,256]{3,2,1,0:T(8,128)(2,1)S(1)}, bf16[32,2,64,256]{3,2,1,0:T(8,128)(2,1)}, u32[]{:S(2)}) copy-start(bf16[32,2,64,256]{3,2,1,0:T(8,128)(2,1)} %copy-done.7) | copy-start | bytes 6291460
  1106.6 18.1 %slice-start.2 = ((s8[16777216]{0:T(1024)(128)(4,1)}), s8[4194304]{0:T(1024)(128)(4,1)S(1)}, s32[]{:S(2)}) async-start(s8[16777216]{0:T(1024)(128)(4,1)} %bitcast.200), calls=%async_computation.14 | async-start | bytes 8388608
  1106.6 18.1 %slice-start.3 = ((s8[16777216]{0:T(1024)(128)(4,1)}), s8[4194304]{0:T(1024)(128)(4,1)S(1)}, s32[]{:S(2)}) async-start(s8[16777216]{0:T(1024)(128)(4,1)} %bitcast.200), calls=%async_computation.15 | async-start | bytes 8388608
  1124.7 3.1 copy-start.12
  1127.8 9.1 copy-start.18
  1127.8 18.1 %slice-start.4 = ((s8[16777216]{0:T(1024)(128)(4,1)}), s8[4194304]{0:T(1024)(128)(4,1)S(1)}, s32[]{:S(2)}) async-start(s8[16777216]{0:T(1024)(128)(4,1)} %bitcast.212), calls=%async_computation.16 | async-start | bytes 8388608
  1127.8 18.1 %slice-start.5 = ((s8[16777216]{0:T(1024)(128)(4,1)}), s8[4194304]{0:T(1024)(128)(4,1)S(1)}, s32[]{:S(2)}) async-start(s8[16777216]{0:T(1024)(128)(4,1)} %bitcast.212), calls=%async_computation.17 | async-start | bytes 8388608
  1136.9 9.1 copy-start.16
  1136.9 9.1 slice-start.6
  1136.9 9.1 slice-start.7
  1146.0 112.0 %copy-start.4 = (bf16[32,32,1024]{2,1,0:T(8,128)(2,1)S(1)}, bf16[32,32,1024]{2,1,0:T(8,128)(2,1)}, u32[]{:S(2)}) copy-start(bf16[32,32,1024]{2,1,0:T(8,128)(2,1)} %param.17) | copy-start | bytes 6291460
  1146.0 112.0 %copy-start.20 = (f32[32,32]{1,0:T(8,128)S(1)}, f32[32,32]{1,0:T(8,128)}, u32[]{:S(2)}) copy-start(f32[32,32]{1,0:T(8,128)} %copy-done.19) | copy-start | bytes 12292
  1146.0 112.0 %copy-start.37 = (f32[1024]{0:T(1024)S(1)}, f32[1024]{0:T(1024)}, u32[]{:S(2)}) copy-start(f32[1024]{0:T(1024)} %param.19) | copy-start | bytes 12292
  1149.0 112.2 %copy-start.34 = (f32[32,32]{1,0:T(8,128)S(1)}, f32[32,32]{1,0:T(8,128)}, u32[]{:S(2)}) copy-start(f32[32,32]{1,0:T(8,128)} %copy-done.33) | copy-start | bytes 12292
  1149.0 113.5 %copy-start.30 = (f32[32,32]{1,0:T(8,128)S(1)}, f32[32,32]{1,0:T(8,128)}, u32[]{:S(2)}) copy-start(f32[32,32]{1,0:T(8,128)} %copy-done.29) | copy-start | bytes 12292
  1261.2 1.3 copy-start.9
  1261.2 3.8 copy-start.38
  1261.2 3.8 copy-start.39
  1261.2 3.8 copy-start.40
  1261.2 3.8 copy-start.41
  1290.5 4.5 copy-start.1
  (4 other events, 2.6 us)
Sparse Core Ops, SparseCore 0:
  15.4 83.9 all-gather.4
  167.7 166.9 reduce-scatter.4
  341.2 80.7 all-gather.6
  423.4 81.6 all-gather.8
  551.8 166.9 reduce-scatter.8
  721.0 166.0 reduce-scatter.6
  893.9 80.7 all-gather.10
  1091.0 166.9 reduce-scatter.10
where the time goes:
time: 1310 us; the launch traced here: 1300 us
  waiting for transfers between devices  894 us (68%)
  matrix products  315 us (24%)
  other arithmetic  43.4 us (3%)
  blocking collectives  24.2 us (2%)
  between operations  15.2 us (1%)
    reduce_scatter x4, waiting for transfers between devices, scatter_sum(): return lax.psum_scatter(part_sum, 'tp', scatter_dimension=1, tiled=True)  582 us
    all_gather x4, waiting for transfers between devices, gather_tokens(): return lax.all_gather(local_rows, 'tp', axis=1, tiled=True)  311 us
    dot_general x1, matrix products, layer_step(): jnp.einsum('bnhd,whd->bnw', d_value, w_v, preferred_element_type=jnp.floa...  33.9 us
    dot_general x1, matrix products, layer_step(): jnp.einsum('bnw,fw->bnf', d_out_all, w_2, preferred_element_type=jnp.floa...  27.5 us
  transfers between devices with their start and end apart: 8, of which 8 were waited for; matrix products, arithmetic and copies ran while one was open for 8% of the time, Pallas kernels for 0%

commit v1 on v0

v1 whole, which is shorter than its diff:
```python
import math
import jax
import jax.numpy as jnp
from jax import lax
from jax.sharding import PartitionSpec as P

LN_EPS = 1e-6
F32 = jnp.float32
BF16 = jnp.bfloat16


def layer_norm(rows, ln_gain, ln_bias):
    row_mean = jnp.mean(rows, axis=-1, keepdims=True)
    centered = rows - row_mean
    variance = jnp.mean(centered * centered, axis=-1, keepdims=True)
    return centered * lax.rsqrt(variance + LN_EPS) * ln_gain + ln_bias


def gelu_tanh(pre_act):
    return jax.nn.gelu(pre_act, approximate=True)


def attention_core(queries, keys, values):
    att_scale = 1.0 / math.sqrt(queries.shape[-1])
    scores = jnp.einsum('bqhd,bkhd->bhqk', queries, keys, preferred_element_type=F32) * att_scale
    probs = jax.nn.softmax(scores, axis=-1).astype(BF16)
    mixed = jnp.einsum('bhqk,bkhd->bqhd', probs, values, preferred_element_type=F32)
    return mixed.astype(BF16)


def dot(a, b, ca, cb):
    return lax.dot_general(a, b, (((ca,), (cb,)), ((), ())), preferred_element_type=F32)


def solution(mesh):
    act_spec = P('dp', 'tp', None)
    replicated = P()
    head_w = P(None, 'tp', None)
    head_b = P('tp', None)
    grad_head_w = P('dp', 'tp', None)
    grad_head_b = P(('dp', 'tp'), None)
    grad_vec = P('dp')
    in_specs = (act_spec, act_spec, replicated, replicated, head_w, head_b, head_w, head_w, head_b,
                P('tp', None, None), replicated, replicated, replicated, P(None, 'tp'), P('tp'), P('tp', None), replicated)
    out_specs = (act_spec, act_spec, grad_vec, grad_vec, grad_head_w, grad_head_b, grad_head_w, grad_head_w, grad_head_b,
                 P(('dp', 'tp'), None, None), grad_vec, grad_vec, grad_vec, P('dp', 'tp'), P(('dp', 'tp')),
                 P(('dp', 'tp'), None), grad_vec)
    tp = mesh.shape['tp']

    def gather_rows(rows):
        return lax.all_gather(rows, 'tp', axis=0, tiled=True)

    def scatter_rows(rows):
        return lax.psum_scatter(rows, 'tp', scatter_dimension=0, tiled=True)

    def layer_step(x, d_out, ln1_gain, ln1_bias, w_q, b_q, w_k, w_v, b_v, w_o, b_o, ln2_gain, ln2_bias, w_1, b_1, w_2, b_2):
        width, my_heads, head_dim = w_q.shape
        cols = my_heads * head_dim
        hid = w_1.shape[1]
        images, patches = x.shape[0] // tp, x.shape[1] * tp
        tokens = images * patches

        def to_images(t):
            return lax.all_to_all(t, 'tp', 0, 1, tiled=True).reshape(tokens, width)

        def to_tokens(t):
            return lax.all_to_all(t.reshape(images, patches, width), 'tp', 1, 0, tiled=True)

        x_img = to_images(x)
        qkv_rows = jnp.concatenate([w_q.reshape(width, cols).T, w_k.reshape(width, cols).T, w_v.reshape(width, cols).T], axis=0)
        w_qkv = gather_rows(qkv_rows)
        b_small = jnp.concatenate([b_q.reshape(cols), jnp.zeros((cols,), BF16), b_v.reshape(cols), b_1])
        b_all = lax.all_gather(b_small, 'tp')
        b_qkv = b_all[:, :3 * cols].reshape(tp * 3 * cols)
        b_1_all = b_all[:, 3 * cols:].reshape(tp * hid)
        wo_all = gather_rows(w_o.reshape(cols, width))
        w1_all = gather_rows(w_1.T)
        w2_all = gather_rows(w_2)
        d_out_img = to_images(d_out)

        x_f32 = x_img.astype(F32)
        h_one_f, ln1_pull = jax.vjp(layer_norm, x_f32, ln1_gain, ln1_bias)
        h_one = h_one_f.astype(BF16)
        qkv = (dot(h_one, w_qkv, 1, 1) + b_qkv.astype(F32)).astype(BF16)
        split = qkv.reshape(images, patches, tp, 3, my_heads, head_dim)

        def pick(i):
            return split[:, :, :, i].reshape(images, patches, tp * my_heads, head_dim)

        mixed, attn_pull = jax.vjp(attention_core, pick(0), pick(1), pick(2))
        mixed = mixed.reshape(tokens, tp * cols)
        x_mid = (x_f32 + dot(mixed, wo_all, 1, 0) + b_o.astype(F32)).astype(BF16)
        mid_f32 = x_mid.astype(F32)
        h_two_f, ln2_pull = jax.vjp(layer_norm, mid_f32, ln2_gain, ln2_bias)
        h_two = h_two_f.astype(BF16)
        pre_act = (dot(h_two, w1_all, 1, 1) + b_1_all.astype(F32)).astype(BF16)
        hidden_f, gelu_pull = jax.vjp(gelu_tanh, pre_act.astype(F32))
        hidden = hidden_f.astype(BF16)
        y_img = (mid_f32 + dot(hidden, w2_all, 1, 0) + b_2.astype(F32)).astype(BF16)
        y_out = to_tokens(y_img)

        grad_w_2 = scatter_rows(dot(hidden, d_out_img, 0, 0)).astype(BF16)
        d_hidden = dot(d_out_img, w2_all, 1, 1).astype(BF16)
        (d_pre_f,) = gelu_pull(d_hidden.astype(F32))
        d_pre = d_pre_f.astype(BF16)
        grad_w_1 = scatter_rows(dot(d_pre, h_two, 0, 0)).astype(BF16).T
        d_h_two = dot(d_pre, w1_all, 1, 0).astype(BF16)
        d_mid_ln, g_ln2_gain, g_ln2_bias = ln2_pull(d_h_two.astype(F32))
        d_mid = (d_out_img.astype(F32) + d_mid_ln).astype(BF16)
        d_mixed = dot(d_mid, wo_all, 1, 1).astype(BF16)
        grad_w_o = scatter_rows(dot(mixed, d_mid, 0, 0)).astype(BF16).reshape(my_heads, head_dim, width)
        d_q, d_k, d_v = attn_pull(d_mixed.reshape(images, patches, tp * my_heads, head_dim))
        d_split = jnp.stack([t.reshape(images, patches, tp, my_heads, head_dim) for t in (d_q, d_k, d_v)], axis=3)
        d_qkv = d_split.reshape(tokens, tp * 3 * cols)
        g_qkv = scatter_rows(dot(d_qkv, h_one, 0, 0)).astype(BF16).reshape(3, cols, width)
        grad_w_q, grad_w_k, grad_w_v = (g_qkv[i].T.reshape(width, my_heads, head_dim) for i in range(3))
        d_h_one = dot(d_qkv, w_qkv, 1, 0).astype(BF16)
        d_in_ln, g_ln1_gain, g_ln1_bias = ln1_pull(d_h_one.astype(F32))
        grad_x = to_tokens((d_mid.astype(F32) + d_in_ln).astype(BF16))

        def token_sum(t):
            return jnp.sum(t, axis=0, dtype=F32)

        vecs = jnp.concatenate([g_ln1_gain, g_ln1_bias, token_sum(d_mid), g_ln2_gain, g_ln2_bias, token_sum(d_out_img),
                                token_sum(d_qkv), token_sum(d_pre)])
        sums = lax.psum(vecs.reshape(-1, width), 'tp').reshape(-1)
        six = [sums[i * width:(i + 1) * width] for i in range(6)]
        me = lax.axis_index('tp')
        g_b_qkv = lax.dynamic_slice(sums, (6 * width + me * 3 * cols,), (3 * cols,)).astype(BF16)
        grad_b_q = g_b_qkv[:cols].reshape(my_heads, head_dim)
        grad_b_v = g_b_qkv[2 * cols:].reshape(my_heads, head_dim)
        grad_b_1 = lax.dynamic_slice(sums, (6 * width + tp * 3 * cols + me * hid,), (hid,)).astype(BF16)
        return (y_out, grad_x, six[0], six[1], grad_w_q, grad_b_q, grad_w_k, grad_w_v, grad_b_v, grad_w_o,
                six[2].astype(BF16), six[3], six[4], grad_w_1, grad_b_1, grad_w_2, six[5].astype(BF16))

    return jax.shard_map(layer_step, mesh=mesh, in_specs=in_specs, out_specs=out_specs, check_vma=False)
```

time: 1310 us -> 650 us (0.50)
  waiting for transfers between devices: 894 us -> 129 us
  blocking collectives: 24.2 us -> 148 us
  matrix products: 315 us -> 204 us
  local copies, waits for them, and re-layouts: 9.25 us -> 88.8 us
    reduce_scatter x4, waiting for transfers between devices: 582 us -> 115 us  [scatter_rows(): return lax.psum_scatter(rows, 'tp', scatter_dimension=0, tiled=True)]
    all_gather x4, waiting for transfers between devices: 311 us -> 0.05 us  [gather_rows(): return lax.all_gather(rows, 'tp', axis=0, tiled=True)]
    dot_general x23 -> x17, matrix products: 304 us -> 192 us  [the longest x12 153 us: dot(): lax.dot_general(a, b, (((ca,), (cb,)), ((), ())), preferred_element_type=...]
    all_to_all x0 -> x1, blocking collectives: none -> 53.4 us  [to_images(): return lax.all_to_all(t, 'tp', 0, 1, tiled=True).reshape(tokens, width)]
    all_gather x0 -> x1, blocking collectives: none -> 49.4 us  [layer_step(): b_all = lax.all_gather(b_small, 'tp')]
    reshape x0 -> x8, local copies, waits for them, and re-layouts: none -> 20.6 us  [the longest x1 11.2 us: layer_step(): split = qkv.reshape(images, patches, tp, 3, my_heads, head_dim)]
    psum x1, blocking collectives: 24.2 us -> 44.7 us  [layer_step(): sums = lax.psum(vecs.reshape(-1, width), 'tp').reshape(-1)]
    unnamed x120 -> x90, local copies, waits for them, and re-layouts: 7.97 us -> 28.2 us
  transfers between devices with their start and end apart: 8 -> 11, of which waited for: 8 -> 3; matrix products, arithmetic and copies ran while one was open for 8% -> 41% of each run, Pallas kernels for 0% -> 0%
where the time goes in v1:
time: 650 us; the launch traced here: 644 us
  matrix products  204 us (31%)
  blocking collectives  148 us (23%)
  waiting for transfers between devices  129 us (20%)
  local copies, waits for them, and re-layouts  88.8 us (14%)
  other arithmetic  47.4 us (7%)
  between operations  15.2 us (2%)
  starting transfers between devices  12.9 us (2%)
    dot_general x12, matrix products, dot(): lax.dot_general(a, b, (((ca,), (cb,)), ((), ())), preferred_element_type=...  153 us
    reduce_scatter x4, waiting for transfers between devices, scatter_rows(): return lax.psum_scatter(rows, 'tp', scatter_dimension=0, tiled=True)  115 us
    all_to_all x1, blocking collectives, to_images(): return lax.all_to_all(t, 'tp', 0, 1, tiled=True).reshape(tokens, width)  53.4 us
    all_gather x1, blocking collectives, layer_step(): b_all = lax.all_gather(b_small, 'tp')  49.4 us
    psum x1, blocking collectives, layer_step(): sums = lax.psum(vecs.reshape(-1, width), 'tp').reshape(-1)  44.7 us
    unnamed x90, local copies, waits for them, and re-layouts  28.2 us
    dot_general x2, matrix products, attention_core(): jnp.einsum('bqhd,bkhd->bhqk', queries, keys, preferred_element_type=F32)  24.8 us
    reduce_sum x3, other arithmetic, token_sum(): return jnp.sum(t, axis=0, dtype=F32)  15 us
  transfers between devices with their start and end apart: 11, of which 3 were waited for; matrix products, arithmetic and copies ran while one was open for 41% of the time, Pallas kernels for 0%

profile of v1, /device:TPU:112, one launch (start us, length us, event | category | flops | bytes accessed | tf_op | source)
XLA Modules:
  0.0 644.1 jit_solution(17215886845733771495)
XLA Ops:
  7.3 2.2 pad_maximum_fusion
  11.2 53.4 %all_to_all.60 = bf16[32,32,1024]{2,1,0:T(8,128)(2,1)} all-to-all(bf16[32,32,1024]{2,1,0:T(8,128)(2,1)S(1)} %copy-done.11), channel_id=1, replica_groups=mesh['dp'=2,'tp'=8] {'tp'}, dimensions={0} | all-to-all | bytes 4194304 | tf_op jit(solution)/shard_map/all_to_all | solution.py:64
  64.6 3.8 all-to-all-start
  69.4 49.4 %all-gather.1 = bf16[8,1,896]{2,1,0:T(2,128)(2,1)S(1)} all-gather(bf16[1,1,896]{2,1,0:T(2,128)(2,1)S(1)} %reshape.291), channel_id=2, replica_groups=mesh['dp'=2,'tp'=8] {'tp'}, dimensions={0}, use_global_device_ids=true | all-gather | bytes 16128 | tf_op jit(solution)/shard_map/all_gather | solution.py:73
  118.8 3.2 copy.76
  122.0 2.4 copy.67
  124.9 1.9 copy-done.3
  127.2 2.7 multiply_reduce_fusion.1
  130.1 2.2 add_convert_fusion.2
  133.8 11.6 %add_convert_fusion.1 = bf16[1024,3072]{1,0:T(8,128)(2,1)} fusion(f32[3072]{0:T(1024)S(1)} %reshape.286, bf16[1024,1024]{1,0:T(8,128)(2,1)S(1)} %add_convert_fusion.4, bf16[3072,1024]{1,0:T(8,128)(2,1)} %all-gather.7.cloned.1.call-done), kind=kOutput, calls=%fused_computation.32 | convolution fusion | flops 6448742400 | bytes 14692352 | tf_op jit(solution)/shard_map/dot_general | solution.py:32
  145.4 8.7 %copy.68 = bf16[1024,3072]{0,1:T(8,128)(2,1)} copy(bf16[1024,3072]{1,0:T(8,128)(2,1)} %add_convert_fusion.1) | data formatting | bytes 12582912 | tf_op jit(solution)/shard_map/convert_element_type | solution.py:84
  154.0 11.2 %reshape.271 = bf16[4,256,8,3,2,64]{1,0,5,4,3,2:T(4,128)(2,1)} reshape(bf16[1024,3072]{0,1:T(8,128)(2,1)} %copy.68) | data formatting | bytes 12582912 | tf_op jit(solution)/shard_map/reshape | solution.py:85
  165.2 4.5 fusion.58
  169.8 1.7 copy.71
  171.5 1.7 copy.70
  173.6 11.4 %fusion.62 = (f32[4,16,256]{2,1,0:T(8,128)S(1)}, f32[4,16,256,256]{2,3,1,0:T(8,128)}) fusion(bf16[4,256,16,64]{1,3,2,0:T(8,128)(2,1)} %bitcast.160, bf16[4,256,16,64]{1,3,2,0:T(8,128)(2,1)} %bitcast.162), kind=kOutput, calls=%fused_computation.128 | convolution fusion | flops 549454080 | bytes 21037056 | tf_op jit(solution)/shard_map/jvp()/sub | solution.py:26
  184.9 7.0 %divide_convert_fusion = bf16[4,16,256,256]{2,3,1,0:T(8,128)(2,1)S(1)} fusion(f32[4,16,256,256]{2,3,1,0:T(8,128)} %get-tuple-element.95, f32[4,16,256]{2,1,0:T(8,128)S(1)} %get-tuple-element.94), kind=kLoop, calls=%fused_computation.27 | loop fusion | flops 8388608 | bytes 25231360 | tf_op jit(solution)/shard_map/jvp()/convert_element_type | solution.py:26
  191.9 1.6 convert_bitcast_fusion
  193.6 1.6 copy-done
  195.1 1.8 copy.73
  196.9 1.9 copy.94
  198.8 6.2 convert_reduce_fusion.4
  205.8 15.0 %add_convert_fusion = bf16[1024,4096]{1,0:T(8,128)(2,1)} fusion(f32[4096]{0:T(1024)S(1)} %bitcast.182, bf16[4096,1024]{0,1:T(8,128)(2,1)} %all-gather.11.cloned.1.call-done, bf16[1024,1024]{1,0:T(8,128)(2,1)S(1)} %get-tuple-element.97, f32[1024]{0:T(1024)S(1)} %copy-done.32, f32[1024]{0:T(1024)S(1)} %copy-done.24, f32[1024]{0:T(1024)S(1)} %fusion.44, ...), kind=kOutput, calls=%fused_computation.26 | convolution fusion | flops 8604614656 | bytes 18907136 | tf_op jit(solution)/shard_map/dot_general | solution.py:32
  220.7 25.6 %convert_reduce_fusion = (f32[4096]{0:T(1024)}, bf16[1024,4096]{1,0:T(8,128)(2,1)}) fusion(bf16[1024,4096]{1,0:T(8,128)(2,1)} %add_convert_fusion, bf16[1024,1024]{1,0:T(8,128)(2,1)} %bitcast.152, bf16[4096,1024]{1,0:T(8,128)(2,1)} %all-gather.13.cloned.1.call-done), kind=kOutput, calls=%fused_computation.25 | convolution fusion | flops 8694788096 | bytes 27279360 | tf_op jit(solution)/shard_map/dot_general | solution.py:32
  246.3 14.9 %convert_reduce_fusion.3 = (f32[1024]{0:T(1024)}, f32[1024]{0:T(1024)S(1)}, bf16[1024,1024]{1,0:T(8,128)(2,1)S(1)}) fusion(f32[1024]{0:T(1024)S(1)} %copy-done.24, f32[1024]{0:T(1024)S(1)} %broadcast_multiply_fusion.1, bf16[1024,1024]{1,0:T(8,128)(2,1)S(1)} %get-tuple-element.97, bf16[1024,4096]{1,0:T(8,128)(2,1)} %get-tuple-element.103, ...), kind=kOutput, calls=%fused_computation.40 | convolution fusion | flops 8598321152 | bytes 20987904 | tf_op jit(solution)/shard_map/dot_general | solution.py:32
  261.3 3.3 fusion.37
  264.6 2.8 convert_reduce_fusion.5
  268.7 4.4 fusion.64
  273.2 4.6 convolution_convert_fusion.5
  277.8 2.6 copy.77
  280.3 3.3 reshape.276
  283.8 10.6 %fusion.9 = (f32[4,16,256]{2,1,0:T(8,128)S(1)}, bf16[4,16,256,256]{2,3,1,0:T(8,128)(2,1)}) fusion(f32[4,16,256,256]{2,3,1,0:T(8,128)} %get-tuple-element.95, f32[4,16,256]{2,1,0:T(8,128)S(1)} %multiply_divide_fusion, bf16[4,256,16,64]{1,3,2,0:T(8,128)(2,1)} %bitcast.148, bf16[4,16,64,256]{3,0,2,1:T(4,128)(2,1)S(1)} %bitcast.145), kind=kOutput, calls=%fused_computation.17 | convolution fusion | flops 557826048 | bytes 29491200 | tf_op jit(solution)/shard_map/transpose(jvp(bhqk,bkhd->bqhd))/dot_general | solution.py:27
  294.5 12.3 %convolution_convert_fusion.4 = bf16[4,16,256,64]{2,3,1,0:T(8,128)(2,1)} fusion(bf16[4,256,16,64]{1,3,2,0:T(8,128)(2,1)} %bitcast.163, f32[4,16,256,256]{2,3,1,0:T(8,128)} %get-tuple-element.95, bf16[4,16,256,256]{2,3,1,0:T(8,128)(2,1)} %get-tuple-element.100, f32[4,16,256]{2,1,0:T(8,128)S(1)} %neg.13, f32[4,16,256]{2,1,0:T(8,128)S(1)} %get-tuple-element.94), kind=kOutput, calls=%fused_computation.85 | convolution fusion | flops 558891008 | bytes 29491200 | tf_op jit(solution)/shard_map/transpose(jvp(bqhd,bkhd->bhqk))/dot_general | solution.py:25
  306.8 4.9 copy_dynamic-update-slice_fusion.2
  311.7 12.5 %convolution_convert_fusion.3 = bf16[4,16,256,64]{2,3,1,0:T(8,128)(2,1)} fusion(bf16[4,256,16,64]{1,3,2,0:T(8,128)(2,1)S(1)} %bitcast.161, f32[4,16,256,256]{2,3,1,0:T(8,128)} %get-tuple-element.95, bf16[4,16,256,256]{2,3,1,0:T(8,128)(2,1)} %get-tuple-element.100, f32[4,16,256]{2,1,0:T(8,128)S(1)} %neg.13, f32[4,16,256]{2,1,0:T(8,128)S(1)} %get-tuple-element.94), kind=kOutput, calls=%fused_computation.84 | convolution fusion | flops 558891008 | bytes 29491200 | tf_op jit(solution)/shard_map/transpose(jvp(bqhd,bkhd->bhqk))/dot_general | solution.py:25
  324.2 4.7 copy_dynamic-update-slice_fusion.1
  328.8 2.6 convolution_convert_fusion.2
  331.5 3.1 copy_dynamic-update-slice_fusion
  334.6 5.0 copy.96
  339.6 2.6 copy-done.10
  342.1 8.9 %fusion.63 = f32[3072,1024]{1,0:T(8,128)} fusion(bf16[1024,3072]{0,1:T(8,128)(2,1)S(1)} %bitcast.157, bf16[1024,1024]{1,0:T(8,128)(2,1)S(1)} %bitcast.159), kind=kOutput, calls=%fused_computation.130 | convolution fusion | flops 6442450944 | bytes 20971520 | tf_op jit(solution)/shard_map/dot_general | solution.py:32
  351.2 1.5 copy-done.6
  352.7 15.2 %fusion.54 = f32[4096,1024]{1,0:T(8,128)} fusion(bf16[1024,4096]{1,0:T(8,128)(2,1)} %get-tuple-element.103, bf16[1024,1024]{1,0:T(8,128)(2,1)S(1)} %copy-done.6, f32[1024]{0:T(1024)S(1)} %copy-done.33, f32[1024]{0:T(1024)S(1)} %copy-done.24, f32[1024]{0:T(1024)S(1)} %fusion.44, f32[1024]{0:T(1024)S(1)} %broadcast_multiply_fusion.1), kind=kOutput, calls=%fused_computation.122 | convolution fusion | flops 8596226048 | bytes 27279360 | tf_op jit(solution)/shard_map/dot_general | solution.py:32
  368.0 18.8 %fusion.51 = f32[4096,1024]{1,0:T(8,128)} fusion(bf16[1024,1024]{1,0:T(8,128)(2,1)} %bitcast.153, bf16[1024,4096]{1,0:T(8,128)(2,1)} %add_convert_fusion), kind=kOutput, calls=%fused_computation.121 | convolution fusion | flops 8631877632 | bytes 27262976 | tf_op jit(solution)/shard_map/dot_general | solution.py:32
  387.4 2.0 convert_reduce_fusion.6
  389.4 15.6 %fusion.36 = bf16[1024,1024]{1,0:T(8,128)(2,1)S(1)} fusion(bf16[1024,1024]{1,0:T(8,128)(2,1)S(1)} %copy-done.6, f32[1024]{0:T(1024)S(1)} %convert_element_type.206, bf16[4096,1024]{1,0:T(8,128)(2,1)} %all-gather.13.cloned.1.call-done, bf16[1024,4096]{1,0:T(8,128)(2,1)} %add_convert_fusion), kind=kOutput, calls=%fused_computation.63 | convolution fusion | flops 8636071936 | bytes 20975616 | tf_op jit(solution)/shard_map/dot_general | solution.py:32
  405.1 2.9 copy.74
  408.0 3.8 all-to-all-start.1
  411.9 11.8 %convert_reduce_fusion.2 = (f32[1024]{0:T(1024)S(1)}, f32[1024]{0:T(1024)S(1)}, bf16[1024,1024]{1,0:T(8,128)(2,1)S(1)}) fusion(f32[1024]{0:T(1024)S(1)} %copy-done.20, f32[1024]{0:T(1024)S(1)} %copy-done.16, f32[8,4,32,1024]{3,2,0,1:T(8,128)} %copy.67, bf16[1024,3072]{0,1:T(8,128)(2,1)} %bitcast.158, bf16[3072,1024]{1,0:T(8,128)(2,1)} %all-gather.7.cloned.1.call-done), kind=kOutput, calls=%fused_computation.36 | convolution fusion | flops 6449788928 | bytes 18890752 | tf_op jit(solution)/shard_map/dot_general | solution.py:32
  423.8 2.9 fusion.38
  426.7 2.1 fusion.32
  428.8 3.0 copy.86
  431.8 11.7 %all-to-all-done.1 = bf16[4,256,1024]{2,0,1:T(4,128)(2,1)S(1)} async-done(((bf16[4,256,1024]{2,0,1:T(4,128)(2,1)}), bf16[4,256,1024]{2,0,1:T(4,128)(2,1)S(1)}, u32[]{:S(2)}, u32[]{:S(2)}) %all-to-all-start.1) | async-done | bytes 2097184 | tf_op jit(solution)/shard_map/all_to_all | solution.py:67
  443.4 4.8 all-to-all-start.3
  448.3 10.3 %convert_reduce_fusion.1 = f32[8,3,2,64]{3,2,1,0:T(2,128)S(1)} fusion(bf16[4,256,8,3,2,64]{1,0,5,4,3,2:T(4,128)(2,1)} %copy_dynamic-update-slice_fusion), kind=kLoop, calls=%fused_computation.31 | loop fusion | flops 6288384 | bytes 6303744 | tf_op jit(solution)/shard_map/reduce_sum | solution.py:122
  458.7 44.7 %psum.7 = f32[13,1024]{1,0:T(8,128)S(1)} all-reduce(f32[13,1024]{1,0:T(8,128)S(1)} %reshape.279), channel_id=1, replica_groups=mesh['dp'=2,'tp'=8] {'tp'}, use_global_device_ids=true, to_apply=%region_19.0 | all-reduce | flops 13312 | bytes 106496 | tf_op jit(solution)/shard_map/psum | solution.py:126
  506.6 2.0 copy.75
  508.6 3.6 copy.87
  512.3 1.8 convert_element_type.235
  514.0 1.5 convert_element_type.233
  516.5 28.3 %reduce-scatter.9.cloned.1.call-done = f32[512,1024]{1,0:T(8,128)} async-done(((f32[4096,1024]{1,0:T(8,128)}), f32[512,1024]{1,0:T(8,128)}) %reduce-scatter.9.cloned.1.call-update) | async-done | bytes 2097168 | tf_op jit(solution)/shard_map/reduce_scatter | solution.py:54
  544.8 1.7 convert_bitcast_fusion.1
  547.8 86.4 %reduce-scatter.11.cloned.1.call-done = f32[512,1024]{1,0:T(8,128)} async-done(((f32[4096,1024]{1,0:T(8,128)}), f32[512,1024]{1,0:T(8,128)}) %reduce-scatter.11.cloned.1.call-update) | async-done | bytes 2097168 | tf_op jit(solution)/shard_map/reduce_scatter | solution.py:54
  634.3 2.7 convert_element_type.239
  (147 shorter events, 14.2 us)
Async XLA Ops:
  7.2 3.9 copy-start.11
  7.2 126.6 %all-gather.7.cloned.1.call-start = ((), (), s32[]{:S(2)}) async-start(), calls=%async_computation.8 | async-start | bytes 7077888 | tf_op jit(solution)/shard_map/all_gather | solution.py:51
  9.5 189.3 %all-gather.9.cloned.1.call-start = ((), (), s32[]{:S(2)}) async-start(), calls=%async_computation.9 | async-start | bytes 2359296 | tf_op jit(solution)/shard_map/all_gather | solution.py:51
  10.3 195.4 %all-gather.11.cloned.1.call-start = ((), (), s32[]{:S(2)}) async-start(), calls=%async_computation.10 | async-start | bytes 9437184 | tf_op jit(solution)/shard_map/all_gather | solution.py:51
  11.1 58.0 %copy-start.34 = (bf16[2,64]{1,0:T(2,128)(2,1)S(1)}, bf16[2,64]{1,0:T(2,128)(2,1)}, u32[]{:S(2)}) copy-start(bf16[2,64]{1,0:T(2,128)(2,1)} %param.22) | copy-start | bytes 772
  11.1 58.1 %copy-start.35 = (bf16[2,64]{1,0:T(2,128)(2,1)S(1)}, bf16[2,64]{1,0:T(2,128)(2,1)}, u32[]{:S(2)}) copy-start(bf16[2,64]{1,0:T(2,128)(2,1)} %param.25) | copy-start | bytes 772
  11.2 58.2 %copy-start.31 = (bf16[512]{0:T(512)(128)(2,1)S(1)}, bf16[512]{0:T(512)(128)(2,1)}, u32[]{:S(2)}) copy-start(bf16[512]{0:T(512)(128)(2,1)} %param.31) | copy-start | bytes 3076
  11.2 58.2 %copy-start.29 = (bf16[1024]{0:T(1024)(128)(2,1)S(1)}, bf16[1024]{0:T(1024)(128)(2,1)}, u32[]{:S(2)}) copy-start(bf16[1024]{0:T(1024)(128)(2,1)} %param.27) | copy-start | bytes 6148
  64.6 57.5 %all-to-all-start = ((bf16[32,32,1024]{2,1,0:T(8,128)(2,1)}), bf16[32,32,1024]{2,1,0:T(8,128)(2,1)S(1)}, u32[]{:S(2)}, u32[]{:S(2)}) async-start(bf16[32,32,1024]{2,1,0:T(8,128)(2,1)} %param.17), calls=%async_computation | async-start | bytes 4194304 | tf_op jit(solution)/shard_map/all_to_all | solution.py:64
  68.4 152.3 %all-gather.13.cloned.1.call-start = ((), (), s32[]{:S(2)}) async-start(), calls=%async_computation.11 | async-start | bytes 9437184 | tf_op jit(solution)/shard_map/all_gather | solution.py:51
  69.1 443.2 %reduce-scatter.7.cloned.1.call-start = ((), (), s32[]{:S(2)}) async-start(), calls=%async_computation.13 | async-start | bytes 4718592 | tf_op jit(solution)/shard_map/reduce_scatter | solution.py:54
  124.9 1.9 copy-start.3
  126.9 3.2 copy-start.19
  126.9 3.2 copy-start.26
  127.2 5.1 copy-start.15
  130.1 3.7 copy-start.21
  130.1 3.0 copy-start.1
  130.1 2.2 copy-start.17
  173.5 18.4 %copy-start.4 = (bf16[4,256,8,1,2,64]{1,5,4,2,0,3:T(8,128)(2,1)}, bf16[4,256,8,1,2,64]{1,5,4,2,0,3:T(8,128)(2,1)S(1)}, u32[]{:S(2)}) copy-start(bf16[4,256,8,1,2,64]{1,5,4,2,0,3:T(8,128)(2,1)S(1)} %copy.69) | copy-start | bytes 6291460
  191.9 3.2 copy-start
  198.8 7.0 %copy-start.24 = (f32[1024]{0:T(1024)S(1)}, f32[1024]{0:T(1024)}, u32[]{:S(2)}) copy-start(f32[1024]{0:T(1024)} %param.28) | copy-start | bytes 12292
  198.8 7.0 %copy-start.32 = (f32[1024]{0:T(1024)S(1)}, f32[1024]{0:T(1024)}, u32[]{:S(2)}) copy-start(f32[1024]{0:T(1024)} %param.29) | copy-start | bytes 12292
  205.0 59.6 %copy-start.5 = (bf16[1024,1024]{1,0:T(8,128)(2,1)}, bf16[1024,1024]{1,0:T(8,128)(2,1)S(1)}, u32[]{:S(2)}) copy-start(bf16[1024,1024]{1,0:T(8,128)(2,1)S(1)} %get-tuple-element.97) | copy-start | bytes 6291460
  261.2 3.3 copy-start.9
  264.6 4.2 copy-start.14
  267.4 1.4 copy-start.7
  283.7 230.3 %reduce-scatter.5.cloned.1.call-start = ((), (), s32[]{:S(2)}) async-start(), calls=%async_computation.12 | async-start | bytes 14155776 | tf_op jit(solution)/shard_map/reduce_scatter | solution.py:54
  294.5 34.4 %slice-start = ((s8[8388608]{0:T(1024)(128)(4,1)}), s8[4194304]{0:T(1024)(128)(4,1)S(1)}, s32[]{:S(2)}) async-start(s8[8388608]{0:T(1024)(128)(4,1)} %bitcast.141), calls=%async_computation.16 | async-start | bytes 8388608
  306.7 4.9 copy-start.13
  311.7 17.2 %slice-start.1 = ((s8[8388608]{0:T(1024)(128)(4,1)}), s8[4194304]{0:T(1024)(128)(4,1)S(1)}, s32[]{:S(2)}) async-start(s8[8388608]{0:T(1024)(128)(4,1)} %bitcast.141), calls=%async_computation.17 | async-start | bytes 8388608
  334.6 7.6 %copy-start.12 = (bf16[4,8,32,1024]{3,2,1,0:T(8,128)(2,1)S(1)}, bf16[4,8,32,1024]{3,2,1,0:T(8,128)(2,1)}, u32[]{:S(2)}) copy-start(bf16[4,8,32,1024]{3,2,1,0:T(8,128)(2,1)} %add_convert_fusion.2) | copy-start | bytes 6291460
  339.6 2.6 copy-start.10
  351.1 1.6 copy-start.6
  351.1 1.6 copy-start.33
  351.2 193.6 %reduce-scatter.9.cloned.1.call-start = ((), (), s32[]{:S(2)}) async-start(), calls=%async_computation.14 | async-start | bytes 18874368 | tf_op jit(solution)/shard_map/reduce_scatter | solution.py:54
  367.9 266.4 %reduce-scatter.11.cloned.1.call-start = ((), (), s32[]{:S(2)}) async-start(), calls=%async_computation.15 | async-start | bytes 18874368 | tf_op jit(solution)/shard_map/reduce_scatter | solution.py:54
  386.7 0.7 copy-start.30
  405.0 6.8 %copy-start.16 = (f32[1024]{0:T(1024)S(1)}, f32[1024]{0:T(1024)}, u32[]{:S(2)}) copy-start(f32[1024]{0:T(1024)} %copy-done.15) | copy-start | bytes 12292
  405.1 6.8 %copy-start.20 = (f32[1024]{0:T(1024)S(1)}, f32[1024]{0:T(1024)}, u32[]{:S(2)}) copy-start(f32[1024]{0:T(1024)} %param.19) | copy-start | bytes 12292
  408.0 35.4 %all-to-all-start.1 = ((bf16[4,256,1024]{2,0,1:T(4,128)(2,1)}), bf16[4,256,1024]{2,0,1:T(4,128)(2,1)S(1)}, u32[]{:S(2)}, u32[]{:S(2)}) async-start(bf16[4,256,1024]{2,0,1:T(4,128)(2,1)} %copy.74), calls=%async_computation.1 | async-start | bytes 4194304 | tf_op jit(solution)/shard_map/all_to_all | solution.py:67
  411.8 11.9 %copy-start.22 = (f32[1024]{0:T(1024)S(1)}, f32[1024]{0:T(1024)}, u32[]{:S(2)}) copy-start(f32[1024]{0:T(1024)} %copy-done.21) | copy-start | bytes 12292
  411.9 11.9 %copy-start.2 = (f32[8,4,32,1024]{3,2,0,1:T(8,128)S(1)}, f32[8,4,32,1024]{3,2,0,1:T(8,128)}, u32[]{:S(2)}) copy-start(f32[8,4,32,1024]{3,2,0,1:T(8,128)} %copy.67) | copy-start | bytes 12582916
  411.9 11.9 %copy-start.18 = (f32[1024]{0:T(1024)S(1)}, f32[1024]{0:T(1024)}, u32[]{:S(2)}) copy-start(f32[1024]{0:T(1024)} %copy-done.17) | copy-start | bytes 12292
  423.7 3.0 copy-start.8
  443.4 65.2 %all-to-all-start.3 = ((bf16[4,256,1024]{2,0,1:T(4,128)(2,1)}), bf16[4,256,1024]{2,0,1:T(4,128)(2,1)}, u32[]{:S(2)}, u32[]{:S(2)}) async-start(bf16[4,256,1024]{2,0,1:T(4,128)(2,1)} %copy.86), calls=%async_computation.3 | async-start | bytes 4194304 | tf_op jit(solution)/shard_map/all_to_all | solution.py:67
  448.2 10.4 %copy-start.23 = (f32[1024]{0:T(1024)S(1)}, f32[1024]{0:T(1024)}, u32[]{:S(2)}) copy-start(f32[1024]{0:T(1024)} %get-tuple-element.78) | copy-start | bytes 12292
  448.2 10.4 %copy-start.27 = (f32[1024]{0:T(1024)S(1)}, f32[1024]{0:T(1024)}, u32[]{:S(2)}) copy-start(f32[1024]{0:T(1024)} %get-tuple-element.70) | copy-start | bytes 12292
  448.3 10.4 %copy-start.28 = (f32[1024]{0:T(1024)S(1)}, f32[1024]{0:T(1024)}, u32[]{:S(2)}) copy-start(f32[1024]{0:T(1024)} %get-tuple-element.72) | copy-start | bytes 12292
  448.3 10.4 %copy-start.25 = (f32[4096]{0:T(1024)S(1)}, f32[4096]{0:T(1024)}, u32[]{:S(2)}) copy-start(f32[4096]{0:T(1024)} %get-tuple-element.102) | copy-start | bytes 49156
Sparse Core Ops, SparseCore 0:
  10.2 59.8 all-gather.6
  71.7 29.5 all-gather.8
  102.8 49.5 all-gather.10
  153.9 45.6 all-gather.12
  283.8 34.8 reduce-scatter.6
  351.3 77.8 reduce-scatter.4
  431.5 113.1 reduce-scatter.8
  547.1 87.1 reduce-scatter.10

commit v2 on v1

v2 whole, which is shorter than its diff:
```python
import functools
import math
import jax
import jax.numpy as jnp
from jax import lax
from jax.experimental import pallas as pl
from jax.sharding import PartitionSpec as P

LN_EPS = 1e-6
F32 = jnp.float32
BF16 = jnp.bfloat16
PAD = 16


def layer_norm(rows, ln_gain, ln_bias):
    row_mean = jnp.mean(rows, axis=-1, keepdims=True)
    centered = rows - row_mean
    variance = jnp.mean(centered * centered, axis=-1, keepdims=True)
    return centered * lax.rsqrt(variance + LN_EPS) * ln_gain + ln_bias


def gelu_tanh(pre_act):
    return jax.nn.gelu(pre_act, approximate=True)


def after(values, token):
    return lax.optimization_barrier((*values, token))[:len(values)]


def dot(a, b, ca, cb):
    return lax.dot_general(a, b, (((ca,), (cb,)), ((), ())), preferred_element_type=F32)


def head_lanes(shape, head, head_dim):
    lane = lax.broadcasted_iota(jnp.int32, shape, 1)
    return (lane >= head * head_dim) & (lane < (head + 1) * head_dim)


def attend_kernel(heads, head_dim, qkv_ref, out_ref):
    cols = heads * head_dim
    q, k, v = (qkv_ref[:, i * cols:(i + 1) * cols] for i in range(3))
    scale = 1.0 / math.sqrt(head_dim)
    total = None
    for head in range(heads):
        mine = head_lanes(q.shape, head, head_dim)
        s = dot(jnp.where(mine, q, jnp.zeros_like(q)), k, 1, 1) * scale
        e = jnp.exp(s - jnp.max(s, axis=1, keepdims=True))
        p = (e / jnp.sum(e, axis=1, keepdims=True)).astype(BF16)
        a = dot(p, v, 1, 0)
        total = a if total is None else jnp.where(mine, a, total)
    out_ref[...] = total.astype(BF16)


def attend_back_kernel(heads, head_dim, qkv_ref, da_ref, dqkv_ref):
    cols = heads * head_dim
    q, k, v = (qkv_ref[:, i * cols:(i + 1) * cols] for i in range(3))
    da = da_ref[...]
    scale = 1.0 / math.sqrt(head_dim)
    dq = dk = dv = None
    for head in range(heads):
        mine = head_lanes(q.shape, head, head_dim)
        zero = jnp.zeros_like(q)
        s = dot(jnp.where(mine, k, zero), q, 1, 1) * scale
        e = jnp.exp(s - jnp.max(s, axis=0, keepdims=True))
        p32 = e / jnp.sum(e, axis=0, keepdims=True)
        dv_h = dot(p32.astype(BF16), da, 1, 0)
        dp = dot(jnp.where(mine, v, zero), da, 1, 1).astype(BF16).astype(F32)
        ds = p32 * (dp - jnp.sum(dp * p32, axis=0, keepdims=True))
        ds = (ds * scale).astype(BF16)
        dk_h = dot(ds, q, 1, 0)
        dq_h = dot(ds, k, 0, 0)
        if head == 0:
            dq, dk, dv = dq_h, dk_h, dv_h
        else:
            dq, dk, dv = jnp.where(mine, dq_h, dq), jnp.where(mine, dk_h, dk), jnp.where(mine, dv_h, dv)
    for i, d in enumerate((dq, dk, dv)):
        dqkv_ref[:, i * cols:(i + 1) * cols] = d.astype(BF16)


def attend(qkv, images, heads, head_dim):
    tokens, wide = qkv.shape
    patches, cols = tokens // images, heads * head_dim
    blocks = wide // (3 * cols)
    return pl.pallas_call(
        functools.partial(attend_kernel, heads, head_dim),
        grid=(images, blocks),
        in_specs=[pl.BlockSpec((patches, 3 * cols), lambda i, j: (i, j))],
        out_specs=pl.BlockSpec((patches, cols), lambda i, j: (i, j)),
        out_shape=jax.ShapeDtypeStruct((tokens, blocks * cols), BF16),
        cost_estimate=pl.CostEstimate(flops=images * blocks * heads * patches * patches * 1024, bytes_accessed=8 * tokens * blocks * cols,
                                      transcendentals=0),
        name="attend",
    )(qkv)


def attend_back(qkv, d_mixed, images, heads, head_dim):
    tokens, wide = qkv.shape
    patches, cols = tokens // images, heads * head_dim
    blocks = wide // (3 * cols)
    return pl.pallas_call(
        functools.partial(attend_back_kernel, heads, head_dim),
        grid=(images, blocks),
        in_specs=[pl.BlockSpec((patches, 3 * cols), lambda i, j: (i, j)), pl.BlockSpec((patches, cols), lambda i, j: (i, j))],
        out_specs=pl.BlockSpec((patches, 3 * cols), lambda i, j: (i, j)),
        out_shape=jax.ShapeDtypeStruct((tokens, wide), BF16),
        cost_estimate=pl.CostEstimate(flops=images * blocks * heads * patches * patches * 2048, bytes_accessed=14 * tokens * blocks * cols,
                                      transcendentals=0),
        name="attend_back",
    )(qkv, d_mixed)


def solution(mesh):
    act_spec = P('dp', 'tp', None)
    replicated = P()
    head_w = P(None, 'tp', None)
    head_b = P('tp', None)
    grad_head_w = P('dp', 'tp', None)
    grad_head_b = P(('dp', 'tp'), None)
    grad_vec = P('dp')
    in_specs = (act_spec, act_spec, replicated, replicated, head_w, head_b, head_w, head_w, head_b,
                P('tp', None, None), replicated, replicated, replicated, P(None, 'tp'), P('tp'), P('tp', None), replicated)
    out_specs = (act_spec, act_spec, grad_vec, grad_vec, grad_head_w, grad_head_b, grad_head_w, grad_head_w, grad_head_b,
                 P(('dp', 'tp'), None, None), grad_vec, grad_vec, grad_vec, P('dp', 'tp'), P(('dp', 'tp')),
                 P(('dp', 'tp'), None), grad_vec)
    tp = mesh.shape['tp']
    chips = tp // 2
    rings = [[2 * i + core for i in range(chips)] for core in range(2)]
    pairs = [(i, i + 1 - 2 * (i % 2)) for i in range(tp)]

    def gather_rows(rows):
        return lax.all_gather(rows, 'tp', axis=0, tiled=True, axis_index_groups=rings)

    def scatter_rows(rows):
        return lax.psum_scatter(rows, 'tp', scatter_dimension=0, tiled=True, axis_index_groups=rings)

    def swap(t):
        return lax.ppermute(t, 'tp', pairs)

    def layer_body(x, d_out, ln1_gain, ln1_bias, w_q, b_q, w_k, w_v, b_v, w_o, b_o, ln2_gain, ln2_bias, w_1, b_1, w_2, b_2):
        width, my_heads, head_dim = w_q.shape
        cols = my_heads * head_dim
        qkv_cols = 3 * cols
        hid = w_1.shape[1]
        images, patches = x.shape[0] // tp, x.shape[1] * tp
        tokens = images * patches

        def to_images(t):
            return lax.all_to_all(t.reshape(tp, images, patches // tp, width), 'tp', 0, 0, tiled=True)

        def join_tokens(blocks):
            return blocks.swapaxes(0, 1).reshape(tokens, width)

        def to_tokens(t):
            return lax.all_to_all(t.reshape(images, patches, width), 'tp', 1, 0, tiled=True)

        def both(mine, token=None):
            return mine, swap(mine if token is None else after((mine,), token)[0])

        bias_row = jnp.concatenate([b_q.reshape(cols), jnp.zeros((cols,), BF16), b_v.reshape(cols), b_1,
                                    jnp.zeros((width - qkv_cols - hid,), BF16)])
        qkv_rows = jnp.concatenate([w_q.reshape(width, cols).T, w_k.reshape(width, cols).T, w_v.reshape(width, cols).T,
                                    jnp.broadcast_to(bias_row[None], (PAD, width))], axis=0)
        packed = both(gather_rows(qkv_rows))
        x_img = lax.optimization_barrier(join_tokens(to_images(x)))
        wo_mine, w1_mine, w2_mine = gather_rows(w_o.reshape(cols, width)), gather_rows(w_1.T), gather_rows(w_2)

        w_qkv, b_qkv, b_1_all = [], [], []
        for half in packed:
            blocks = half.reshape(chips, qkv_cols + PAD, width)
            w_qkv.append(blocks[:, :qkv_cols].reshape(chips * qkv_cols, width))
            b_qkv.append(blocks[:, qkv_cols, :qkv_cols].reshape(chips * qkv_cols).astype(F32))
            b_1_all.append(blocks[:, qkv_cols, qkv_cols:qkv_cols + hid].reshape(chips * hid).astype(F32))

        x_f32 = x_img.astype(F32)
        h_one_f, ln1_pull = jax.vjp(layer_norm, x_f32, ln1_gain, ln1_bias)
        h_one = h_one_f.astype(BF16)
        qkv = [(dot(h_one, w, 1, 1) + b).astype(BF16) for w, b in zip(w_qkv, b_qkv)]
        d_moved = to_images(after((d_out,), qkv[0])[0])
        wo = both(wo_mine, qkv[0])
        mixed = [attend(t, images, my_heads, head_dim) for t in qkv]
        w1 = both(w1_mine, mixed[1])
        x_mid = (x_f32 + dot(mixed[0], wo[0], 1, 0) + dot(mixed[1], wo[1], 1, 0) + b_o.astype(F32)).astype(BF16)
        mid_f32 = x_mid.astype(F32)
        h_two_f, ln2_pull = jax.vjp(layer_norm, mid_f32, ln2_gain, ln2_bias)
        h_two = h_two_f.astype(BF16)
        pre_act = [(dot(h_two, w, 1, 1) + b).astype(BF16) for w, b in zip(w1, b_1_all)]
        gelus = [jax.vjp(gelu_tanh, t.astype(F32)) for t in pre_act]
        hidden = [g[0].astype(BF16) for g in gelus]

        w2 = both(w2_mine, hidden[1])
        d_out_img = lax.optimization_barrier(join_tokens(after((d_moved,), hidden[0])[0]))
        theirs_2 = dot(hidden[1], d_out_img, 0, 0)
        w2_late = after(w2, theirs_2)
        d_hidden = [dot(d_out_img, w, 1, 1).astype(BF16) for w in w2_late]
        sum_2 = dot(hidden[0], d_out_img, 0, 0) + swap(theirs_2)
        grad_w_2 = scatter_rows(sum_2).astype(BF16)
        d_pre = [g[1](d.astype(F32))[0].astype(BF16) for g, d in zip(gelus, d_hidden)]
        (h_two_late,) = after((h_two,), sum_2)
        theirs_1 = dot(d_pre[1], h_two_late, 0, 0)
        w1_late = after(w1, theirs_1)
        d_h_two = (dot(d_pre[0], w1_late[0], 1, 0) + dot(d_pre[1], w1_late[1], 1, 0)).astype(BF16)
        sum_1 = dot(d_pre[0], h_two_late, 0, 0) + swap(theirs_1)
        grad_w_1 = scatter_rows(sum_1).astype(BF16).T
        w2_late = after(w2, sum_1)
        y_img = (mid_f32 + dot(hidden[0], w2_late[0], 1, 0) + dot(hidden[1], w2_late[1], 1, 0) + b_2.astype(F32)).astype(BF16)
        y_out = to_tokens(y_img)
        d_mid_ln, g_ln2_gain, g_ln2_bias = ln2_pull(d_h_two.astype(F32))
        d_mid = (d_out_img.astype(F32) + d_mid_ln).astype(BF16)
        mixed_late = after(mixed, sum_1)
        theirs_o = dot(mixed_late[1], d_mid, 0, 0)
        d_mixed = [dot(d_mid, w, 1, 1).astype(BF16) for w in wo]
        sum_o = dot(mixed_late[0], d_mid, 0, 0) + swap(theirs_o)
        grad_w_o = scatter_rows(sum_o).astype(BF16).reshape(my_heads, head_dim, width)
        qkv_late = after(qkv, sum_o)
        d_qkv = [attend_back(t, d, images, my_heads, head_dim) for t, d in zip(qkv_late, d_mixed)]
        theirs_qkv = dot(d_qkv[1], h_one, 0, 0)
        w_qkv_late = after(w_qkv, theirs_qkv)
        d_h_one = (dot(d_qkv[0], w_qkv_late[0], 1, 0) + dot(d_qkv[1], w_qkv_late[1], 1, 0)).astype(BF16)
        sum_qkv = dot(d_qkv[0], h_one, 0, 0) + swap(theirs_qkv)
        g_qkv = scatter_rows(sum_qkv).astype(BF16).reshape(3, cols, width)
        grad_w_q, grad_w_k, grad_w_v = (g_qkv[i].T.reshape(width, my_heads, head_dim) for i in range(3))
        d_in_ln, g_ln1_gain, g_ln1_bias = ln1_pull(d_h_one.astype(F32))
        grad_x = to_tokens((d_mid.astype(F32) + d_in_ln).astype(BF16))

        def token_sum(t):
            return jnp.sum(t, axis=0, dtype=F32)

        me = lax.axis_index('tp')
        core, chip = lax.rem(me, 2), me // 2

        def halves(pair):
            sums = [token_sum(t) for t in pair]
            first = jnp.where(core == 0, sums[0], sums[1])
            second = jnp.where(core == 0, sums[1], sums[0])
            return [first, second]

        vecs = jnp.concatenate([g_ln1_gain, g_ln1_bias, token_sum(d_mid), g_ln2_gain, g_ln2_bias, token_sum(d_out_img)]
                               + halves(d_qkv) + halves(d_pre))
        sums = lax.psum(vecs.reshape(-1, width), 'tp').reshape(-1)
        six = [sums[i * width:(i + 1) * width] for i in range(6)]
        base = 6 * width
        g_b_qkv = lax.dynamic_slice(sums, (base + (core * chips + chip) * qkv_cols,), (qkv_cols,)).astype(BF16)
        grad_b_q = g_b_qkv[:cols].reshape(my_heads, head_dim)
        grad_b_v = g_b_qkv[2 * cols:].reshape(my_heads, head_dim)
        base += tp * qkv_cols
        grad_b_1 = lax.dynamic_slice(sums, (base + (core * chips + chip) * hid,), (hid,)).astype(BF16)
        return (y_out, grad_x, six[0], six[1], grad_w_q, grad_b_q, grad_w_k, grad_w_v, grad_b_v, grad_w_o,
                six[2].astype(BF16), six[3], six[4], grad_w_1, grad_b_1, grad_w_2, six[5].astype(BF16))

    return jax.shard_map(layer_body, mesh=mesh, in_specs=in_specs, out_specs=out_specs, check_vma=False)
```

time: 650 us -> 637 us (0.980)
  waiting for transfers between devices: 129 us -> 220 us
  blocking collectives: 148 us -> 65.7 us
  Pallas kernels: 0 us -> 76.1 us
  local copies, waits for them, and re-layouts: 88.8 us -> 37.8 us
  matrix products: 204 us -> 168 us
  other arithmetic: 47.4 us -> 25.3 us
  starting transfers between devices: 12.9 us -> 21 us
    all_gather x4, waiting for transfers between devices: 0.05 us -> 79 us  [gather_rows(): lax.all_gather(rows, 'tp', axis=0, tiled=True, axis_index_groups=rings)]
    pallas_call x0 -> x4, Pallas kernels: none -> 76.1 us  [the longest x2 42.9 us: attend_back(): pl.pallas_call(functools.partial(attend_back_kernel, heads, head_dim), gr...]
    reduce_scatter x4, waiting for transfers between devices: 115 us -> 56.9 us  [scatter_rows(): lax.psum_scatter(rows, 'tp', scatter_dimension=0, tiled=True, axis_index_...]
    all_to_all x1 -> x0, blocking collectives: 53.4 us -> none  [to_images(): return lax.all_to_all(t, 'tp', 0, 1, tiled=True).reshape(tokens, width)]
    all_gather x1 -> x0, blocking collectives: 49.4 us -> none  [layer_step(): b_all = lax.all_gather(b_small, 'tp')]
    dot_general x5 -> x0, matrix products: 39.7 us -> none  [the longest x2 24.8 us: attention_core(): jnp.einsum('bqhd,bkhd->bhqk', queries, keys, preferred_element_type=F32)]
    all_to_all x2, waiting for transfers between devices: 11.7 us -> 47.2 us  [to_tokens(): lax.all_to_all(t.reshape(images, patches, width), 'tp', 1, 0, tiled=True)]
    ppermute x0 -> x8, waiting for transfers between devices: none -> 22.7 us  [swap(): return lax.ppermute(t, 'tp', pairs)]
  transfers between devices with their start and end apart: 11 -> 20, of which waited for: 3 -> 8; matrix products, arithmetic and copies ran while one was open for 41% -> 27% of each run, Pallas kernels for 0% -> 12%
where the time goes in v2:
time: 637 us; the launch traced here: 629 us
  waiting for transfers between devices  220 us (35%)
  matrix products  168 us (26%)
  Pallas kernels  76.1 us (12%)
  blocking collectives  65.7 us (10%)
  local copies, waits for them, and re-layouts  37.8 us (6%)
  other arithmetic  25.3 us (4%)
  starting transfers between devices  21 us (3%)
  between operations  15.1 us (2%)
    dot_general x24, matrix products, dot(): lax.dot_general(a, b, (((ca,), (cb,)), ((), ())), preferred_element_type=...  168 us
    all_gather x4, waiting for transfers between devices, gather_rows(): lax.all_gather(rows, 'tp', axis=0, tiled=True, axis_index_groups=rings)  79 us
    psum x1, blocking collectives, layer_body(): sums = lax.psum(vecs.reshape(-1, width), 'tp').reshape(-1)  65.7 us
    reduce_scatter x4, waiting for transfers between devices, scatter_rows(): lax.psum_scatter(rows, 'tp', scatter_dimension=0, tiled=True, axis_index_...  56.9 us
    all_to_all x2, waiting for transfers between devices, to_tokens(): lax.all_to_all(t.reshape(images, patches, width), 'tp', 1, 0, tiled=True)  47.2 us
    pallas_call x2, Pallas kernels, attend_back(): pl.pallas_call(functools.partial(attend_back_kernel, heads, head_dim), gr...  42.9 us
    pallas_call x2, Pallas kernels, attend(): pl.pallas_call(functools.partial(attend_kernel, heads, head_dim), grid=(i...  33.2 us
    ppermute x8, waiting for transfers between devices, swap(): return lax.ppermute(t, 'tp', pairs)  22.7 us
  transfers between devices with their start and end apart: 20, of which 8 were waited for; matrix products, arithmetic and copies ran while one was open for 27% of the time, Pallas kernels for 12%

profile of v2, /device:TPU:112, one launch (start us, length us, event | category | flops | bytes accessed | tf_op | source)
XLA Modules:
  0.0 628.7 jit_solution(4452426464985163697)
XLA Ops:
  9.3 0.9 dynamic-update-slice.13
  10.4 2.1 pad_maximum_fusion
  14.1 5.3 all-to-all-start
  19.5 53.5 %all-gather.5.cloned.1.call-done = bf16[1600,1024]{1,0:T(8,128)(2,1)} async-done(((bf16[400,1024]{1,0:T(8,128)(2,1)}), bf16[1600,1024]{1,0:T(8,128)(2,1)}) %all-gather.5.cloned.1.call-update) | async-done | bytes 3276816 | tf_op jit(solution)/shard_map/all_gather | solution.py:131
  73.0 1.3 copy-done.4
  74.3 2.0 copy.39
  78.0 1.9 slice.113
  80.0 7.1 %add_convert_fusion.3.qkv_ref = bf16[1024,1536]{1,0:T(8,128)(2,1)} fusion(bf16[1536,1024]{1,0:T(8,128)(2,1)} %bitcast.106, f32[1536]{0:T(1024)S(1)} %reshape.250, bf16[1024,1024]{1,0:T(8,128)(2,1)S(1)} %bitcast.95, f32[1024]{0:T(1024)S(1)} %copy-done.40, f32[1024]{0:T(1024)S(1)} %copy-done.29, f32[1024]{0:T(1024)S(1)} %fusion.56, ...), kind=kOutput, calls=%fused_computation.56 | convolution fusion | flops 3230662656 | bytes 8411136 | tf_op jit(solution)/shard_map/dot_general | solution.py:31
  87.1 7.8 %all-gather.7.cloned.1.call-done = bf16[512,1024]{1,0:T(8,128)(2,1)} async-done(((bf16[128,1024]{1,0:T(8,128)(2,1)}), bf16[512,1024]{1,0:T(8,128)(2,1)}) %all-gather.7.cloned.1.call-update) | async-done | bytes 1048592 | tf_op jit(solution)/shard_map/all_gather | solution.py:131
  94.9 3.9 slice.115
  99.6 7.1 %add_convert_fusion.2.qkv_ref = bf16[1024,1536]{1,0:T(8,128)(2,1)} fusion(bf16[1536,1024]{1,0:T(8,128)(2,1)} %bitcast.108, f32[1536]{0:T(1024)S(1)} %reshape.251, bf16[1024,1024]{1,0:T(8,128)(2,1)S(1)} %bitcast.96, f32[1024]{0:T(1024)S(1)} %copy-done.40, f32[1024]{0:T(1024)S(1)} %copy-done.29, f32[1024]{0:T(1024)S(1)} %fusion.56, ...), kind=kOutput, calls=%fused_computation.55 | convolution fusion | flops 3230662656 | bytes 8411136 | tf_op jit(solution)/shard_map/dot_general | solution.py:31
  106.7 16.6 %attend.3 = bf16[1024,512]{1,0:T(8,128)(2,1)} custom-call(bf16[1024,1536]{1,0:T(8,128)(2,1)} %add_convert_fusion.2.qkv_ref), custom_call_target="tpu_custom_call" | custom-call | flops 2147483648 | bytes 4194304 | tf_op jit(solution)/shard_map/attend/pallas_call | solution.py:84
  123.3 17.6 %all-gather.9.cloned.1.call-done = bf16[2048,1024]{0,1:T(8,128)(2,1)} async-done(((bf16[512,1024]{0,1:T(8,128)(2,1)}), bf16[2048,1024]{0,1:T(8,128)(2,1)}) %all-gather.9.cloned.1.call-update) | async-done | bytes 4194320 | tf_op jit(solution)/shard_map/all_gather | solution.py:131
  141.0 4.6 all-to-all-start.1
  146.2 16.7 %attend.2 = bf16[1024,512]{1,0:T(8,128)(2,1)} custom-call(bf16[1024,1536]{1,0:T(8,128)(2,1)} %add_convert_fusion.3.qkv_ref), custom_call_target="tpu_custom_call" | custom-call | flops 2147483648 | bytes 4194304 | tf_op jit(solution)/shard_map/attend/pallas_call | solution.py:84
  163.6 2.9 fusion.67
  166.5 2.8 convert_reduce_fusion.6
  171.5 1.3 copy-done.16
  172.8 8.5 %fusion.13 = (bf16[1024,2048]{1,0:T(8,128)(2,1)}, bf16[1024,2048]{1,0:T(8,128)(2,1)}) fusion(f32[2048]{0:T(1024)S(1)} %bitcast.132, bf16[1024,1024]{1,0:T(8,128)(2,1)S(1)} %fusion.35, bf16[2048,1024]{0,1:T(8,128)(2,1)S(1)} %copy-done.35), kind=kOutput, calls=%fused_computation.25 | convolution fusion | flops 4320133120 | bytes 14688256 | tf_op jit(solution)/shard_map/dot_general | solution.py:31
  181.3 11.4 %all-to-all-done.1 = bf16[8,4,32,1024]{3,2,1,0:T(8,128)(2,1)} async-done(((bf16[8,4,32,1024]{3,2,1,0:T(8,128)(2,1)}), bf16[8,4,32,1024]{3,2,1,0:T(8,128)(2,1)}, u32[]{:S(2)}, u32[]{:S(2)}) %all-to-all-start.1) | async-done | bytes 2097184 | tf_op jit(solution)/shard_map/all_to_all | solution.py:148
  192.7 2.0 copy.40
  195.5 10.3 %fusion.19 = (bf16[1024,2048]{1,0:T(8,128)(2,1)S(1)}, bf16[1024,2048]{1,0:T(8,128)(2,1)}) fusion(f32[2048]{0:T(1024)S(1)} %bitcast.133, bf16[1024,1024]{1,0:T(8,128)(2,1)S(1)} %copy-done.17, bf16[2048,1024]{0,1:T(8,128)(2,1)} %collective-permute-done.2), kind=kOutput, calls=%fused_computation.31 | convolution fusion | flops 4320133120 | bytes 14688256 | tf_op jit(solution)/shard_map/dot_general | solution.py:31
  205.8 7.0 %fusion.68 = f32[2048,1024]{1,0:T(8,128)} fusion(bf16[1024,2048]{1,0:T(8,128)(2,1)S(1)} %get-tuple-element.114, bf16[1024,1024]{1,0:T(8,128)(2,1)S(1)} %bitcast.116), kind=kOutput, calls=%fused_computation.137 | convolution fusion | flops 4294967296 | bytes 14680064 | tf_op jit(solution)/shard_map/dot_general | solution.py:31
  213.3 18.9 %collective-permute-done.3 = bf16[2048,1024]{1,0:T(8,128)(2,1)S(1)} collective-permute-done((bf16[2048,1024]{1,0:T(8,128)(2,1)}, bf16[2048,1024]{1,0:T(8,128)(2,1)S(1)}, u32[]{:S(2)}, u32[]{:S(2)}) %collective-permute-start.3) | collective-permute-done | bytes 4194336 | tf_op jit(solution)/shard_map/ppermute | solution.py:137
  232.2 14.3 %convert_reduce_fusion = (f32[2048]{0:T(1024)}, bf16[1024,2048]{1,0:T(8,128)(2,1)}) fusion(bf16[1024,2048]{1,0:T(8,128)(2,1)} %get-tuple-element.115, bf16[1024,1024]{1,0:T(8,128)(2,1)S(1)} %bitcast.117, bf16[2048,1024]{1,0:T(8,128)(2,1)S(1)} %collective-permute-done.3), kind=kOutput, calls=%fused_computation.34 | convolution fusion | flops 4347394048 | bytes 14688256 | tf_op jit(solution)/shard_map/dot_general | solution.py:31
  246.4 9.1 %convolution_add_fusion.2 = f32[2048,1024]{1,0:T(8,128)} fusion(f32[2048,1024]{1,0:T(8,128)} %collective-permute-done.4, bf16[1024,2048]{1,0:T(8,128)(2,1)S(1)} %copy-done.43, bf16[1024,1024]{1,0:T(8,128)(2,1)S(1)} %bitcast.118), kind=kOutput, calls=%fused_computation.94 | convolution fusion | flops 4297064448 | bytes 23068672 | tf_op jit(solution)/shard_map/dot_general | solution.py:31
  255.5 7.3 %fusion.69 = f32[2048,1024]{1,0:T(8,128)S(1)} fusion(bf16[1024,2048]{1,0:T(8,128)(2,1)} %get-tuple-element.121, bf16[1024,1024]{1,0:T(8,128)(2,1)} %copy-done.16), kind=kOutput, calls=%fused_computation.138 | convolution fusion | flops 4294967296 | bytes 14680064 | tf_op jit(solution)/shard_map/dot_general | solution.py:31
  263.0 12.8 %convert_reduce_fusion.1 = (f32[2048]{0:T(1024)S(1)}, bf16[1024,2048]{1,0:T(8,128)(2,1)}) fusion(bf16[1024,2048]{1,0:T(8,128)(2,1)} %get-tuple-element.113, bf16[1024,1024]{1,0:T(8,128)(2,1)S(1)} %bitcast.119, bf16[2048,1024]{1,0:T(8,128)(2,1)S(1)} %copy-done.36), kind=kOutput, calls=%fused_computation.35 | convolution fusion | flops 4347394048 | bytes 14688256 | tf_op jit(solution)/shard_map/dot_general | solution.py:31
  275.8 8.4 %fusion.71 = f32[1024,1024]{1,0:T(8,128)} fusion(bf16[1024,2048]{1,0:T(8,128)(2,1)S(1)} %copy-done.46, bf16[2048,1024]{0,1:T(8,128)(2,1)} %collective-permute-done.2), kind=kOutput, calls=%fused_computation.140 | convolution fusion | flops 4294967296 | bytes 12582912 | tf_op jit(solution)/shard_map/dot_general | solution.py:31
  284.2 9.5 %convert_reduce_fusion.5 = (f32[1024]{0:T(1024)S(1)}, f32[1024]{0:T(1024)S(1)}, bf16[1024,1024]{1,0:T(8,128)(2,1)S(1)}) fusion(f32[1024]{0:T(1024)S(1)} %copy-done.31, f32[1024]{0:T(1024)S(1)} %broadcast_multiply_fusion, bf16[1024,1024]{1,0:T(8,128)(2,1)S(1)} %copy-done.3, f32[1024,1024]{1,0:T(8,128)} %fusion.71, ...), kind=kOutput, calls=%fused_computation.45 | convolution fusion | flops 4304402432 | bytes 16793600 | tf_op jit(solution)/shard_map/dot_general | solution.py:31
  293.8 1.3 copy-done.19
  295.1 2.7 fusion.50
  297.8 9.7 %convolution_add_fusion.1 = f32[2048,1024]{1,0:T(8,128)} fusion(f32[2048,1024]{1,0:T(8,128)S(1)} %collective-permute-done.5, bf16[1024,2048]{1,0:T(8,128)(2,1)} %get-tuple-element.119, bf16[1024,1024]{1,0:T(8,128)(2,1)S(1)} %copy-done.18), kind=kOutput, calls=%fused_computation.93 | convolution fusion | flops 4297064448 | bytes 23068672 | tf_op jit(solution)/shard_map/dot_general | solution.py:31
  307.5 7.7 %fusion.70 = f32[1024,1024]{1,0:T(8,128)S(1)} fusion(bf16[1024,2048]{1,0:T(8,128)(2,1)} %get-tuple-element.112, bf16[2048,1024]{1,0:T(8,128)(2,1)} %all-gather.11.cloned.1.call-done), kind=kOutput, calls=%fused_computation.139 | convolution fusion | flops 4294967296 | bytes 12582912 | tf_op jit(solution)/shard_map/dot_general | solution.py:31
  315.2 7.4 %convert_reduce_fusion.8 = (f32[1024]{0:T(1024)S(1)}, bf16[1024,1024]{1,0:T(8,128)(2,1)S(1)}, f32[1024]{0:T(1024)S(1)}, bf16[1024,1024]{1,0:T(8,128)(2,1)}) fusion(f32[1024]{0:T(1024)S(1)} %negate_multiply_fusion.1, f32[1024]{0:T(1024)S(1)} %multiply_multiply_fusion.1, f32[1024]{0:T(1024)S(1)} %broadcast_multiply_fusion, ...), kind=kOutput, calls=%fused_computation.64 | convolution fusion | flops 4314888192 | bytes 23101440 | tf_op jit(solution)/shard_map/dot_general | solution.py:31
  322.6 1.3 fusion.72
  324.3 3.8 collective-permute-done.6
  328.1 2.6 convolution_add_fusion.3
  333.0 3.6 convolution_convert_fusion.da_ref
  336.6 21.6 %attend_back.3 = bf16[1024,1536]{1,0:T(8,128)(2,1)} custom-call(bf16[1024,1536]{1,0:T(8,128)(2,1)} %add_convert_fusion.2.qkv_ref, bf16[1024,512]{1,0:T(8,128)(2,1)} %convolution_convert_fusion.da_ref), custom_call_target="tpu_custom_call" | custom-call | flops 4294967296 | bytes 7340032 | tf_op jit(solution)/shard_map/attend_back/pallas_call | solution.py:100
  358.2 7.7 %fusion.59 = f32[1536,1024]{1,0:T(8,128)} fusion(bf16[1024,1536]{1,0:T(8,128)(2,1)} %attend_back.3, bf16[1024,1024]{1,0:T(8,128)(2,1)S(1)} %bitcast.98, f32[1024]{0:T(1024)S(1)} %copy-done.41, f32[1024]{0:T(1024)S(1)} %copy-done.30, f32[1024]{0:T(1024)S(1)} %copy-done.27, f32[1024]{0:T(1024)S(1)} %copy-done.23), kind=kOutput, calls=%fused_computation.132 | convolution fusion | flops 3227516928 | bytes 11550720 | tf_op jit(solution)/shard_map/dot_general | solution.py:31
  366.4 2.3 convolution_convert_fusion.1.da_ref
  368.6 21.3 %attend_back.2 = bf16[1024,1536]{1,0:T(8,128)(2,1)} custom-call(bf16[1024,1536]{1,0:T(8,128)(2,1)} %add_convert_fusion.3.qkv_ref, bf16[1024,512]{1,0:T(8,128)(2,1)} %convolution_convert_fusion.1.da_ref), custom_call_target="tpu_custom_call" | custom-call | flops 4294967296 | bytes 7340032 | tf_op jit(solution)/shard_map/attend_back/pallas_call | solution.py:100
  389.9 8.7 %convolution_add_fusion = f32[1536,1024]{1,0:T(8,128)} fusion(f32[1536,1024]{1,0:T(8,128)} %collective-permute-done.7, bf16[1024,1536]{1,0:T(8,128)(2,1)} %attend_back.2, bf16[1024,1024]{1,0:T(8,128)(2,1)S(1)} %bitcast.99, f32[1024]{0:T(1024)S(1)} %copy-done.41, f32[1024]{0:T(1024)S(1)} %copy-done.30, f32[1024]{0:T(1024)S(1)} %copy-done.27, ...), kind=kOutput, calls=%fused_computation.72 | convolution fusion | flops 3229089792 | bytes 17842176 | tf_op jit(solution)/shard_map/dot_general | solution.py:31
  398.7 4.5 copy.41
  403.2 4.7 all-to-all-start.2
  408.0 47.2 %all-to-all-done.2 = bf16[4,256,1024]{2,0,1:T(4,128)(2,1)} async-done(((bf16[4,256,1024]{2,0,1:T(4,128)(2,1)}), bf16[4,256,1024]{2,0,1:T(4,128)(2,1)}, u32[]{:S(2)}, u32[]{:S(2)}) %all-to-all-start.2) | async-done | bytes 2097184 | tf_op jit(solution)/shard_map/all_to_all | solution.py:154
  455.2 3.8 copy.42
  459.0 5.4 fusion.73
  464.5 4.2 convert_reduce_fusion.4
  468.7 2.7 fusion.51
  471.4 2.0 fusion.39
  473.4 2.9 copy.43
  476.3 3.8 all-to-all-start.3
  480.2 2.6 convert_reduce_fusion.3
  483.7 65.7 %psum.7 = f32[13,1024]{1,0:T(8,128)S(1)} all-reduce(f32[13,1024]{1,0:T(8,128)S(1)} %reshape.244), channel_id=1, replica_groups=mesh['dp'=2,'tp'=8] {'tp'}, use_global_device_ids=true, to_apply=%region_18.0 | all-reduce | flops 13312 | bytes 106496 | tf_op jit(solution)/shard_map/psum | solution.py:239
  552.5 2.0 copy.44
  554.6 1.8 convert_element_type.222
  556.4 2.8 convert_element_type.226
  559.2 1.7 convert_bitcast_fusion
  560.9 1.3 copy.45
  562.2 56.9 %reduce-scatter.5.cloned.1.call-done = f32[384,1024]{1,0:T(8,128)} async-done(((f32[1536,1024]{1,0:T(8,128)}), f32[384,1024]{1,0:T(8,128)}) %reduce-scatter.5.cloned.1.call-update) | async-done | bytes 1572880 | tf_op jit(solution)/shard_map/reduce_scatter | solution.py:134
  619.2 1.5 convert_element_type.220
  620.7 0.9 fusion.64
  (176 shorter events, 18.8 us)
Async XLA Ops:
  7.2 65.8 %all-gather.5.cloned.1.call-start = ((), (), s32[]{:S(2)}) async-start(), calls=%async_computation.8 | async-start | bytes 4096000 | tf_op jit(solution)/shard_map/all_gather | solution.py:131
  12.5 82.4 %all-gather.7.cloned.1.call-start = ((), (), s32[]{:S(2)}) async-start(), calls=%async_computation.9 | async-start | bytes 1310720 | tf_op jit(solution)/shard_map/all_gather | solution.py:131
  13.3 127.6 %all-gather.9.cloned.1.call-start = ((), (), s32[]{:S(2)}) async-start(), calls=%async_computation.10 | async-start | bytes 5242880 | tf_op jit(solution)/shard_map/all_gather | solution.py:131
  14.1 58.9 %all-to-all-start = ((bf16[8,4,32,1024]{3,2,1,0:T(8,128)(2,1)}), bf16[8,4,32,1024]{3,2,1,0:T(8,128)(2,1)S(1)}, u32[]{:S(2)}, u32[]{:S(2)}) async-start(bf16[8,4,32,1024]{3,2,1,0:T(8,128)(2,1)} %bitcast.113), calls=%async_computation | async-start | bytes 4194304 | tf_op jit(solution)/shard_map/all_to_all | solution.py:148
  19.4 193.4 %all-gather.11.cloned.1.call-start = ((), (), s32[]{:S(2)}) async-start(), calls=%async_computation.11 | async-start | bytes 5242880 | tf_op jit(solution)/shard_map/all_gather | solution.py:131
  73.0 21.9 %collective-permute-start = (bf16[1600,1024]{1,0:T(8,128)(2,1)}, bf16[1600,1024]{1,0:T(8,128)(2,1)}, u32[]{:S(2)}, u32[]{:S(2)}) collective-permute-start(bf16[1600,1024]{1,0:T(8,128)(2,1)} %all-gather.5.cloned.1.call-done), channel_id=1, source_target_pairs={{0,1},{1,0},{2,3},{3,2},{4,5},{5,4},{6,7},{7,6},{8,9},{9,8},{10,11... | collective-permute-start | bytes 9830408 | tf_op jit(solution)/shard_map/ppermute | solution.py:137
  74.3 3.7 copy-start.13
  76.3 90.2 %copy-start = (bf16[4,8,32,1024]{3,2,1,0:T(8,128)(2,1)}, bf16[4,8,32,1024]{3,2,1,0:T(8,128)(2,1)S(1)}, u32[]{:S(2)}) copy-start(bf16[4,8,32,1024]{3,2,1,0:T(8,128)(2,1)S(1)} %copy.39) | copy-start | bytes 6291460
  76.6 22.9 %copy-start.22 = (f32[1024]{0:T(1024)}, f32[1024]{0:T(1024)S(1)}, u32[]{:S(2)}) copy-start(f32[1024]{0:T(1024)S(1)} %broadcast_multiply_fusion.1) | copy-start | bytes 12292
  76.6 3.3 copy-start.29
  76.7 3.3 copy-start.40
  78.0 21.6 %copy-start.26 = (f32[1024]{0:T(1024)}, f32[1024]{0:T(1024)S(1)}, u32[]{:S(2)}) copy-start(f32[1024]{0:T(1024)S(1)} %fusion.56) | copy-start | bytes 12292
  94.9 71.6 %collective-permute-start.1 = (bf16[512,1024]{1,0:T(8,128)(2,1)}, bf16[512,1024]{1,0:T(8,128)(2,1)}, u32[]{:S(2)}, u32[]{:S(2)}) collective-permute-start(bf16[512,1024]{1,0:T(8,128)(2,1)} %all-gather.7.cloned.1.call-done), channel_id=1, source_target_pairs={{0,1},{1,0},{2,3},{3,2},{4,5},{5,4},{6,7},{7,6},{8,9},{9,8},{10,11... | collective-permute-start | bytes 3145736 | tf_op jit(solution)/shard_map/ppermute | solution.py:137
  106.7 34.3 %copy-start.33 = (bf16[1024]{0:T(1024)(128)(2,1)S(1)}, bf16[1024]{0:T(1024)(128)(2,1)}, u32[]{:S(2)}) copy-start(bf16[1024]{0:T(1024)(128)(2,1)} %param.27) | copy-start | bytes 6148
  140.9 54.5 %collective-permute-start.2 = (bf16[2048,1024]{0,1:T(8,128)(2,1)}, bf16[2048,1024]{0,1:T(8,128)(2,1)}, u32[]{:S(2)}, u32[]{:S(2)}) collective-permute-start(bf16[2048,1024]{0,1:T(8,128)(2,1)} %all-gather.9.cloned.1.call-done), channel_id=1, source_target_pairs={{0,1},{1,0},{2,3},{3,2},{4,5},{5,4},{6,7},{7,6},{8,9},{9,8},{10,11... | collective-permute-start | bytes 12582920 | tf_op jit(solution)/shard_map/ppermute | solution.py:137
  141.0 51.7 %all-to-all-start.1 = ((bf16[8,4,32,1024]{3,2,1,0:T(8,128)(2,1)}), bf16[8,4,32,1024]{3,2,1,0:T(8,128)(2,1)}, u32[]{:S(2)}, u32[]{:S(2)}) async-start(bf16[8,4,32,1024]{3,2,1,0:T(8,128)(2,1)} %bitcast.114), calls=%async_computation.1 | async-start | bytes 4194304 | tf_op jit(solution)/shard_map/all_to_all | solution.py:148
  145.6 409.0 %reduce-scatter.7.cloned.1.call-start = ((), (), s32[]{:S(2)}) async-start(), calls=%async_computation.13 | async-start | bytes 2621440 | tf_op jit(solution)/shard_map/reduce_scatter | solution.py:134
  163.6 2.9 copy-start.21
  166.5 4.2 copy-start.31
  166.5 4.2 copy-start.32
  169.3 1.3 copy-start.2
  169.3 3.5 copy-start.35
  192.7 2.8 copy-start.17
  194.7 68.3 %copy-start.14 = (bf16[4,8,32,1024]{3,2,1,0:T(8,128)(2,1)}, bf16[4,8,32,1024]{3,2,1,0:T(8,128)(2,1)S(1)}, u32[]{:S(2)}) copy-start(bf16[4,8,32,1024]{3,2,1,0:T(8,128)(2,1)S(1)} %copy.40) | copy-start | bytes 6291460
  205.8 7.0 %copy-start.44 = (bf16[1024,2048]{1,0:T(8,128)(2,1)}, bf16[1024,2048]{1,0:T(8,128)(2,1)S(1)}, u32[]{:S(2)}) copy-start(bf16[1024,2048]{1,0:T(8,128)(2,1)S(1)} %get-tuple-element.114) | copy-start | bytes 12582916
  212.8 33.7 %collective-permute-start.4 = (f32[2048,1024]{1,0:T(8,128)}, f32[2048,1024]{1,0:T(8,128)}, u32[]{:S(2)}, u32[]{:S(2)}) collective-permute-start(f32[2048,1024]{1,0:T(8,128)} %fusion.68), channel_id=1, source_target_pairs={{0,1},{1,0},{2,3},{3,2},{4,5},{5,4},{6,7},{7,6},{8,9},{9,8},{10,11... | collective-permute-start | bytes 25165832 | tf_op jit(solution)/shard_map/ppermute | solution.py:137
  212.8 19.4 %collective-permute-start.3 = (bf16[2048,1024]{1,0:T(8,128)(2,1)}, bf16[2048,1024]{1,0:T(8,128)(2,1)S(1)}, u32[]{:S(2)}, u32[]{:S(2)}) collective-permute-start(bf16[2048,1024]{1,0:T(8,128)(2,1)} %all-gather.11.cloned.1.call-done), channel_id=1, source_target_pairs={{0,1},{1,0},{2,3},{3,2},{4,5},{5,4},{6,7},{7,6},{8,9},{9,8},{10,11... | collective-permute-start | bytes 12582920 | tf_op jit(solution)/shard_map/ppermute | solution.py:137
  232.1 14.3 %copy-start.37 = (bf16[2048,1024]{1,0:T(8,128)(2,1)}, bf16[2048,1024]{1,0:T(8,128)(2,1)S(1)}, u32[]{:S(2)}) copy-start(bf16[2048,1024]{1,0:T(8,128)(2,1)S(1)} %collective-permute-done.3) | copy-start | bytes 12582916
  232.2 14.3 %copy-start.43 = (bf16[1024,2048]{1,0:T(8,128)(2,1)S(1)}, bf16[1024,2048]{1,0:T(8,128)(2,1)}, u32[]{:S(2)}) copy-start(bf16[1024,2048]{1,0:T(8,128)(2,1)} %get-tuple-element.112) | copy-start | bytes 12582916
  255.5 7.5 %copy-start.34 = (bf16[1024]{0:T(1024)(128)(2,1)S(1)}, bf16[1024]{0:T(1024)(128)(2,1)}, u32[]{:S(2)}) copy-start(bf16[1024]{0:T(1024)(128)(2,1)} %param.33) | copy-start | bytes 6148
  255.5 7.5 %copy-start.36 = (bf16[2048,1024]{1,0:T(8,128)(2,1)S(1)}, bf16[2048,1024]{1,0:T(8,128)(2,1)}, u32[]{:S(2)}) copy-start(bf16[2048,1024]{1,0:T(8,128)(2,1)} %all-gather.11.cloned.1.call-done) | copy-start | bytes 12582916
  262.8 35.0 %collective-permute-start.5 = (f32[2048,1024]{1,0:T(8,128)S(1)}, f32[2048,1024]{1,0:T(8,128)S(1)}, u32[]{:S(2)}, u32[]{:S(2)}) collective-permute-start(f32[2048,1024]{1,0:T(8,128)S(1)} %fusion.69), channel_id=1, source_target_pairs={{0,1},{1,0},{2,3},{3,2},{4,5},{5,4},{6,7},{7,6},{8,9},{9,8},{10,11... | collective-permute-start | bytes 25165832 | tf_op jit(solution)/shard_map/ppermute | solution.py:137
  263.0 12.8 %copy-start.46 = (bf16[1024,2048]{1,0:T(8,128)(2,1)S(1)}, bf16[1024,2048]{1,0:T(8,128)(2,1)}, u32[]{:S(2)}) copy-start(bf16[1024,2048]{1,0:T(8,128)(2,1)} %get-tuple-element.121) | copy-start | bytes 12582916
  275.8 8.4 %copy-start.3 = (bf16[1024,1024]{1,0:T(8,128)(2,1)S(1)}, bf16[1024,1024]{1,0:T(8,128)(2,1)}, u32[]{:S(2)}) copy-start(bf16[1024,1024]{1,0:T(8,128)(2,1)} %copy-done.2) | copy-start | bytes 6291460
  293.8 1.3 copy-start.19
  293.8 4.0 copy-start.18
  307.5 7.7 %copy-start.15 = (bf16[4,8,32,1024]{3,2,1,0:T(8,128)(2,1)S(1)}, bf16[4,8,32,1024]{3,2,1,0:T(8,128)(2,1)}, u32[]{:S(2)}) copy-start(bf16[4,8,32,1024]{3,2,1,0:T(8,128)(2,1)} %copy-done.14) | copy-start | bytes 6291460
  307.5 7.7 %copy-start.20 = (bf16[1024,1024]{1,0:T(8,128)(2,1)S(1)}, bf16[1024,1024]{1,0:T(8,128)(2,1)}, u32[]{:S(2)}) copy-start(bf16[1024,1024]{1,0:T(8,128)(2,1)} %copy-done.19) | copy-start | bytes 6291460
  307.5 7.7 %copy-start.38 = (bf16[2048,1024]{1,0:T(8,128)(2,1)S(1)}, bf16[2048,1024]{1,0:T(8,128)(2,1)}, u32[]{:S(2)}) copy-start(bf16[2048,1024]{1,0:T(8,128)(2,1)} %copy-done.37) | copy-start | bytes 12582916
  307.5 7.7 %copy-start.45 = (bf16[1024,2048]{1,0:T(8,128)(2,1)S(1)}, bf16[1024,2048]{1,0:T(8,128)(2,1)}, u32[]{:S(2)}) copy-start(bf16[1024,2048]{1,0:T(8,128)(2,1)} %copy-done.44) | copy-start | bytes 12582916
  322.6 5.5 copy-start.5
  322.6 5.5 copy-start.42
  323.9 4.2 collective-permute-start.6
  330.8 225.6 %reduce-scatter.11.cloned.1.call-start = ((), (), s32[]{:S(2)}) async-start(), calls=%async_computation.15 | async-start | bytes 10485760 | tf_op jit(solution)/shard_map/reduce_scatter | solution.py:134
  331.4 1.6 copy-start.6
  331.4 227.7 %reduce-scatter.9.cloned.1.call-start = ((), (), s32[]{:S(2)}) async-start(), calls=%async_computation.14 | async-start | bytes 10485760 | tf_op jit(solution)/shard_map/reduce_scatter | solution.py:134
  332.3 286.9 %reduce-scatter.5.cloned.1.call-start = ((), (), s32[]{:S(2)}) async-start(), calls=%async_computation.12 | async-start | bytes 7864320 | tf_op jit(solution)/shard_map/reduce_scatter | solution.py:134
  336.6 21.6 %copy-start.1 = (bf16[4,8,32,1024]{3,2,1,0:T(8,128)(2,1)S(1)}, bf16[4,8,32,1024]{3,2,1,0:T(8,128)(2,1)}, u32[]{:S(2)}) copy-start(bf16[4,8,32,1024]{3,2,1,0:T(8,128)(2,1)} %copy-done) | copy-start | bytes 6291460
  336.6 21.6 %copy-start.23 = (f32[1024]{0:T(1024)S(1)}, f32[1024]{0:T(1024)}, u32[]{:S(2)}) copy-start(f32[1024]{0:T(1024)} %copy-done.22) | copy-start | bytes 12292
  336.6 21.6 %copy-start.27 = (f32[1024]{0:T(1024)S(1)}, f32[1024]{0:T(1024)}, u32[]{:S(2)}) copy-start(f32[1024]{0:T(1024)} %copy-done.26) | copy-start | bytes 12292
  336.6 21.6 %copy-start.30 = (f32[1024]{0:T(1024)S(1)}, f32[1024]{0:T(1024)}, u32[]{:S(2)}) copy-start(f32[1024]{0:T(1024)} %param.19) | copy-start | bytes 12292
  336.6 21.6 %copy-start.41 = (f32[1024]{0:T(1024)S(1)}, f32[1024]{0:T(1024)}, u32[]{:S(2)}) copy-start(f32[1024]{0:T(1024)} %param.20) | copy-start | bytes 12292
  358.2 8.1 %copy-start.7 = (bf16[1024,1024]{1,0:T(8,128)(2,1)S(1)}, bf16[1024,1024]{1,0:T(8,128)(2,1)}, u32[]{:S(2)}) copy-start(bf16[1024,1024]{1,0:T(8,128)(2,1)} %copy-done.5) | copy-start | bytes 6291460
  358.2 8.1 %copy-start.39 = (bf16[512,1024]{1,0:T(8,128)(2,1)S(1)}, bf16[512,1024]{1,0:T(8,128)(2,1)}, u32[]{:S(2)}) copy-start(bf16[512,1024]{1,0:T(8,128)(2,1)} %all-gather.7.cloned.1.call-done) | copy-start | bytes 3145732
  366.0 23.9 %collective-permute-start.7 = (f32[1536,1024]{1,0:T(8,128)}, f32[1536,1024]{1,0:T(8,128)}, u32[]{:S(2)}, u32[]{:S(2)}) collective-permute-start(f32[1536,1024]{1,0:T(8,128)} %fusion.59), channel_id=1, source_target_pairs={{0,1},{1,0},{2,3},{3,2},{4,5},{5,4},{6,7},{7,6},{8,9},{9,8},{10,11... | collective-permute-start | bytes 18874376 | tf_op jit(solution)/shard_map/ppermute | solution.py:137
  403.2 52.0 %all-to-all-start.2 = ((bf16[4,256,1024]{2,0,1:T(4,128)(2,1)}), bf16[4,256,1024]{2,0,1:T(4,128)(2,1)}, u32[]{:S(2)}, u32[]{:S(2)}) async-start(bf16[4,256,1024]{2,0,1:T(4,128)(2,1)} %copy.41), calls=%async_computation.2 | async-start | bytes 4194304 | tf_op jit(solution)/shard_map/all_to_all | solution.py:154
  455.2 3.8 copy-start.9
  459.0 5.5 copy-start.10
  459.0 5.5 copy-start.11
  464.5 4.2 copy-start.25
  468.7 2.8 copy-start.8
  476.3 76.2 %all-to-all-start.3 = ((bf16[4,256,1024]{2,0,1:T(4,128)(2,1)}), bf16[4,256,1024]{2,0,1:T(4,128)(2,1)S(1)}, u32[]{:S(2)}, u32[]{:S(2)}) async-start(bf16[4,256,1024]{2,0,1:T(4,128)(2,1)} %copy.43), calls=%async_computation.3 | async-start | bytes 4194304 | tf_op jit(solution)/shard_map/all_to_all | solution.py:154
  480.2 2.9 copy-start.12
  480.2 3.4 copy-start.28
  (3 other events, 3.2 us)
Sparse Core Ops, SparseCore 0:
  12.6 60.3 all-gather.4
  74.5 20.3 all-gather.6
  96.5 44.4 all-gather.8
  142.3 63.9 all-gather.10
  330.9 24.4 reduce-scatter.6
  357.6 95.7 reduce-scatter.10
  455.8 101.4 reduce-scatter.8
  559.6 59.4 reduce-scatter.4

commit v3 on v2

--- a/solution.py
+++ b/solution.py
@@ -4,6 +4,7 @@
 import jax.numpy as jnp
 from jax import lax
 from jax.experimental import pallas as pl
+from jax.experimental.pallas import tpu as pltpu
 from jax.sharding import PartitionSpec as P
 
 LN_EPS = 1e-6
@@ -109,6 +110,41 @@
     )(qkv, d_mixed)
 
 
+def sum_kernel(n, vec_ref, out_ref, slots, send_sems, recv_sems, local_sem):
+    me = lax.axis_index('tp')
+    barrier = pltpu.get_barrier_semaphore()
+    for step in range(1, n):
+        pl.semaphore_signal(barrier, inc=1, device_id={'tp': lax.rem(me + step, n)}, device_id_type=pl.DeviceIdType.MESH)
+    pl.semaphore_wait(barrier, n - 1)
+    own = pltpu.make_async_copy(vec_ref, slots.at[me], local_sem)
+    own.start()
+    copies = [pltpu.make_async_remote_copy(src_ref=vec_ref, dst_ref=slots.at[me], send_sem=send_sems.at[step - 1],
+                                           recv_sem=recv_sems.at[step - 1], device_id={'tp': lax.rem(me + step, n)},
+                                           device_id_type=pl.DeviceIdType.MESH) for step in range(1, n)]
+    for copy in copies:
+        copy.start()
+    own.wait()
+    for copy in copies:
+        copy.wait()
+    total = slots[0]
+    for i in range(1, n):
+        total = total + slots[i]
+    out_ref[...] = total
+
+
+def sum_over_tp(vecs, n):
+    return pl.pallas_call(
+        functools.partial(sum_kernel, n),
+        out_shape=jax.ShapeDtypeStruct(vecs.shape, F32),
+        in_specs=[pl.BlockSpec(memory_space=pltpu.VMEM)],
+        out_specs=pl.BlockSpec(memory_space=pltpu.VMEM),
+        scratch_shapes=[pltpu.VMEM((n, *vecs.shape), F32), pltpu.SemaphoreType.DMA((n - 1,)), pltpu.SemaphoreType.DMA((n - 1,)),
+                        pltpu.SemaphoreType.DMA],
+        compiler_params=pltpu.CompilerParams(collective_id=0, has_side_effects=True),
+        name="sum_over_tp",
+    )(vecs)
+
+
 def solution(mesh):
     act_spec = P('dp', 'tp', None)
     replicated = P()
@@ -140,6 +176,7 @@
         width, my_heads, head_dim = w_q.shape
         cols = my_heads * head_dim
         qkv_cols = 3 * cols
+        my_rows = qkv_cols + cols
         hid = w_1.shape[1]
         images, patches = x.shape[0] // tp, x.shape[1] * tp
         tokens = images * patches
@@ -151,7 +188,11 @@
             return blocks.swapaxes(0, 1).reshape(tokens, width)
 
         def to_tokens(t):
-            return lax.all_to_all(t.reshape(images, patches, width), 'tp', 1, 0, tiled=True)
+            blocks = t.reshape(images, tp, patches // tp, width).swapaxes(0, 1)
+            return lax.all_to_all(blocks, 'tp', 0, 0, tiled=True).reshape(tp * images, patches // tp, width)
+
+        def token_sum(t):
+            return jnp.sum(t, axis=0, dtype=F32)
 
         def both(mine, token=None):
             return mine, swap(mine if token is None else after((mine,), token)[0])
@@ -159,27 +200,27 @@
         bias_row = jnp.concatenate([b_q.reshape(cols), jnp.zeros((cols,), BF16), b_v.reshape(cols), b_1,
                                     jnp.zeros((width - qkv_cols - hid,), BF16)])
         qkv_rows = jnp.concatenate([w_q.reshape(width, cols).T, w_k.reshape(width, cols).T, w_v.reshape(width, cols).T,
-                                    jnp.broadcast_to(bias_row[None], (PAD, width))], axis=0)
+                                    w_o.reshape(cols, width), jnp.broadcast_to(bias_row[None], (PAD, width))], axis=0)
         packed = both(gather_rows(qkv_rows))
         x_img = lax.optimization_barrier(join_tokens(to_images(x)))
-        wo_mine, w1_mine, w2_mine = gather_rows(w_o.reshape(cols, width)), gather_rows(w_1.T), gather_rows(w_2)
-
-        w_qkv, b_qkv, b_1_all = [], [], []
+        w1_mine, w2_mine = gather_rows(w_1.T), gather_rows(w_2)
+
+        w_qkv, wo, b_qkv, b_1_all = [], [], [], []
         for half in packed:
-            blocks = half.reshape(chips, qkv_cols + PAD, width)
+            blocks = half.reshape(chips, my_rows + PAD, width)
             w_qkv.append(blocks[:, :qkv_cols].reshape(chips * qkv_cols, width))
-            b_qkv.append(blocks[:, qkv_cols, :qkv_cols].reshape(chips * qkv_cols).astype(F32))
-            b_1_all.append(blocks[:, qkv_cols, qkv_cols:qkv_cols + hid].reshape(chips * hid).astype(F32))
+            wo.append(blocks[:, qkv_cols:my_rows].reshape(chips * cols, width))
+            b_qkv.append(blocks[:, my_rows, :qkv_cols].reshape(chips * qkv_cols).astype(F32))
+            b_1_all.append(blocks[:, my_rows, qkv_cols:qkv_cols + hid].reshape(chips * hid).astype(F32))
 
         x_f32 = x_img.astype(F32)
         h_one_f, ln1_pull = jax.vjp(layer_norm, x_f32, ln1_gain, ln1_bias)
         h_one = h_one_f.astype(BF16)
         qkv = [(dot(h_one, w, 1, 1) + b).astype(BF16) for w, b in zip(w_qkv, b_qkv)]
         d_moved = to_images(after((d_out,), qkv[0])[0])
-        wo = both(wo_mine, qkv[0])
         mixed = [attend(t, images, my_heads, head_dim) for t in qkv]
-        w1 = both(w1_mine, mixed[1])
         x_mid = (x_f32 + dot(mixed[0], wo[0], 1, 0) + dot(mixed[1], wo[1], 1, 0) + b_o.astype(F32)).astype(BF16)
+        w1 = both(w1_mine, x_mid)
         mid_f32 = x_mid.astype(F32)
         h_two_f, ln2_pull = jax.vjp(layer_norm, mid_f32, ln2_gain, ln2_bias)
         h_two = h_two_f.astype(BF16)
@@ -187,14 +228,15 @@
         gelus = [jax.vjp(gelu_tanh, t.astype(F32)) for t in pre_act]
         hidden = [g[0].astype(BF16) for g in gelus]
 
-        w2 = both(w2_mine, hidden[1])
         d_out_img = lax.optimization_barrier(join_tokens(after((d_moved,), hidden[0])[0]))
         theirs_2 = dot(hidden[1], d_out_img, 0, 0)
-        w2_late = after(w2, theirs_2)
-        d_hidden = [dot(d_out_img, w, 1, 1).astype(BF16) for w in w2_late]
         sum_2 = dot(hidden[0], d_out_img, 0, 0) + swap(theirs_2)
         grad_w_2 = scatter_rows(sum_2).astype(BF16)
+        w2 = both(w2_mine, sum_2)
+        d_first = dot(d_out_img, after(w2[:1], sum_2)[0], 1, 1).astype(BF16)
+        d_hidden = [d_first, dot(d_out_img, after(w2[1:], d_first)[0], 1, 1).astype(BF16)]
         d_pre = [g[1](d.astype(F32))[0].astype(BF16) for g, d in zip(gelus, d_hidden)]
+        d_pre_sums = [token_sum(t) for t in d_pre]
         (h_two_late,) = after((h_two,), sum_2)
         theirs_1 = dot(d_pre[1], h_two_late, 0, 0)
         w1_late = after(w1, theirs_1)
@@ -210,33 +252,31 @@
         theirs_o = dot(mixed_late[1], d_mid, 0, 0)
         d_mixed = [dot(d_mid, w, 1, 1).astype(BF16) for w in wo]
         sum_o = dot(mixed_late[0], d_mid, 0, 0) + swap(theirs_o)
-        grad_w_o = scatter_rows(sum_o).astype(BF16).reshape(my_heads, head_dim, width)
         qkv_late = after(qkv, sum_o)
         d_qkv = [attend_back(t, d, images, my_heads, head_dim) for t, d in zip(qkv_late, d_mixed)]
         theirs_qkv = dot(d_qkv[1], h_one, 0, 0)
         w_qkv_late = after(w_qkv, theirs_qkv)
         d_h_one = (dot(d_qkv[0], w_qkv_late[0], 1, 0) + dot(d_qkv[1], w_qkv_late[1], 1, 0)).astype(BF16)
         sum_qkv = dot(d_qkv[0], h_one, 0, 0) + swap(theirs_qkv)
-        g_qkv = scatter_rows(sum_qkv).astype(BF16).reshape(3, cols, width)
+        sum_all = jnp.concatenate([sum_qkv.reshape(chips, qkv_cols, width), sum_o.reshape(chips, cols, width)], axis=1)
+        g_all = scatter_rows(sum_all.reshape(chips * my_rows, width)).astype(BF16)
+        grad_w_o = g_all[qkv_cols:].reshape(my_heads, head_dim, width)
+        g_qkv = g_all[:qkv_cols].reshape(3, cols, width)
         grad_w_q, grad_w_k, grad_w_v = (g_qkv[i].T.reshape(width, my_heads, head_dim) for i in range(3))
         d_in_ln, g_ln1_gain, g_ln1_bias = ln1_pull(d_h_one.astype(F32))
         grad_x = to_tokens((d_mid.astype(F32) + d_in_ln).astype(BF16))
 
-        def token_sum(t):
-            return jnp.sum(t, axis=0, dtype=F32)
-
         me = lax.axis_index('tp')
         core, chip = lax.rem(me, 2), me // 2
 
-        def halves(pair):
-            sums = [token_sum(t) for t in pair]
+        def halves(sums):
             first = jnp.where(core == 0, sums[0], sums[1])
             second = jnp.where(core == 0, sums[1], sums[0])
             return [first, second]
 
         vecs = jnp.concatenate([g_ln1_gain, g_ln1_bias, token_sum(d_mid), g_ln2_gain, g_ln2_bias, token_sum(d_out_img)]
-                               + halves(d_qkv) + halves(d_pre))
-        sums = lax.psum(vecs.reshape(-1, width), 'tp').reshape(-1)
+                               + halves([token_sum(t) for t in d_qkv]) + halves(d_pre_sums))
+        sums = sum_over_tp(vecs.reshape(-1, width), tp).reshape(-1)
         six = [sums[i * width:(i + 1) * width] for i in range(6)]
         base = 6 * width
         g_b_qkv = lax.dynamic_slice(sums, (base + (core * chips + chip) * qkv_cols,), (qkv_cols,)).astype(BF16)

time: 637 us -> 569 us (0.89)
  the two profiles are of different devices: /device:TPU:112 before, /device:TPU:113 now
where the time goes in v3:
time: 569 us; the launch traced here: 559 us
  waiting for transfers between devices  166 us (29%)
  matrix products  163 us (29%)
  Pallas kernels  115 us (20%)
  local copies, waits for them, and re-layouts  40.7 us (7%)
  other arithmetic  34.5 us (6%)
  starting transfers between devices  23.9 us (4%)
  between operations  15.1 us (3%)
    dot_general x24, matrix products, dot(): lax.dot_general(a, b, (((ca,), (cb,)), ((), ())), preferred_element_type=...  163 us
    all_gather x3, waiting for transfers between devices, gather_rows(): lax.all_gather(rows, 'tp', axis=0, tiled=True, axis_index_groups=rings)  78 us
    all_to_all x2, waiting for transfers between devices, to_tokens(): lax.all_to_all(blocks, 'tp', 0, 0, tiled=True)  49.2 us
    pallas_call x2, Pallas kernels, attend_back(): pl.pallas_call(functools.partial(attend_back_kernel, heads, head_dim), gr...  42.6 us
    pallas_call x1, Pallas kernels, sum_over_tp(): pl.pallas_call(functools.partial(sum_kernel, n), out_shape=jax.ShapeDtype...  39.8 us
    pallas_call x2, Pallas kernels, attend(): pl.pallas_call(functools.partial(attend_kernel, heads, head_dim), grid=(i...  33.1 us
    ppermute x7, waiting for transfers between devices, swap(): return lax.ppermute(t, 'tp', pairs)  27.9 us
    unnamed x92, local copies, waits for them, and re-layouts  18.4 us
  transfers between devices with their start and end apart: 17, of which 7 were waited for; matrix products, arithmetic and copies ran while one was open for 36% of the time, Pallas kernels for 21%

profile of v3, /device:TPU:113, one launch (start us, length us, event | category | flops | bytes accessed | tf_op | source)
XLA Modules:
  0.0 559.0 jit_solution(13985712483645150102)
XLA Ops:
  15.4 6.0 %all-to-all-start = ((bf16[8,4,32,1024]{3,2,1,0:T(8,128)(2,1)}), bf16[8,4,32,1024]{3,2,1,0:T(8,128)(2,1)S(1)}, u32[]{:S(2)}, u32[]{:S(2)}) async-start(bf16[8,4,32,1024]{3,2,1,0:T(8,128)(2,1)} %bitcast.126), calls=%async_computation | async-start | bytes 4194304 | tf_op jit(solution)/shard_map/all_to_all | solution.py:185
  22.2 60.7 %all-gather.4.cloned.1.call-done = bf16[2112,1024]{1,0:T(8,128)(2,1)} async-done(((bf16[528,1024]{1,0:T(8,128)(2,1)}), bf16[2112,1024]{1,0:T(8,128)(2,1)}) %all-gather.4.cloned.1.call-update) | async-done | bytes 4325392 | tf_op jit(solution)/shard_map/all_gather | solution.py:167
  83.4 1.3 copy-done.8
  84.7 2.0 copy.39
  88.4 2.0 slice.129
  90.5 7.2 %add_convert_fusion.3.qkv_ref = bf16[1024,1536]{1,0:T(8,128)(2,1)} fusion(bf16[1536,1024]{1,0:T(8,128)(2,1)} %bitcast.122, f32[1536]{0:T(1024)S(1)} %reshape.278, bf16[1024,1024]{1,0:T(8,128)(2,1)S(1)} %bitcast.98, f32[1024]{0:T(1024)S(1)} %copy-done.30, f32[1024]{0:T(1024)S(1)} %copy-done.24, f32[1024]{0:T(1024)S(1)} %fusion.56, ...), kind=kOutput, calls=%fused_computation.57 | convolution fusion | flops 3230662656 | bytes 8411136 | tf_op jit(solution)/shard_map/dot_general | solution.py:32
  97.7 16.6 %attend.2 = bf16[1024,512]{1,0:T(8,128)(2,1)} custom-call(bf16[1024,1536]{1,0:T(8,128)(2,1)} %add_convert_fusion.3.qkv_ref), custom_call_target="tpu_custom_call" | custom-call | flops 2147483648 | bytes 4194304 | tf_op jit(solution)/shard_map/attend/pallas_call | solution.py:85
  114.2 4.5 fusion.74
  118.7 1.3 slice.134
  120.0 3.8 slice.132
  124.6 7.0 %add_convert_fusion.2.qkv_ref = bf16[1024,1536]{1,0:T(8,128)(2,1)} fusion(bf16[1536,1024]{1,0:T(8,128)(2,1)} %bitcast.124, f32[1536]{0:T(1024)S(1)} %reshape.279, bf16[1024,1024]{1,0:T(8,128)(2,1)S(1)} %bitcast.99, f32[1024]{0:T(1024)S(1)} %copy-done.30, f32[1024]{0:T(1024)S(1)} %copy-done.24, f32[1024]{0:T(1024)S(1)} %fusion.56, ...), kind=kOutput, calls=%fused_computation.56 | convolution fusion | flops 3230662656 | bytes 8411136 | tf_op jit(solution)/shard_map/dot_general | solution.py:32
  131.6 16.5 %attend.3 = bf16[1024,512]{1,0:T(8,128)(2,1)} custom-call(bf16[1024,1536]{1,0:T(8,128)(2,1)} %add_convert_fusion.2.qkv_ref), custom_call_target="tpu_custom_call" | custom-call | flops 2147483648 | bytes 4194304 | tf_op jit(solution)/shard_map/attend/pallas_call | solution.py:85
  148.1 5.2 convert_reduce_fusion.6
  153.4 4.7 all-to-all-start.1
  159.5 2.5 fusion.45
  162.1 2.4 fusion.35
  164.5 1.3 copy-done.13
  165.8 8.5 %fusion.13 = (bf16[1024,2048]{1,0:T(8,128)(2,1)}, bf16[1024,2048]{1,0:T(8,128)(2,1)}) fusion(f32[2048]{0:T(1024)S(1)} %bitcast.143, bf16[1024,1024]{1,0:T(8,128)(2,1)S(1)} %fusion.35, bf16[2048,1024]{0,1:T(8,128)(2,1)S(1)} %copy-done.28), kind=kOutput, calls=%fused_computation.25 | convolution fusion | flops 4320133120 | bytes 14688256 | tf_op jit(solution)/shard_map/dot_general | solution.py:32
  174.3 10.2 %all-to-all-done.1 = bf16[8,4,32,1024]{3,2,1,0:T(8,128)(2,1)} async-done(((bf16[8,4,32,1024]{3,2,1,0:T(8,128)(2,1)}), bf16[8,4,32,1024]{3,2,1,0:T(8,128)(2,1)}, u32[]{:S(2)}, u32[]{:S(2)}) %all-to-all-start.1) | async-done | bytes 2097184 | tf_op jit(solution)/shard_map/all_to_all | solution.py:185
  184.5 1.9 copy.40
  187.3 7.0 %add_convert_fusion = bf16[1024,2048]{1,0:T(8,128)(2,1)S(1)} fusion(f32[2048]{0:T(1024)S(1)} %bitcast.144, bf16[1024,1024]{1,0:T(8,128)(2,1)S(1)} %copy-done.14, bf16[2048,1024]{0,1:T(8,128)(2,1)} %collective-permute-done.1), kind=kOutput, calls=%fused_computation.37 | convolution fusion | flops 4299161600 | bytes 10493952 | tf_op jit(solution)/shard_map/dot_general | solution.py:32
  194.3 8.0 %fusion.60 = f32[2048,1024]{1,0:T(8,128)} fusion(bf16[1024,1024]{1,0:T(8,128)(2,1)S(1)} %bitcast.107, bf16[1024,2048]{1,0:T(8,128)(2,1)S(1)} %add_convert_fusion), kind=kOutput, calls=%fused_computation.141 | convolution fusion | flops 4315938816 | bytes 14680064 | tf_op jit(solution)/shard_map/dot_general | solution.py:32
  203.4 13.0 %collective-permute-done.2 = f32[2048,1024]{1,0:T(8,128)} collective-permute-done((f32[2048,1024]{1,0:T(8,128)}, f32[2048,1024]{1,0:T(8,128)}, u32[]{:S(2)}, u32[]{:S(2)}) %collective-permute-start.2) | collective-permute-done | bytes 8388640 | tf_op jit(solution)/shard_map/ppermute | solution.py:173
  216.4 13.2 %convolution_add_fusion.2 = f32[2048,1024]{1,0:T(8,128)} fusion(f32[2048,1024]{1,0:T(8,128)} %collective-permute-done.2, bf16[1024,2048]{1,0:T(8,128)(2,1)} %get-tuple-element.110, bf16[1024,1024]{1,0:T(8,128)(2,1)} %bitcast.108), kind=kOutput, calls=%fused_computation.95 | convolution fusion | flops 4297064448 | bytes 23068672 | tf_op jit(solution)/shard_map/dot_general | solution.py:32
  229.6 17.3 %all-gather.8.cloned.1.call-done = bf16[2048,1024]{1,0:T(8,128)(2,1)} async-done(((bf16[512,1024]{1,0:T(8,128)(2,1)}), bf16[2048,1024]{1,0:T(8,128)(2,1)}) %all-gather.8.cloned.1.call-update) | async-done | bytes 4194320 | tf_op jit(solution)/shard_map/all_gather | solution.py:167
  248.0 13.3 %convert_reduce_fusion.1 = (f32[2048]{0:T(1024)}, bf16[1024,2048]{1,0:T(8,128)(2,1)S(1)}) fusion(bf16[1024,2048]{1,0:T(8,128)(2,1)} %get-tuple-element.111, bf16[1024,1024]{1,0:T(8,128)(2,1)} %bitcast.109, bf16[2048,1024]{1,0:T(8,128)(2,1)} %all-gather.8.cloned.1.call-done), kind=kOutput, calls=%fused_computation.36 | convolution fusion | flops 4347394048 | bytes 14688256 | tf_op jit(solution)/shard_map/dot_general | solution.py:32
  261.3 13.0 %convert_reduce_fusion = (f32[2048]{0:T(1024)S(1)}, bf16[1024,2048]{1,0:T(8,128)(2,1)S(1)}) fusion(bf16[1024,2048]{1,0:T(8,128)(2,1)S(1)} %copy-done.36, bf16[1024,1024]{1,0:T(8,128)(2,1)S(1)} %bitcast.110, bf16[2048,1024]{1,0:T(8,128)(2,1)} %collective-permute-done.3), kind=kOutput, calls=%fused_computation.35 | convolution fusion | flops 4347394048 | bytes 14688256 | tf_op jit(solution)/shard_map/dot_general | solution.py:32
  274.4 1.9 copy-done.34
  276.3 4.7 fusion.75
  281.1 13.1 %collective-permute-done.4 = f32[2048,1024]{1,0:T(8,128)S(1)} collective-permute-done((f32[2048,1024]{1,0:T(8,128)S(1)}, f32[2048,1024]{1,0:T(8,128)S(1)}, u32[]{:S(2)}, u32[]{:S(2)}) %collective-permute-start.4) | collective-permute-done | bytes 8388640 | tf_op jit(solution)/shard_map/ppermute | solution.py:173
  294.2 7.1 %convolution_add_fusion.1 = f32[2048,1024]{1,0:T(8,128)} fusion(f32[2048,1024]{1,0:T(8,128)S(1)} %collective-permute-done.4, bf16[1024,2048]{1,0:T(8,128)(2,1)S(1)} %get-tuple-element.94, bf16[1024,1024]{1,0:T(8,128)(2,1)S(1)} %copy-done.15), kind=kOutput, calls=%fused_computation.94 | convolution fusion | flops 4297064448 | bytes 23068672 | tf_op jit(solution)/shard_map/dot_general | solution.py:32
  301.4 8.3 %fusion.77 = f32[1024,1024]{1,0:T(8,128)S(1)} fusion(bf16[1024,2048]{1,0:T(8,128)(2,1)} %copy-done.34, bf16[2048,1024]{0,1:T(8,128)(2,1)} %collective-permute-done.1), kind=kOutput, calls=%fused_computation.149 | convolution fusion | flops 4294967296 | bytes 12582912 | tf_op jit(solution)/shard_map/dot_general | solution.py:32
  309.8 5.4 convert_reduce_fusion.5
  315.2 2.7 fusion.50
  317.9 2.3 convert_reduce_fusion.8
  321.7 2.3 convolution_convert_fusion.1.da_ref
  324.0 1.8 collective-permute-done.5
  325.8 2.6 convolution_add_fusion.3
  328.4 21.3 %attend_back.3 = bf16[1024,1536]{1,0:T(8,128)(2,1)} custom-call(bf16[1024,1536]{1,0:T(8,128)(2,1)} %add_convert_fusion.2.qkv_ref, bf16[1024,512]{1,0:T(8,128)(2,1)} %convolution_convert_fusion.1.da_ref), custom_call_target="tpu_custom_call" | custom-call | flops 4294967296 | bytes 7340032 | tf_op jit(solution)/shard_map/attend_back/pallas_call | solution.py:101
  349.7 8.0 %fusion.65 = f32[1536,1024]{1,0:T(8,128)} fusion(bf16[1024,1536]{1,0:T(8,128)(2,1)} %attend_back.3, bf16[1024,1024]{1,0:T(8,128)(2,1)S(1)} %bitcast.101, f32[1024]{0:T(1024)S(1)} %copy-done.30, f32[1024]{0:T(1024)S(1)} %copy-done.24, f32[1024]{0:T(1024)S(1)} %fusion.56, f32[1024]{0:T(1024)S(1)} %broadcast_multiply_fusion.1), kind=kOutput, calls=%fused_computation.142 | convolution fusion | flops 3227516928 | bytes 11550720 | tf_op jit(solution)/shard_map/dot_general | solution.py:32
  357.7 2.3 convolution_convert_fusion.2.da_ref
  359.9 21.3 %attend_back.2 = bf16[1024,1536]{1,0:T(8,128)(2,1)} custom-call(bf16[1024,1536]{1,0:T(8,128)(2,1)} %add_convert_fusion.3.qkv_ref, bf16[1024,512]{1,0:T(8,128)(2,1)} %convolution_convert_fusion.2.da_ref), custom_call_target="tpu_custom_call" | custom-call | flops 4294967296 | bytes 7340032 | tf_op jit(solution)/shard_map/attend_back/pallas_call | solution.py:101
  381.2 7.9 %convolution_add_fusion = f32[1536,1024]{1,0:T(8,128)S(1)} fusion(f32[1536,1024]{1,0:T(8,128)} %collective-permute-done.6, bf16[1024,1536]{1,0:T(8,128)(2,1)} %attend_back.2, bf16[1024,1024]{1,0:T(8,128)(2,1)S(1)} %bitcast.102, f32[1024]{0:T(1024)S(1)} %copy-done.30, f32[1024]{0:T(1024)S(1)} %copy-done.24, f32[1024]{0:T(1024)S(1)} %fusion.56, ...), kind=kOutput, calls=%fused_computation.73 | convolution fusion | flops 3229089792 | bytes 17842176 | tf_op jit(solution)/shard_map/dot_general | solution.py:32
  389.1 6.2 %pad_maximum_fusion = f32[4,512,1024]{2,1,0:T(8,128)} fusion(f32[4,128,1024]{2,1,0:T(8,128)} %bitcast.129, f32[4,384,1024]{2,1,0:T(8,128)S(1)} %bitcast.117), kind=kLoop, calls=%fused_computation.34 | loop fusion | flops 2097152 | bytes 16777216 | tf_op jit(solution)/shard_map/concatenate | solution.py:261
  396.0 7.7 %fusion.76 = f32[1024,1024]{1,0:T(8,128)S(1)} fusion(bf16[1024,2048]{1,0:T(8,128)(2,1)} %get-tuple-element.110, bf16[2048,1024]{1,0:T(8,128)(2,1)} %all-gather.8.cloned.1.call-done), kind=kOutput, calls=%fused_computation.148 | convolution fusion | flops 4294967296 | bytes 12582912 | tf_op jit(solution)/shard_map/dot_general | solution.py:32
  403.7 8.0 %fusion.49 = bf16[1024,1024]{1,0:T(8,128)(2,1)S(1)} fusion(f32[1024,1024]{1,0:T(8,128)S(1)} %fusion.76, bf16[1024,1024]{1,0:T(8,128)(2,1)S(1)} %copy-done.1, f32[1024]{0:T(1024)S(1)} %convert_element_type.201, bf16[2048,1024]{1,0:T(8,128)(2,1)} %collective-permute-done.3, bf16[1024,2048]{1,0:T(8,128)(2,1)S(1)} %copy-done.37), kind=kOutput, calls=%fused_computation.89 | convolution fusion | flops 4321181696 | bytes 16781312 | tf_op jit(solution)/shard_map/dot_general | solution.py:32
  411.7 1.6 copy.47
  413.3 5.1 all-to-all-start.2
  418.4 49.2 %all-to-all-done.2 = bf16[8,4,32,1024]{3,2,1,0:T(8,128)(2,1)} async-done(((bf16[8,4,32,1024]{3,2,1,0:T(8,128)(2,1)}), bf16[8,4,32,1024]{3,2,1,0:T(8,128)(2,1)}, u32[]{:S(2)}, u32[]{:S(2)}) %all-to-all-start.2) | async-done | bytes 2097184 | tf_op jit(solution)/shard_map/all_to_all | solution.py:192
  467.7 6.5 %fusion.79 = f32[1024,1024]{1,0:T(8,128)S(1)} fusion(bf16[1024,1536]{1,0:T(8,128)(2,1)} %attend_back.2, bf16[1536,1024]{1,0:T(8,128)(2,1)} %bitcast.123), kind=kOutput, calls=%fused_computation.151 | convolution fusion | flops 3221225472 | bytes 10485760 | tf_op jit(solution)/shard_map/dot_general | solution.py:32
  474.2 4.2 convert_reduce_fusion.4
  478.5 2.7 fusion.51
  481.3 2.0 fusion.39
  483.2 1.5 copy.46
  484.7 4.5 all-to-all-start.3
  489.3 2.5 convert_reduce_fusion.3
  493.3 39.8 %sum_over_tp.1 = f32[13,1024]{1,0:T(8,128)} custom-call(f32[13,1024]{1,0:T(8,128)} %reshape.269.vec_ref), custom_call_target="tpu_custom_call" | custom-call | tf_op jit(solution)/shard_map/sum_over_tp/pallas_call | solution.py:136
  537.3 1.5 fusion.72
  538.9 2.7 convert_element_type.222
  541.6 1.7 convert_bitcast_fusion
  543.4 1.3 copy.43
  544.7 1.7 convert_element_type.217
  547.4 3.2 copy.68
  550.6 1.3 copy.69
  (156 shorter events, 25.7 us)
Async XLA Ops:
  7.2 75.7 %all-gather.4.cloned.1.call-start = ((), (), s32[]{:S(2)}) async-start(), calls=%async_computation.7 | async-start | bytes 5406720 | tf_op jit(solution)/shard_map/all_gather | solution.py:167
  8.8 74.7 %copy-start.26 = (bf16[1024]{0:T(1024)(128)(2,1)S(1)}, bf16[1024]{0:T(1024)(128)(2,1)}, u32[]{:S(2)}) copy-start(bf16[1024]{0:T(1024)(128)(2,1)} %param.27) | copy-start | bytes 6148
  14.3 1.0 copy-start.16
  15.4 68.0 %all-to-all-start = ((bf16[8,4,32,1024]{3,2,1,0:T(8,128)(2,1)}), bf16[8,4,32,1024]{3,2,1,0:T(8,128)(2,1)S(1)}, u32[]{:S(2)}, u32[]{:S(2)}) async-start(bf16[8,4,32,1024]{3,2,1,0:T(8,128)(2,1)} %bitcast.126), calls=%async_computation | async-start | bytes 4194304 | tf_op jit(solution)/shard_map/all_to_all | solution.py:185
  21.4 132.0 %all-gather.6.cloned.1.call-start = ((), (), s32[]{:S(2)}) async-start(), calls=%async_computation.8 | async-start | bytes 5242880 | tf_op jit(solution)/shard_map/all_gather | solution.py:167
  82.9 35.8 %collective-permute-start = (bf16[2112,1024]{1,0:T(8,128)(2,1)}, bf16[2112,1024]{1,0:T(8,128)(2,1)}, u32[]{:S(2)}, u32[]{:S(2)}) collective-permute-start(bf16[2112,1024]{1,0:T(8,128)(2,1)} %all-gather.4.cloned.1.call-done), channel_id=1, source_target_pairs={{0,1},{1,0},{2,3},{3,2},{4,5},{5,4},{6,7},{7,6},{8,9},{9,8},{10,11... | collective-permute-start | bytes 12976136 | tf_op jit(solution)/shard_map/ppermute | solution.py:173
  83.4 1.3 copy-start.8
  84.7 3.6 copy-start.9
  87.8 0.6 copy-start.20
  88.4 2.1 copy-start.24
  88.4 2.1 copy-start.30
  88.4 25.8 %copy-start.18 = (bf16[4,128,1024]{2,1,0:T(8,128)(2,1)}, bf16[4,128,1024]{2,1,0:T(8,128)(2,1)S(1)}, u32[]{:S(2)}) copy-start(bf16[4,128,1024]{2,1,0:T(8,128)(2,1)S(1)} %slice.131) | copy-start | bytes 3145732
  153.4 8.7 %copy-start.22 = (f32[1024]{0:T(1024)S(1)}, f32[1024]{0:T(1024)}, u32[]{:S(2)}) copy-start(f32[1024]{0:T(1024)} %param.28) | copy-start | bytes 12292
  153.4 8.7 %copy-start.25 = (f32[1024]{0:T(1024)S(1)}, f32[1024]{0:T(1024)}, u32[]{:S(2)}) copy-start(f32[1024]{0:T(1024)} %param.29) | copy-start | bytes 12292
  153.4 33.9 %collective-permute-start.1 = (bf16[2048,1024]{0,1:T(8,128)(2,1)}, bf16[2048,1024]{0,1:T(8,128)(2,1)}, u32[]{:S(2)}, u32[]{:S(2)}) collective-permute-start(bf16[2048,1024]{0,1:T(8,128)(2,1)} %all-gather.6.cloned.1.call-done), channel_id=1, source_target_pairs={{0,1},{1,0},{2,3},{3,2},{4,5},{5,4},{6,7},{7,6},{8,9},{9,8},{10,11... | collective-permute-start | bytes 12582920 | tf_op jit(solution)/shard_map/ppermute | solution.py:173
  153.4 31.1 %all-to-all-start.1 = ((bf16[8,4,32,1024]{3,2,1,0:T(8,128)(2,1)}), bf16[8,4,32,1024]{3,2,1,0:T(8,128)(2,1)}, u32[]{:S(2)}, u32[]{:S(2)}) async-start(bf16[8,4,32,1024]{3,2,1,0:T(8,128)(2,1)} %bitcast.127), calls=%async_computation.1 | async-start | bytes 4194304 | tf_op jit(solution)/shard_map/all_to_all | solution.py:185
  158.1 88.7 %all-gather.8.cloned.1.call-start = ((), (), s32[]{:S(2)}) async-start(), calls=%async_computation.9 | async-start | bytes 5242880 | tf_op jit(solution)/shard_map/all_gather | solution.py:167
  158.6 7.2 %copy-start.28 = (bf16[2048,1024]{0,1:T(8,128)(2,1)S(1)}, bf16[2048,1024]{0,1:T(8,128)(2,1)}, u32[]{:S(2)}) copy-start(bf16[2048,1024]{0,1:T(8,128)(2,1)} %all-gather.6.cloned.1.call-done) | copy-start | bytes 12582916
  164.5 1.3 copy-start.13
  184.5 2.7 copy-start.14
  186.5 7.8 %copy-start.5 = (bf16[4,8,32,1024]{3,2,1,0:T(8,128)(2,1)}, bf16[4,8,32,1024]{3,2,1,0:T(8,128)(2,1)S(1)}, u32[]{:S(2)}) copy-start(bf16[4,8,32,1024]{3,2,1,0:T(8,128)(2,1)S(1)} %copy.40) | copy-start | bytes 6291460
  194.3 8.0 %copy-start.35 = (bf16[1024,2048]{1,0:T(8,128)(2,1)}, bf16[1024,2048]{1,0:T(8,128)(2,1)S(1)}, u32[]{:S(2)}) copy-start(bf16[1024,2048]{1,0:T(8,128)(2,1)S(1)} %add_convert_fusion) | copy-start | bytes 12582916
  202.3 14.1 %collective-permute-start.2 = (f32[2048,1024]{1,0:T(8,128)}, f32[2048,1024]{1,0:T(8,128)}, u32[]{:S(2)}, u32[]{:S(2)}) collective-permute-start(f32[2048,1024]{1,0:T(8,128)} %fusion.60), channel_id=1, source_target_pairs={{0,1},{1,0},{2,3},{3,2},{4,5},{5,4},{6,7},{7,6},{8,9},{9,8},{10,11... | collective-permute-start | bytes 25165832 | tf_op jit(solution)/shard_map/ppermute | solution.py:173
  203.3 335.6 %reduce-scatter.8.cloned.1.call-start = ((), (), s32[]{:S(2)}) async-start(), calls=%async_computation.12 | async-start | bytes 10485760 | tf_op jit(solution)/shard_map/reduce_scatter | solution.py:170
  246.8 14.5 %collective-permute-start.3 = (bf16[2048,1024]{1,0:T(8,128)(2,1)}, bf16[2048,1024]{1,0:T(8,128)(2,1)}, u32[]{:S(2)}, u32[]{:S(2)}) collective-permute-start(bf16[2048,1024]{1,0:T(8,128)(2,1)} %all-gather.8.cloned.1.call-done), channel_id=1, source_target_pairs={{0,1},{1,0},{2,3},{3,2},{4,5},{5,4},{6,7},{7,6},{8,9},{9,8},{10,11... | collective-permute-start | bytes 12582920 | tf_op jit(solution)/shard_map/ppermute | solution.py:173
  247.8 293.9 %reduce-scatter.6.cloned.1.call-start = ((), (), s32[]{:S(2)}) async-start(), calls=%async_computation.11 | async-start | bytes 10485760 | tf_op jit(solution)/shard_map/reduce_scatter | solution.py:170
  248.0 13.3 %copy-start.6 = (bf16[4,8,32,1024]{3,2,1,0:T(8,128)(2,1)S(1)}, bf16[4,8,32,1024]{3,2,1,0:T(8,128)(2,1)}, u32[]{:S(2)}) copy-start(bf16[4,8,32,1024]{3,2,1,0:T(8,128)(2,1)} %copy-done.5) | copy-start | bytes 6291460
  248.0 13.3 %copy-start.36 = (bf16[1024,2048]{1,0:T(8,128)(2,1)S(1)}, bf16[1024,2048]{1,0:T(8,128)(2,1)}, u32[]{:S(2)}) copy-start(bf16[1024,2048]{1,0:T(8,128)(2,1)} %copy-done.35) | copy-start | bytes 12582916
  261.3 32.9 %copy-start.32 = (bf16[1024,2048]{1,0:T(8,128)(2,1)}, bf16[1024,2048]{1,0:T(8,128)(2,1)S(1)}, u32[]{:S(2)}) copy-start(bf16[1024,2048]{1,0:T(8,128)(2,1)S(1)} %get-tuple-element.94) | copy-start | bytes 12582916
  261.3 15.0 %copy-start.15 = (bf16[1024,1024]{1,0:T(8,128)(2,1)S(1)}, bf16[1024,1024]{1,0:T(8,128)(2,1)}, u32[]{:S(2)}) copy-start(bf16[1024,1024]{1,0:T(8,128)(2,1)} %copy-done.13) | copy-start | bytes 6291460
  274.4 1.9 copy-start.34
  281.0 13.2 %collective-permute-start.4 = (f32[2048,1024]{1,0:T(8,128)S(1)}, f32[2048,1024]{1,0:T(8,128)S(1)}, u32[]{:S(2)}, u32[]{:S(2)}) collective-permute-start(f32[2048,1024]{1,0:T(8,128)S(1)} %fusion.75), channel_id=1, source_target_pairs={{0,1},{1,0},{2,3},{3,2},{4,5},{5,4},{6,7},{7,6},{8,9},{9,8},{10,11... | collective-permute-start | bytes 25165832 | tf_op jit(solution)/shard_map/ppermute | solution.py:173
  301.3 243.4 %reduce-scatter.4.cloned.1.call-start = ((), (), s32[]{:S(2)}) async-start(), calls=%async_computation.10 | async-start | bytes 10485760 | tf_op jit(solution)/shard_map/reduce_scatter | solution.py:170
  301.4 8.3 %copy-start = (bf16[1024,1024]{1,0:T(8,128)(2,1)S(1)}, bf16[1024,1024]{1,0:T(8,128)(2,1)}, u32[]{:S(2)}) copy-start(bf16[1024,1024]{1,0:T(8,128)(2,1)} %get-tuple-element.109) | copy-start | bytes 6291460
  301.4 8.3 %copy-start.29 = (bf16[2048,1024]{0,1:T(8,128)(2,1)S(1)}, bf16[2048,1024]{0,1:T(8,128)(2,1)}, u32[]{:S(2)}) copy-start(bf16[2048,1024]{0,1:T(8,128)(2,1)} %all-gather.6.cloned.1.call-done) | copy-start | bytes 12582916
  301.4 8.3 %copy-start.33 = (bf16[1024,2048]{1,0:T(8,128)(2,1)S(1)}, bf16[1024,2048]{1,0:T(8,128)(2,1)}, u32[]{:S(2)}) copy-start(bf16[1024,2048]{1,0:T(8,128)(2,1)} %copy-done.32) | copy-start | bytes 12582916
  315.1 2.7 copy-start.7
  317.9 2.4 copy-start.17
  320.2 5.5 copy-start.2
  321.5 4.2 copy-start.31
  321.5 4.2 collective-permute-start.5
  349.7 8.0 %copy-start.3 = (bf16[1024,1024]{1,0:T(8,128)(2,1)S(1)}, bf16[1024,1024]{1,0:T(8,128)(2,1)}, u32[]{:S(2)}) copy-start(bf16[1024,1024]{1,0:T(8,128)(2,1)} %copy-done.2) | copy-start | bytes 6291460
  349.7 8.0 %copy-start.19 = (bf16[4,128,1024]{2,1,0:T(8,128)(2,1)S(1)}, bf16[4,128,1024]{2,1,0:T(8,128)(2,1)}, u32[]{:S(2)}) copy-start(bf16[4,128,1024]{2,1,0:T(8,128)(2,1)} %copy-done.18) | copy-start | bytes 3145732
  357.6 23.6 %collective-permute-start.6 = (f32[1536,1024]{1,0:T(8,128)}, f32[1536,1024]{1,0:T(8,128)}, u32[]{:S(2)}, u32[]{:S(2)}) collective-permute-start(f32[1536,1024]{1,0:T(8,128)} %fusion.65), channel_id=1, source_target_pairs={{0,1},{1,0},{2,3},{3,2},{4,5},{5,4},{6,7},{7,6},{8,9},{9,8},{10,11... | collective-permute-start | bytes 18874376 | tf_op jit(solution)/shard_map/ppermute | solution.py:173
  395.3 0.7 copy-start.27
  396.0 7.7 %copy-start.1 = (bf16[1024,1024]{1,0:T(8,128)(2,1)S(1)}, bf16[1024,1024]{1,0:T(8,128)(2,1)}, u32[]{:S(2)}) copy-start(bf16[1024,1024]{1,0:T(8,128)(2,1)} %get-tuple-element.109) | copy-start | bytes 6291460
  396.0 7.7 %copy-start.37 = (bf16[1024,2048]{1,0:T(8,128)(2,1)S(1)}, bf16[1024,2048]{1,0:T(8,128)(2,1)}, u32[]{:S(2)}) copy-start(bf16[1024,2048]{1,0:T(8,128)(2,1)} %copy-done.35) | copy-start | bytes 12582916
  413.3 54.4 %all-to-all-start.2 = ((bf16[8,4,32,1024]{3,2,1,0:T(8,128)(2,1)}), bf16[8,4,32,1024]{3,2,1,0:T(8,128)(2,1)}, u32[]{:S(2)}, u32[]{:S(2)}) async-start(bf16[8,4,32,1024]{3,2,1,0:T(8,128)(2,1)} %bitcast.113), calls=%async_computation.2 | async-start | bytes 4194304 | tf_op jit(solution)/shard_map/all_to_all | solution.py:192
  467.7 6.5 %copy-start.10 = (bf16[4,384,1024]{2,1,0:T(8,128)(2,1)S(1)}, bf16[4,384,1024]{2,1,0:T(8,128)(2,1)}, u32[]{:S(2)}) copy-start(bf16[4,384,1024]{2,1,0:T(8,128)(2,1)} %slice.132) | copy-start | bytes 9437188
  467.7 6.5 %copy-start.11 = (bf16[1024,1536]{1,0:T(8,128)(2,1)S(1)}, bf16[1024,1536]{1,0:T(8,128)(2,1)}, u32[]{:S(2)}) copy-start(bf16[1024,1536]{1,0:T(8,128)(2,1)} %attend_back.3) | copy-start | bytes 9437188
  474.2 4.3 copy-start.21
  478.5 2.8 copy-start.4
  484.7 54.2 %all-to-all-start.3 = ((bf16[8,4,32,1024]{3,2,1,0:T(8,128)(2,1)}), bf16[8,4,32,1024]{3,2,1,0:T(8,128)(2,1)S(1)}, u32[]{:S(2)}, u32[]{:S(2)}) async-start(bf16[8,4,32,1024]{3,2,1,0:T(8,128)(2,1)} %bitcast.114), calls=%async_computation.3 | async-start | bytes 4194304 | tf_op jit(solution)/shard_map/all_to_all | solution.py:192
  489.2 2.9 copy-start.12
  489.2 3.4 copy-start.23
Sparse Core Ops, SparseCore 0:
  15.5 67.3 all-gather.3
  84.4 44.0 all-gather.5
  203.4 43.3 all-gather.7
  249.1 76.8 reduce-scatter.7
  328.1 76.1 reduce-scatter.5
  406.6 112.7 reduce-scatter.3

commit v4 on v3

--- a/solution.py
+++ b/solution.py
@@ -37,56 +37,64 @@
     return (lane >= head * head_dim) & (lane < (head + 1) * head_dim)
 
 
-def attend_kernel(heads, head_dim, qkv_ref, out_ref):
+def attend_kernel(blocks, heads, head_dim, qkv_ref, out_ref):
     cols = heads * head_dim
-    q, k, v = (qkv_ref[:, i * cols:(i + 1) * cols] for i in range(3))
     scale = 1.0 / math.sqrt(head_dim)
-    total = None
-    for head in range(heads):
-        mine = head_lanes(q.shape, head, head_dim)
-        s = dot(jnp.where(mine, q, jnp.zeros_like(q)), k, 1, 1) * scale
-        e = jnp.exp(s - jnp.max(s, axis=1, keepdims=True))
-        p = (e / jnp.sum(e, axis=1, keepdims=True)).astype(BF16)
-        a = dot(p, v, 1, 0)
-        total = a if total is None else jnp.where(mine, a, total)
-    out_ref[...] = total.astype(BF16)
-
-
-def attend_back_kernel(heads, head_dim, qkv_ref, da_ref, dqkv_ref):
+    for block in range(blocks):
+        base = block * 3 * cols
+        q, k, v = (qkv_ref[:, base + i * cols:base + (i + 1) * cols] for i in range(3))
+        total = None
+        for head in range(heads):
+            mine = head_lanes(q.shape, head, head_dim)
+            s = dot(jnp.where(mine, q, jnp.zeros_like(q)), k, 1, 1) * scale
+            e = jnp.exp(s - jnp.max(s, axis=1, keepdims=True))
+            p = (e * (1.0 / jnp.sum(e, axis=1, keepdims=True))).astype(BF16)
+            a = dot(p, v, 1, 0)
+            total = a if total is None else jnp.where(mine, a, total)
+        out_ref[:, block * cols:(block + 1) * cols] = total.astype(BF16)
+
+
+def attend_back_kernel(blocks, heads, head_dim, qkv_ref, da_ref, dqkv_ref):
     cols = heads * head_dim
-    q, k, v = (qkv_ref[:, i * cols:(i + 1) * cols] for i in range(3))
-    da = da_ref[...]
     scale = 1.0 / math.sqrt(head_dim)
-    dq = dk = dv = None
-    for head in range(heads):
-        mine = head_lanes(q.shape, head, head_dim)
-        zero = jnp.zeros_like(q)
-        s = dot(jnp.where(mine, k, zero), q, 1, 1) * scale
-        e = jnp.exp(s - jnp.max(s, axis=0, keepdims=True))
-        p32 = e / jnp.sum(e, axis=0, keepdims=True)
-        dv_h = dot(p32.astype(BF16), da, 1, 0)
-        dp = dot(jnp.where(mine, v, zero), da, 1, 1).astype(BF16).astype(F32)
-        ds = p32 * (dp - jnp.sum(dp * p32, axis=0, keepdims=True))
-        ds = (ds * scale).astype(BF16)
-        dk_h = dot(ds, q, 1, 0)
-        dq_h = dot(ds, k, 0, 0)
-        if head == 0:
-            dq, dk, dv = dq_h, dk_h, dv_h
-        else:
-            dq, dk, dv = jnp.where(mine, dq_h, dq), jnp.where(mine, dk_h, dk), jnp.where(mine, dv_h, dv)
-    for i, d in enumerate((dq, dk, dv)):
-        dqkv_ref[:, i * cols:(i + 1) * cols] = d.astype(BF16)
+    for block in range(blocks):
+        base = block * 3 * cols
+        q, k, v = (qkv_ref[:, base + i * cols:base + (i + 1) * cols] for i in range(3))
+        da = da_ref[:, block * cols:(block + 1) * cols]
+        dq = dk = dv = None
+        for head in range(heads):
+            mine = head_lanes(q.shape, head, head_dim)
+            zero = jnp.zeros_like(q)
+            s = dot(jnp.where(mine, k, zero), q, 1, 1) * scale
+            e = jnp.exp(s - jnp.max(s, axis=0, keepdims=True))
+            p32 = e * (1.0 / jnp.sum(e, axis=0, keepdims=True))
+            dv_h = dot(p32.astype(BF16), da, 1, 0)
+            dp = dot(jnp.where(mine, v, zero), da, 1, 1).astype(BF16).astype(F32)
+            ds = p32 * (dp - jnp.sum(dp * p32, axis=0, keepdims=True))
+            ds = (ds * scale).astype(BF16)
+            dk_h = dot(ds, q, 1, 0)
+            dq_h = dot(ds, k, 0, 0)
+            if head == 0:
+                dq, dk, dv = dq_h, dk_h, dv_h
+            else:
+                dq, dk, dv = jnp.where(mine, dq_h, dq), jnp.where(mine, dk_h, dk), jnp.where(mine, dv_h, dv)
+        for i, d in enumerate((dq, dk, dv)):
+            dqkv_ref[:, base + i * cols:base + (i + 1) * cols] = d.astype(BF16)
+
+
+GROUP = 4
 
 
 def attend(qkv, images, heads, head_dim):
     tokens, wide = qkv.shape
     patches, cols = tokens // images, heads * head_dim
     blocks = wide // (3 * cols)
+    group = min(GROUP, blocks)
     return pl.pallas_call(
-        functools.partial(attend_kernel, heads, head_dim),
-        grid=(images, blocks),
-        in_specs=[pl.BlockSpec((patches, 3 * cols), lambda i, j: (i, j))],
-        out_specs=pl.BlockSpec((patches, cols), lambda i, j: (i, j)),
+        functools.partial(attend_kernel, group, heads, head_dim),
+        grid=(images, blocks // group),
+        in_specs=[pl.BlockSpec((patches, group * 3 * cols), lambda i, j: (i, j))],
+        out_specs=pl.BlockSpec((patches, group * cols), lambda i, j: (i, j)),
         out_shape=jax.ShapeDtypeStruct((tokens, blocks * cols), BF16),
         cost_estimate=pl.CostEstimate(flops=images * blocks * heads * patches * patches * 1024, bytes_accessed=8 * tokens * blocks * cols,
                                       transcendentals=0),
@@ -98,11 +106,13 @@
     tokens, wide = qkv.shape
     patches, cols = tokens // images, heads * head_dim
     blocks = wide // (3 * cols)
+    group = min(GROUP, blocks)
     return pl.pallas_call(
-        functools.partial(attend_back_kernel, heads, head_dim),
-        grid=(images, blocks),
-        in_specs=[pl.BlockSpec((patches, 3 * cols), lambda i, j: (i, j)), pl.BlockSpec((patches, cols), lambda i, j: (i, j))],
-        out_specs=pl.BlockSpec((patches, 3 * cols), lambda i, j: (i, j)),
+        functools.partial(attend_back_kernel, group, heads, head_dim),
+        grid=(images, blocks // group),
+        in_specs=[pl.BlockSpec((patches, group * 3 * cols), lambda i, j: (i, j)),
+                  pl.BlockSpec((patches, group * cols), lambda i, j: (i, j))],
+        out_specs=pl.BlockSpec((patches, group * 3 * cols), lambda i, j: (i, j)),
         out_shape=jax.ShapeDtypeStruct((tokens, wide), BF16),
         cost_estimate=pl.CostEstimate(flops=images * blocks * heads * patches * patches * 2048, bytes_accessed=14 * tokens * blocks * cols,
                                       transcendentals=0),
@@ -188,8 +198,7 @@
             return blocks.swapaxes(0, 1).reshape(tokens, width)
 
         def to_tokens(t):
-            blocks = t.reshape(images, tp, patches // tp, width).swapaxes(0, 1)
-            return lax.all_to_all(blocks, 'tp', 0, 0, tiled=True).reshape(tp * images, patches // tp, width)
+            return lax.all_to_all(t.reshape(images, patches, width), 'tp', 1, 0, tiled=True)
 
         def token_sum(t):
             return jnp.sum(t, axis=0, dtype=F32)
@@ -197,10 +206,20 @@
         def both(mine, token=None):
             return mine, swap(mine if token is None else after((mine,), token)[0])
 
-        bias_row = jnp.concatenate([b_q.reshape(cols), jnp.zeros((cols,), BF16), b_v.reshape(cols), b_1,
-                                    jnp.zeros((width - qkv_cols - hid,), BF16)])
-        qkv_rows = jnp.concatenate([w_q.reshape(width, cols).T, w_k.reshape(width, cols).T, w_v.reshape(width, cols).T,
-                                    w_o.reshape(cols, width), jnp.broadcast_to(bias_row[None], (PAD, width))], axis=0)
+        def place(parts, rows):
+            low, placed = jnp.array(-jnp.inf, BF16), None
+            for t, start in parts:
+                spans = [(start, rows - start - t.shape[0], 0)] + [(0, 0, 0)] * (t.ndim - 1)
+                padded = lax.pad(t, low, spans)
+                placed = padded if placed is None else jnp.maximum(placed, padded)
+            return placed
+
+        rest = width - qkv_cols - hid
+        bias_row = place([(b_q.reshape(cols), 0), (jnp.zeros((cols,), BF16), cols), (b_v.reshape(cols), 2 * cols), (b_1, qkv_cols),
+                          (jnp.zeros((rest,), BF16), width - rest)], width)
+        pieces = [w_q.reshape(width, cols).T, w_k.reshape(width, cols).T, w_v.reshape(width, cols).T, w_o.reshape(cols, width)]
+        qkv_rows = place([(t, i * cols) for i, t in enumerate(pieces)]
+                         + [(jnp.broadcast_to(bias_row[None], (PAD, width)), my_rows)], my_rows + PAD)
         packed = both(gather_rows(qkv_rows))
         x_img = lax.optimization_barrier(join_tokens(to_images(x)))
         w1_mine, w2_mine = gather_rows(w_1.T), gather_rows(w_2)
@@ -259,10 +278,10 @@
         d_h_one = (dot(d_qkv[0], w_qkv_late[0], 1, 0) + dot(d_qkv[1], w_qkv_late[1], 1, 0)).astype(BF16)
         sum_qkv = dot(d_qkv[0], h_one, 0, 0) + swap(theirs_qkv)
         sum_all = jnp.concatenate([sum_qkv.reshape(chips, qkv_cols, width), sum_o.reshape(chips, cols, width)], axis=1)
-        g_all = scatter_rows(sum_all.reshape(chips * my_rows, width)).astype(BF16)
-        grad_w_o = g_all[qkv_cols:].reshape(my_heads, head_dim, width)
+        g_all = scatter_rows(sum_all.reshape(chips * my_rows, width))
+        grad_w_o = g_all[qkv_cols:].astype(BF16).reshape(my_heads, head_dim, width)
         g_qkv = g_all[:qkv_cols].reshape(3, cols, width)
-        grad_w_q, grad_w_k, grad_w_v = (g_qkv[i].T.reshape(width, my_heads, head_dim) for i in range(3))
+        grad_w_q, grad_w_k, grad_w_v = (g_qkv[i].T.astype(BF16).reshape(width, my_heads, head_dim) for i in range(3))
         d_in_ln, g_ln1_gain, g_ln1_bias = ln1_pull(d_h_one.astype(F32))
         grad_x = to_tokens((d_mid.astype(F32) + d_in_ln).astype(BF16))
 

time: 569 us -> 546 us (0.960)
  the two profiles are of different devices: /device:TPU:113 before, /device:TPU:112 now
where the time goes in v4:
time: 546 us; the launch traced here: 536 us
  matrix products  162 us (30%)
  waiting for transfers between devices  159 us (29%)
  Pallas kernels  92.3 us (17%)
  local copies, waits for them, and re-layouts  38.3 us (7%)
  other arithmetic  37.5 us (7%)
  starting transfers between devices  30.8 us (6%)
  between operations  15 us (3%)
    dot_general x24, matrix products, dot(): lax.dot_general(a, b, (((ca,), (cb,)), ((), ())), preferred_element_type=...  162 us
    all_gather x3, waiting for transfers between devices, gather_rows(): lax.all_gather(rows, 'tp', axis=0, tiled=True, axis_index_groups=rings)  79.5 us
    all_to_all x2, waiting for transfers between devices, to_tokens(): lax.all_to_all(t.reshape(images, patches, width), 'tp', 1, 0, tiled=True)  49.9 us
    pallas_call x1, Pallas kernels, sum_over_tp(): pl.pallas_call(functools.partial(sum_kernel, n), out_shape=jax.ShapeDtype...  41.1 us
    pallas_call x2, Pallas kernels, attend_back(): pl.pallas_call(functools.partial(attend_back_kernel, group, heads, head_d...  34.8 us
    ppermute x7, waiting for transfers between devices, swap(): return lax.ppermute(t, 'tp', pairs)  27.7 us
    pallas_call x2, Pallas kernels, attend(): pl.pallas_call(functools.partial(attend_kernel, group, heads, head_dim),...  16.4 us
  transfers between devices with their start and end apart: 17, of which 7 were waited for; matrix products, arithmetic and copies ran while one was open for 39% of the time, Pallas kernels for 17%

profile of v4, /device:TPU:112, one launch (start us, length us, event | category | flops | bytes accessed | tf_op | source)
XLA Modules:
  0.0 535.5 jit_solution(18086283995600635118)
XLA Ops:
  9.5 2.2 pad_maximum_fusion.1
  11.8 5.3 all-to-all-start
  17.9 61.2 %all-gather.4.cloned.1.call-done = bf16[2112,1024]{1,0:T(8,128)(2,1)} async-done(((bf16[528,1024]{1,0:T(8,128)(2,1)}), bf16[2112,1024]{1,0:T(8,128)(2,1)}) %all-gather.4.cloned.1.call-update) | async-done | bytes 4325392 | tf_op jit(solution)/shard_map/all_gather | solution.py:177
  80.4 2.0 copy.39
  84.2 2.0 slice.133
  86.2 7.2 %add_convert_fusion.3.qkv_ref = bf16[1024,1536]{1,0:T(8,128)(2,1)} fusion(bf16[1536,1024]{1,0:T(8,128)(2,1)} %bitcast.120, f32[1536]{0:T(1024)S(1)} %reshape.270, bf16[1024,1024]{1,0:T(8,128)(2,1)S(1)} %bitcast.98, f32[1024]{0:T(1024)S(1)} %copy-done.30, f32[1024]{0:T(1024)S(1)} %copy-done.24, f32[1024]{0:T(1024)S(1)} %fusion.56, ...), kind=kOutput, calls=%fused_computation.57 | convolution fusion | flops 3230662656 | bytes 8411136 | tf_op jit(solution)/shard_map/dot_general | solution.py:32
  93.4 8.2 %attend.2 = bf16[1024,512]{1,0:T(8,128)(2,1)} custom-call(bf16[1024,1536]{1,0:T(8,128)(2,1)} %add_convert_fusion.3.qkv_ref), custom_call_target="tpu_custom_call" | custom-call | flops 2147483648 | bytes 4194304 | tf_op jit(solution)/shard_map/attend/pallas_call | solution.py:93
  101.6 4.5 fusion.74
  106.1 1.3 slice.138
  107.4 3.8 slice.136
  112.0 7.0 %add_convert_fusion.2.qkv_ref = bf16[1024,1536]{1,0:T(8,128)(2,1)} fusion(bf16[1536,1024]{1,0:T(8,128)(2,1)} %bitcast.122, f32[1536]{0:T(1024)S(1)} %reshape.271, bf16[1024,1024]{1,0:T(8,128)(2,1)S(1)} %bitcast.99, f32[1024]{0:T(1024)S(1)} %copy-done.30, f32[1024]{0:T(1024)S(1)} %copy-done.24, f32[1024]{0:T(1024)S(1)} %fusion.56, ...), kind=kOutput, calls=%fused_computation.56 | convolution fusion | flops 3230662656 | bytes 8411136 | tf_op jit(solution)/shard_map/dot_general | solution.py:32
  119.1 8.2 %attend.3 = bf16[1024,512]{1,0:T(8,128)(2,1)} custom-call(bf16[1024,1536]{1,0:T(8,128)(2,1)} %add_convert_fusion.2.qkv_ref), custom_call_target="tpu_custom_call" | custom-call | flops 2147483648 | bytes 4194304 | tf_op jit(solution)/shard_map/attend/pallas_call | solution.py:93
  127.3 5.2 convert_reduce_fusion.6
  133.0 4.6 all-to-all-start.1
  137.6 10.0 %all-gather.8.cloned.1.call-start = ((), (), s32[]{:S(2)}) async-start(), calls=%async_computation.9 | async-start | bytes 5242880 | tf_op jit(solution)/shard_map/all_gather | solution.py:177
  148.5 2.5 fusion.45
  151.0 2.4 fusion.35
  154.8 8.5 %fusion.13 = (bf16[1024,2048]{1,0:T(8,128)(2,1)}, bf16[1024,2048]{1,0:T(8,128)(2,1)}) fusion(f32[2048]{0:T(1024)S(1)} %bitcast.143, bf16[1024,1024]{1,0:T(8,128)(2,1)S(1)} %fusion.35, bf16[2048,1024]{0,1:T(8,128)(2,1)S(1)} %copy-done.28), kind=kOutput, calls=%fused_computation.25 | convolution fusion | flops 4320133120 | bytes 14688256 | tf_op jit(solution)/shard_map/dot_general | solution.py:32
  163.3 1.4 all-to-all-done.1
  164.6 1.9 copy.40
  167.4 7.0 %add_convert_fusion = bf16[1024,2048]{1,0:T(8,128)(2,1)S(1)} fusion(f32[2048]{0:T(1024)S(1)} %bitcast.144, bf16[1024,1024]{1,0:T(8,128)(2,1)S(1)} %copy-done.15, bf16[2048,1024]{0,1:T(8,128)(2,1)} %collective-permute-done.1), kind=kOutput, calls=%fused_computation.37 | convolution fusion | flops 4299161600 | bytes 10493952 | tf_op jit(solution)/shard_map/dot_general | solution.py:32
  174.3 8.0 %fusion.60 = f32[2048,1024]{1,0:T(8,128)} fusion(bf16[1024,1024]{1,0:T(8,128)(2,1)S(1)} %bitcast.107, bf16[1024,2048]{1,0:T(8,128)(2,1)S(1)} %add_convert_fusion), kind=kOutput, calls=%fused_computation.136 | convolution fusion | flops 4315938816 | bytes 14680064 | tf_op jit(solution)/shard_map/dot_general | solution.py:32
  182.5 13.4 %collective-permute-done.2 = f32[2048,1024]{1,0:T(8,128)} collective-permute-done((f32[2048,1024]{1,0:T(8,128)}, f32[2048,1024]{1,0:T(8,128)}, u32[]{:S(2)}, u32[]{:S(2)}) %collective-permute-start.2) | collective-permute-done | bytes 8388640 | tf_op jit(solution)/shard_map/ppermute | solution.py:183
  195.9 13.2 %convolution_add_fusion.2 = f32[2048,1024]{1,0:T(8,128)} fusion(f32[2048,1024]{1,0:T(8,128)} %collective-permute-done.2, bf16[1024,2048]{1,0:T(8,128)(2,1)} %get-tuple-element.110, bf16[1024,1024]{1,0:T(8,128)(2,1)} %bitcast.108), kind=kOutput, calls=%fused_computation.95 | convolution fusion | flops 4297064448 | bytes 23068672 | tf_op jit(solution)/shard_map/dot_general | solution.py:32
  209.0 18.3 %all-gather.8.cloned.1.call-done = bf16[2048,1024]{1,0:T(8,128)(2,1)} async-done(((bf16[512,1024]{1,0:T(8,128)(2,1)}), bf16[2048,1024]{1,0:T(8,128)(2,1)}) %all-gather.8.cloned.1.call-update) | async-done | bytes 4194320 | tf_op jit(solution)/shard_map/all_gather | solution.py:177
  227.7 13.3 %convert_reduce_fusion.1 = (f32[2048]{0:T(1024)}, bf16[1024,2048]{1,0:T(8,128)(2,1)S(1)}) fusion(bf16[1024,2048]{1,0:T(8,128)(2,1)} %get-tuple-element.111, bf16[1024,1024]{1,0:T(8,128)(2,1)} %bitcast.109, bf16[2048,1024]{1,0:T(8,128)(2,1)} %all-gather.8.cloned.1.call-done), kind=kOutput, calls=%fused_computation.36 | convolution fusion | flops 4347394048 | bytes 14688256 | tf_op jit(solution)/shard_map/dot_general | solution.py:32
  241.0 13.2 %convert_reduce_fusion = (f32[2048]{0:T(1024)S(1)}, bf16[1024,2048]{1,0:T(8,128)(2,1)S(1)}) fusion(bf16[1024,2048]{1,0:T(8,128)(2,1)S(1)} %copy-done.36, bf16[1024,1024]{1,0:T(8,128)(2,1)S(1)} %bitcast.110, bf16[2048,1024]{1,0:T(8,128)(2,1)} %collective-permute-done.3), kind=kOutput, calls=%fused_computation.35 | convolution fusion | flops 4347394048 | bytes 14688256 | tf_op jit(solution)/shard_map/dot_general | solution.py:32
  254.2 1.9 copy-done.34
  256.2 4.7 fusion.75
  261.4 12.8 %collective-permute-done.4 = f32[2048,1024]{1,0:T(8,128)S(1)} collective-permute-done((f32[2048,1024]{1,0:T(8,128)S(1)}, f32[2048,1024]{1,0:T(8,128)S(1)}, u32[]{:S(2)}, u32[]{:S(2)}) %collective-permute-start.4) | collective-permute-done | bytes 8388640 | tf_op jit(solution)/shard_map/ppermute | solution.py:183
  274.2 7.1 %convolution_add_fusion.1 = f32[2048,1024]{1,0:T(8,128)} fusion(f32[2048,1024]{1,0:T(8,128)S(1)} %collective-permute-done.4, bf16[1024,2048]{1,0:T(8,128)(2,1)S(1)} %get-tuple-element.94, bf16[1024,1024]{1,0:T(8,128)(2,1)S(1)} %copy-done.16), kind=kOutput, calls=%fused_computation.94 | convolution fusion | flops 4297064448 | bytes 23068672 | tf_op jit(solution)/shard_map/dot_general | solution.py:32
  281.4 7.9 %fusion.77 = f32[1024,1024]{1,0:T(8,128)S(1)} fusion(bf16[1024,2048]{1,0:T(8,128)(2,1)} %copy-done.34, bf16[2048,1024]{0,1:T(8,128)(2,1)} %collective-permute-done.1), kind=kOutput, calls=%fused_computation.144 | convolution fusion | flops 4294967296 | bytes 12582912 | tf_op jit(solution)/shard_map/dot_general | solution.py:32
  289.4 5.4 %convert_reduce_fusion.5 = (f32[1024]{0:T(1024)S(1)}, f32[1024]{0:T(1024)S(1)}, bf16[1024,1024]{1,0:T(8,128)(2,1)S(1)}) fusion(f32[1024]{0:T(1024)S(1)} %copy-done.22, f32[1024]{0:T(1024)S(1)} %broadcast_multiply_fusion, bf16[1024,1024]{1,0:T(8,128)(2,1)S(1)} %copy-done, f32[1024,1024]{1,0:T(8,128)S(1)} %fusion.77, bf16[1024,2048]{1,0:T(8,128)(2,1)S(1)} %copy-done.33, ...), kind=kOutput, calls=%fused_computation.46 | convolution fusion | flops 4304402432 | bytes 16793600 | tf_op jit(solution)/shard_map/dot_general | solution.py:32
  294.8 2.7 fusion.50
  297.5 2.3 convert_reduce_fusion.8
  301.7 2.3 convolution_convert_fusion.1.da_ref
  304.0 1.5 collective-permute-done.5
  305.5 2.6 convolution_add_fusion.3
  308.1 17.5 %attend_back.3 = bf16[1024,1536]{1,0:T(8,128)(2,1)} custom-call(bf16[1024,1536]{1,0:T(8,128)(2,1)} %add_convert_fusion.2.qkv_ref, bf16[1024,512]{1,0:T(8,128)(2,1)} %convolution_convert_fusion.1.da_ref), custom_call_target="tpu_custom_call" | custom-call | flops 4294967296 | bytes 7340032 | tf_op jit(solution)/shard_map/attend_back/pallas_call | solution.py:110
  325.6 7.7 %fusion.65 = f32[1536,1024]{1,0:T(8,128)} fusion(bf16[1024,1536]{1,0:T(8,128)(2,1)} %attend_back.3, bf16[1024,1024]{1,0:T(8,128)(2,1)S(1)} %bitcast.101, f32[1024]{0:T(1024)S(1)} %copy-done.30, f32[1024]{0:T(1024)S(1)} %copy-done.24, f32[1024]{0:T(1024)S(1)} %fusion.56, f32[1024]{0:T(1024)S(1)} %broadcast_multiply_fusion.1), kind=kOutput, calls=%fused_computation.137 | convolution fusion | flops 3227516928 | bytes 11550720 | tf_op jit(solution)/shard_map/dot_general | solution.py:32
  333.7 2.3 convolution_convert_fusion.2.da_ref
  335.9 17.3 %attend_back.2 = bf16[1024,1536]{1,0:T(8,128)(2,1)} custom-call(bf16[1024,1536]{1,0:T(8,128)(2,1)} %add_convert_fusion.3.qkv_ref, bf16[1024,512]{1,0:T(8,128)(2,1)} %convolution_convert_fusion.2.da_ref), custom_call_target="tpu_custom_call" | custom-call | flops 4294967296 | bytes 7340032 | tf_op jit(solution)/shard_map/attend_back/pallas_call | solution.py:110
  353.2 8.3 %convolution_add_fusion = f32[1536,1024]{1,0:T(8,128)S(1)} fusion(f32[1536,1024]{1,0:T(8,128)} %collective-permute-done.6, bf16[1024,1536]{1,0:T(8,128)(2,1)} %attend_back.2, bf16[1024,1024]{1,0:T(8,128)(2,1)S(1)} %bitcast.102, f32[1024]{0:T(1024)S(1)} %copy-done.30, f32[1024]{0:T(1024)S(1)} %copy-done.24, f32[1024]{0:T(1024)S(1)} %fusion.56, ...), kind=kOutput, calls=%fused_computation.73 | convolution fusion | flops 3229089792 | bytes 17842176 | tf_op jit(solution)/shard_map/dot_general | solution.py:32
  361.5 6.2 %pad_maximum_fusion = f32[4,512,1024]{2,1,0:T(8,128)} fusion(f32[4,128,1024]{2,1,0:T(8,128)} %bitcast.129, f32[4,384,1024]{2,1,0:T(8,128)S(1)} %bitcast.115), kind=kLoop, calls=%fused_computation.34 | loop fusion | flops 2097152 | bytes 16777216 | tf_op jit(solution)/shard_map/concatenate | solution.py:280
  368.4 7.7 %fusion.76 = f32[1024,1024]{1,0:T(8,128)S(1)} fusion(bf16[1024,2048]{1,0:T(8,128)(2,1)} %get-tuple-element.110, bf16[2048,1024]{1,0:T(8,128)(2,1)} %all-gather.8.cloned.1.call-done), kind=kOutput, calls=%fused_computation.143 | convolution fusion | flops 4294967296 | bytes 12582912 | tf_op jit(solution)/shard_map/dot_general | solution.py:32
  376.1 8.0 %fusion.49 = bf16[1024,1024]{1,0:T(8,128)(2,1)S(1)} fusion(f32[1024,1024]{1,0:T(8,128)S(1)} %fusion.76, bf16[1024,1024]{1,0:T(8,128)(2,1)S(1)} %copy-done.1, f32[1024]{0:T(1024)S(1)} %convert_element_type.211, bf16[2048,1024]{1,0:T(8,128)(2,1)} %collective-permute-done.3, bf16[1024,2048]{1,0:T(8,128)(2,1)S(1)} %copy-done.37), kind=kOutput, calls=%fused_computation.89 | convolution fusion | flops 4321181696 | bytes 16781312 | tf_op jit(solution)/shard_map/dot_general | solution.py:32
  384.1 2.9 copy.41
  387.0 4.7 all-to-all-start.2
  391.8 49.9 %all-to-all-done.2 = bf16[4,256,1024]{2,0,1:T(4,128)(2,1)} async-done(((bf16[4,256,1024]{2,0,1:T(4,128)(2,1)}), bf16[4,256,1024]{2,0,1:T(4,128)(2,1)}, u32[]{:S(2)}, u32[]{:S(2)}) %all-to-all-start.2) | async-done | bytes 2097184 | tf_op jit(solution)/shard_map/all_to_all | solution.py:201
  441.7 3.8 copy.42
  445.5 5.7 %fusion.79 = f32[1024,1024]{1,0:T(8,128)S(1)} fusion(bf16[1024,1536]{1,0:T(8,128)(2,1)} %attend_back.2, bf16[1536,1024]{1,0:T(8,128)(2,1)S(1)} %bitcast.121), kind=kOutput, calls=%fused_computation.146 | convolution fusion | flops 3221225472 | bytes 10485760 | tf_op jit(solution)/shard_map/dot_general | solution.py:32
  451.2 4.2 convert_reduce_fusion.4
  455.4 2.7 fusion.51
  458.2 2.0 fusion.39
  460.2 2.9 copy.43
  463.1 3.8 all-to-all-start.3
  467.0 2.5 convert_reduce_fusion.3
  471.0 41.1 %sum_over_tp.1 = f32[13,1024]{1,0:T(8,128)} custom-call(f32[13,1024]{1,0:T(8,128)} %reshape.261.vec_ref), custom_call_target="tpu_custom_call" | custom-call | tf_op jit(solution)/shard_map/sum_over_tp/pallas_call | solution.py:146
  516.4 1.5 fusion.72
  517.9 2.0 copy.44
  519.9 2.7 convert_element_type.234
  522.7 1.7 convert_bitcast_fusion
  524.4 1.3 copy.45
  525.7 1.7 convert.14
  (148 shorter events, 21.2 us)
Async XLA Ops:
  7.2 71.9 %all-gather.4.cloned.1.call-start = ((), (), s32[]{:S(2)}) async-start(), calls=%async_computation.7 | async-start | bytes 5406720 | tf_op jit(solution)/shard_map/all_gather | solution.py:177
  9.4 69.6 %copy-start.26 = (bf16[1024]{0:T(1024)(128)(2,1)S(1)}, bf16[1024]{0:T(1024)(128)(2,1)}, u32[]{:S(2)}) copy-start(bf16[1024]{0:T(1024)(128)(2,1)} %param.27) | copy-start | bytes 6148
  11.8 67.3 %all-to-all-start = ((bf16[8,4,32,1024]{3,2,1,0:T(8,128)(2,1)}), bf16[8,4,32,1024]{3,2,1,0:T(8,128)(2,1)S(1)}, u32[]{:S(2)}, u32[]{:S(2)}) async-start(bf16[8,4,32,1024]{3,2,1,0:T(8,128)(2,1)} %bitcast.124), calls=%async_computation | async-start | bytes 4194304 | tf_op jit(solution)/shard_map/all_to_all | solution.py:195
  17.1 115.5 %all-gather.6.cloned.1.call-start = ((), (), s32[]{:S(2)}) async-start(), calls=%async_computation.8 | async-start | bytes 5242880 | tf_op jit(solution)/shard_map/all_gather | solution.py:177
  79.1 27.0 %collective-permute-start = (bf16[2112,1024]{1,0:T(8,128)(2,1)}, bf16[2112,1024]{1,0:T(8,128)(2,1)}, u32[]{:S(2)}, u32[]{:S(2)}) collective-permute-start(bf16[2112,1024]{1,0:T(8,128)(2,1)} %all-gather.4.cloned.1.call-done), channel_id=1, source_target_pairs={{0,1},{1,0},{2,3},{3,2},{4,5},{5,4},{6,7},{7,6},{8,9},{9,8},{10,11... | collective-permute-start | bytes 12976136 | tf_op jit(solution)/shard_map/ppermute | solution.py:183
  79.1 1.3 copy-start.8
  80.4 3.7 copy-start.9
  83.5 0.6 copy-start.20
  84.1 2.1 copy-start.24
  84.1 2.1 copy-start.30
  84.2 17.5 %copy-start.18 = (bf16[4,128,1024]{2,1,0:T(8,128)(2,1)}, bf16[4,128,1024]{2,1,0:T(8,128)(2,1)S(1)}, u32[]{:S(2)}) copy-start(bf16[4,128,1024]{2,1,0:T(8,128)(2,1)S(1)} %slice.135) | copy-start | bytes 3145732
  132.5 18.5 %copy-start.22 = (f32[1024]{0:T(1024)S(1)}, f32[1024]{0:T(1024)}, u32[]{:S(2)}) copy-start(f32[1024]{0:T(1024)} %param.28) | copy-start | bytes 12292
  132.5 18.5 %copy-start.25 = (f32[1024]{0:T(1024)S(1)}, f32[1024]{0:T(1024)}, u32[]{:S(2)}) copy-start(f32[1024]{0:T(1024)} %param.29) | copy-start | bytes 12292
  132.5 34.8 %collective-permute-start.1 = (bf16[2048,1024]{0,1:T(8,128)(2,1)}, bf16[2048,1024]{0,1:T(8,128)(2,1)}, u32[]{:S(2)}, u32[]{:S(2)}) collective-permute-start(bf16[2048,1024]{0,1:T(8,128)(2,1)} %all-gather.6.cloned.1.call-done), channel_id=1, source_target_pairs={{0,1},{1,0},{2,3},{3,2},{4,5},{5,4},{6,7},{7,6},{8,9},{9,8},{10,11... | collective-permute-start | bytes 12582920 | tf_op jit(solution)/shard_map/ppermute | solution.py:183
  133.0 31.6 %all-to-all-start.1 = ((bf16[8,4,32,1024]{3,2,1,0:T(8,128)(2,1)}), bf16[8,4,32,1024]{3,2,1,0:T(8,128)(2,1)}, u32[]{:S(2)}, u32[]{:S(2)}) async-start(bf16[8,4,32,1024]{3,2,1,0:T(8,128)(2,1)} %bitcast.125), calls=%async_computation.1 | async-start | bytes 4194304 | tf_op jit(solution)/shard_map/all_to_all | solution.py:195
  137.6 89.7 %all-gather.8.cloned.1.call-start = ((), (), s32[]{:S(2)}) async-start(), calls=%async_computation.9 | async-start | bytes 5242880 | tf_op jit(solution)/shard_map/all_gather | solution.py:177
  147.5 7.2 %copy-start.28 = (bf16[2048,1024]{0,1:T(8,128)(2,1)S(1)}, bf16[2048,1024]{0,1:T(8,128)(2,1)}, u32[]{:S(2)}) copy-start(bf16[2048,1024]{0,1:T(8,128)(2,1)} %all-gather.6.cloned.1.call-done) | copy-start | bytes 12582916
  153.4 1.3 copy-start.14
  164.6 2.7 copy-start.15
  166.5 7.8 %copy-start.5 = (bf16[4,8,32,1024]{3,2,1,0:T(8,128)(2,1)}, bf16[4,8,32,1024]{3,2,1,0:T(8,128)(2,1)S(1)}, u32[]{:S(2)}) copy-start(bf16[4,8,32,1024]{3,2,1,0:T(8,128)(2,1)S(1)} %copy.40) | copy-start | bytes 6291460
  174.3 8.0 %copy-start.35 = (bf16[1024,2048]{1,0:T(8,128)(2,1)}, bf16[1024,2048]{1,0:T(8,128)(2,1)S(1)}, u32[]{:S(2)}) copy-start(bf16[1024,2048]{1,0:T(8,128)(2,1)S(1)} %add_convert_fusion) | copy-start | bytes 12582916
  182.4 13.5 %collective-permute-start.2 = (f32[2048,1024]{1,0:T(8,128)}, f32[2048,1024]{1,0:T(8,128)}, u32[]{:S(2)}, u32[]{:S(2)}) collective-permute-start(f32[2048,1024]{1,0:T(8,128)} %fusion.60), channel_id=1, source_target_pairs={{0,1},{1,0},{2,3},{3,2},{4,5},{5,4},{6,7},{7,6},{8,9},{9,8},{10,11... | collective-permute-start | bytes 25165832 | tf_op jit(solution)/shard_map/ppermute | solution.py:183
  182.4 337.5 %reduce-scatter.8.cloned.1.call-start = ((), (), s32[]{:S(2)}) async-start(), calls=%async_computation.12 | async-start | bytes 10485760 | tf_op jit(solution)/shard_map/reduce_scatter | solution.py:180
  227.3 13.7 %collective-permute-start.3 = (bf16[2048,1024]{1,0:T(8,128)(2,1)}, bf16[2048,1024]{1,0:T(8,128)(2,1)}, u32[]{:S(2)}, u32[]{:S(2)}) collective-permute-start(bf16[2048,1024]{1,0:T(8,128)(2,1)} %all-gather.8.cloned.1.call-done), channel_id=1, source_target_pairs={{0,1},{1,0},{2,3},{3,2},{4,5},{5,4},{6,7},{7,6},{8,9},{9,8},{10,11... | collective-permute-start | bytes 12582920 | tf_op jit(solution)/shard_map/ppermute | solution.py:183
  227.4 295.3 %reduce-scatter.6.cloned.1.call-start = ((), (), s32[]{:S(2)}) async-start(), calls=%async_computation.11 | async-start | bytes 10485760 | tf_op jit(solution)/shard_map/reduce_scatter | solution.py:180
  227.7 13.3 %copy-start.6 = (bf16[4,8,32,1024]{3,2,1,0:T(8,128)(2,1)S(1)}, bf16[4,8,32,1024]{3,2,1,0:T(8,128)(2,1)}, u32[]{:S(2)}) copy-start(bf16[4,8,32,1024]{3,2,1,0:T(8,128)(2,1)} %copy-done.5) | copy-start | bytes 6291460
  227.7 13.3 %copy-start.36 = (bf16[1024,2048]{1,0:T(8,128)(2,1)S(1)}, bf16[1024,2048]{1,0:T(8,128)(2,1)}, u32[]{:S(2)}) copy-start(bf16[1024,2048]{1,0:T(8,128)(2,1)} %copy-done.35) | copy-start | bytes 12582916
  241.0 33.2 %copy-start.32 = (bf16[1024,2048]{1,0:T(8,128)(2,1)}, bf16[1024,2048]{1,0:T(8,128)(2,1)S(1)}, u32[]{:S(2)}) copy-start(bf16[1024,2048]{1,0:T(8,128)(2,1)S(1)} %get-tuple-element.94) | copy-start | bytes 12582916
  241.0 15.2 %copy-start.16 = (bf16[1024,1024]{1,0:T(8,128)(2,1)S(1)}, bf16[1024,1024]{1,0:T(8,128)(2,1)}, u32[]{:S(2)}) copy-start(bf16[1024,1024]{1,0:T(8,128)(2,1)} %copy-done.14) | copy-start | bytes 6291460
  254.2 1.9 copy-start.34
  260.8 13.4 %collective-permute-start.4 = (f32[2048,1024]{1,0:T(8,128)S(1)}, f32[2048,1024]{1,0:T(8,128)S(1)}, u32[]{:S(2)}, u32[]{:S(2)}) collective-permute-start(f32[2048,1024]{1,0:T(8,128)S(1)} %fusion.75), channel_id=1, source_target_pairs={{0,1},{1,0},{2,3},{3,2},{4,5},{5,4},{6,7},{7,6},{8,9},{9,8},{10,11... | collective-permute-start | bytes 25165832 | tf_op jit(solution)/shard_map/ppermute | solution.py:183
  281.3 244.4 %reduce-scatter.4.cloned.1.call-start = ((), (), s32[]{:S(2)}) async-start(), calls=%async_computation.10 | async-start | bytes 10485760 | tf_op jit(solution)/shard_map/reduce_scatter | solution.py:180
  281.4 8.0 %copy-start = (bf16[1024,1024]{1,0:T(8,128)(2,1)S(1)}, bf16[1024,1024]{1,0:T(8,128)(2,1)}, u32[]{:S(2)}) copy-start(bf16[1024,1024]{1,0:T(8,128)(2,1)} %get-tuple-element.109) | copy-start | bytes 6291460
  281.4 8.0 %copy-start.29 = (bf16[2048,1024]{0,1:T(8,128)(2,1)S(1)}, bf16[2048,1024]{0,1:T(8,128)(2,1)}, u32[]{:S(2)}) copy-start(bf16[2048,1024]{0,1:T(8,128)(2,1)} %all-gather.6.cloned.1.call-done) | copy-start | bytes 12582916
  281.4 8.0 %copy-start.33 = (bf16[1024,2048]{1,0:T(8,128)(2,1)S(1)}, bf16[1024,2048]{1,0:T(8,128)(2,1)}, u32[]{:S(2)}) copy-start(bf16[1024,2048]{1,0:T(8,128)(2,1)} %copy-done.32) | copy-start | bytes 12582916
  294.8 2.7 copy-start.7
  297.5 2.4 copy-start.17
  299.9 5.6 %copy-start.2 = (bf16[1024,1024]{1,0:T(8,128)(2,1)}, bf16[1024,1024]{1,0:T(8,128)(2,1)S(1)}, u32[]{:S(2)}) copy-start(bf16[1024,1024]{1,0:T(8,128)(2,1)S(1)} %get-tuple-element.96) | copy-start | bytes 6291460
  301.2 4.3 copy-start.31
  301.2 4.3 collective-permute-start.5
  325.6 8.1 %copy-start.3 = (bf16[1024,1024]{1,0:T(8,128)(2,1)S(1)}, bf16[1024,1024]{1,0:T(8,128)(2,1)}, u32[]{:S(2)}) copy-start(bf16[1024,1024]{1,0:T(8,128)(2,1)} %copy-done.2) | copy-start | bytes 6291460
  325.6 8.1 %copy-start.19 = (bf16[4,128,1024]{2,1,0:T(8,128)(2,1)S(1)}, bf16[4,128,1024]{2,1,0:T(8,128)(2,1)}, u32[]{:S(2)}) copy-start(bf16[4,128,1024]{2,1,0:T(8,128)(2,1)} %copy-done.18) | copy-start | bytes 3145732
  333.3 19.9 %collective-permute-start.6 = (f32[1536,1024]{1,0:T(8,128)}, f32[1536,1024]{1,0:T(8,128)}, u32[]{:S(2)}, u32[]{:S(2)}) collective-permute-start(f32[1536,1024]{1,0:T(8,128)} %fusion.65), channel_id=1, source_target_pairs={{0,1},{1,0},{2,3},{3,2},{4,5},{5,4},{6,7},{7,6},{8,9},{9,8},{10,11... | collective-permute-start | bytes 18874376 | tf_op jit(solution)/shard_map/ppermute | solution.py:183
  367.7 0.7 copy-start.27
  368.4 7.7 %copy-start.1 = (bf16[1024,1024]{1,0:T(8,128)(2,1)S(1)}, bf16[1024,1024]{1,0:T(8,128)(2,1)}, u32[]{:S(2)}) copy-start(bf16[1024,1024]{1,0:T(8,128)(2,1)} %get-tuple-element.109) | copy-start | bytes 6291460
  368.4 7.7 %copy-start.37 = (bf16[1024,2048]{1,0:T(8,128)(2,1)S(1)}, bf16[1024,2048]{1,0:T(8,128)(2,1)}, u32[]{:S(2)}) copy-start(bf16[1024,2048]{1,0:T(8,128)(2,1)} %copy-done.35) | copy-start | bytes 12582916
  387.0 54.7 %all-to-all-start.2 = ((bf16[4,256,1024]{2,0,1:T(4,128)(2,1)}), bf16[4,256,1024]{2,0,1:T(4,128)(2,1)}, u32[]{:S(2)}, u32[]{:S(2)}) async-start(bf16[4,256,1024]{2,0,1:T(4,128)(2,1)} %copy.41), calls=%async_computation.2 | async-start | bytes 4194304 | tf_op jit(solution)/shard_map/all_to_all | solution.py:201
  441.7 3.8 copy-start.10
  445.5 5.7 %copy-start.11 = (bf16[4,384,1024]{2,1,0:T(8,128)(2,1)S(1)}, bf16[4,384,1024]{2,1,0:T(8,128)(2,1)}, u32[]{:S(2)}) copy-start(bf16[4,384,1024]{2,1,0:T(8,128)(2,1)} %slice.136) | copy-start | bytes 9437188
  445.5 5.7 %copy-start.12 = (bf16[1024,1536]{1,0:T(8,128)(2,1)S(1)}, bf16[1024,1536]{1,0:T(8,128)(2,1)}, u32[]{:S(2)}) copy-start(bf16[1024,1536]{1,0:T(8,128)(2,1)} %attend_back.3) | copy-start | bytes 9437188
  451.2 4.2 copy-start.21
  455.4 2.8 copy-start.4
  463.1 54.8 %all-to-all-start.3 = ((bf16[4,256,1024]{2,0,1:T(4,128)(2,1)}), bf16[4,256,1024]{2,0,1:T(4,128)(2,1)S(1)}, u32[]{:S(2)}, u32[]{:S(2)}) async-start(bf16[4,256,1024]{2,0,1:T(4,128)(2,1)} %copy.43), calls=%async_computation.3 | async-start | bytes 4194304 | tf_op jit(solution)/shard_map/all_to_all | solution.py:201
  466.9 2.9 copy-start.13
  466.9 3.4 copy-start.23
Sparse Core Ops, SparseCore 0:
  11.9 67.1 all-gather.3
  80.6 44.4 all-gather.5
  182.5 44.7 all-gather.7
  229.5 76.7 reduce-scatter.7
  308.5 76.1 reduce-scatter.5
  386.9 122.9 reduce-scatter.3

commit v5 on v4

--- a/solution.py
+++ b/solution.py
@@ -179,6 +179,9 @@
     def scatter_rows(rows):
         return lax.psum_scatter(rows, 'tp', scatter_dimension=0, tiled=True, axis_index_groups=rings)
 
+    def shift(t, chip_steps):
+        return lax.ppermute(t, 'tp', [(i, (i + 2 * chip_steps) % tp) for i in range(tp)])
+
     def swap(t):
         return lax.ppermute(t, 'tp', pairs)
 
@@ -221,8 +224,10 @@
         qkv_rows = place([(t, i * cols) for i, t in enumerate(pieces)]
                          + [(jnp.broadcast_to(bias_row[None], (PAD, width)), my_rows)], my_rows + PAD)
         packed = both(gather_rows(qkv_rows))
+        me = lax.axis_index('tp')
+        core, chip = lax.rem(me, 2), me // 2
         x_img = lax.optimization_barrier(join_tokens(to_images(x)))
-        w1_mine, w2_mine = gather_rows(w_1.T), gather_rows(w_2)
+        w1_mine = gather_rows(w_1.T)
 
         w_qkv, wo, b_qkv, b_1_all = [], [], [], []
         for half in packed:
@@ -235,23 +240,39 @@
         x_f32 = x_img.astype(F32)
         h_one_f, ln1_pull = jax.vjp(layer_norm, x_f32, ln1_gain, ln1_bias)
         h_one = h_one_f.astype(BF16)
-        qkv = [(dot(h_one, w, 1, 1) + b).astype(BF16) for w, b in zip(w_qkv, b_qkv)]
-        d_moved = to_images(after((d_out,), qkv[0])[0])
-        mixed = [attend(t, images, my_heads, head_dim) for t in qkv]
+        qkv_mine = (dot(h_one, w_qkv[0], 1, 1) + b_qkv[0]).astype(BF16)
+        mixed_mine = attend(qkv_mine, images, my_heads, head_dim)
+        d_moved = to_images(after((d_out,), mixed_mine)[0])
+        qkv_theirs = (dot(h_one, w_qkv[1], 1, 1) + b_qkv[1]).astype(BF16)
+        mixed_theirs = attend(qkv_theirs, images, my_heads, head_dim)
+        qkv, mixed = [qkv_mine, qkv_theirs], [mixed_mine, mixed_theirs]
+        (w_2_late,) = after((w_2,), mixed_theirs)
+        steps = sorted(range(1, chips), key=lambda k: min(k, chips - k))
+        w2_pieces = [shift(w_2_late, k) for k in steps]
         x_mid = (x_f32 + dot(mixed[0], wo[0], 1, 0) + dot(mixed[1], wo[1], 1, 0) + b_o.astype(F32)).astype(BF16)
         w1 = both(w1_mine, x_mid)
         mid_f32 = x_mid.astype(F32)
         h_two_f, ln2_pull = jax.vjp(layer_norm, mid_f32, ln2_gain, ln2_bias)
         h_two = h_two_f.astype(BF16)
-        pre_act = [(dot(h_two, w, 1, 1) + b).astype(BF16) for w, b in zip(w1, b_1_all)]
-        gelus = [jax.vjp(gelu_tanh, t.astype(F32)) for t in pre_act]
-        hidden = [g[0].astype(BF16) for g in gelus]
-
-        d_out_img = lax.optimization_barrier(join_tokens(after((d_moved,), hidden[0])[0]))
-        theirs_2 = dot(hidden[1], d_out_img, 0, 0)
+
+        def mlp_up(rows, half):
+            pre_act = (dot(rows, w1[half], 1, 1) + b_1_all[half]).astype(BF16)
+            return jax.vjp(gelu_tanh, pre_act.astype(F32))
+
+        gelu_theirs = mlp_up(h_two, 1)
+        hidden_theirs = gelu_theirs[0].astype(BF16)
+        d_out_img = lax.optimization_barrier(join_tokens(after((d_moved,), hidden_theirs)[0]))
+        theirs_2 = dot(hidden_theirs, d_out_img, 0, 0)
+        gelus = [mlp_up(after((h_two,), theirs_2)[0], 0), gelu_theirs]
+        hidden = [gelus[0][0].astype(BF16), hidden_theirs]
         sum_2 = dot(hidden[0], d_out_img, 0, 0) + swap(theirs_2)
         grad_w_2 = scatter_rows(sum_2).astype(BF16)
-        w2 = both(w2_mine, sum_2)
+        (d_out_late,) = after((d_out_img,), sum_2)
+        d_out_sum = lax.optimization_barrier(token_sum(d_out_late))
+        w2_mine = jnp.zeros((chips * hid, width), BF16)
+        for k, piece in zip([0, *steps], after((w_2_late, *w2_pieces), sum_2)):
+            w2_mine = lax.dynamic_update_slice(w2_mine, piece, (lax.rem(chip + chips - k, chips) * hid, 0))
+        w2 = both(w2_mine)
         d_first = dot(d_out_img, after(w2[:1], sum_2)[0], 1, 1).astype(BF16)
         d_hidden = [d_first, dot(d_out_img, after(w2[1:], d_first)[0], 1, 1).astype(BF16)]
         d_pre = [g[1](d.astype(F32))[0].astype(BF16) for g, d in zip(gelus, d_hidden)]
@@ -265,6 +286,7 @@
         w2_late = after(w2, sum_1)
         y_img = (mid_f32 + dot(hidden[0], w2_late[0], 1, 0) + dot(hidden[1], w2_late[1], 1, 0) + b_2.astype(F32)).astype(BF16)
         y_out = to_tokens(y_img)
+        (d_h_two,) = after((d_h_two,), y_img)
         d_mid_ln, g_ln2_gain, g_ln2_bias = ln2_pull(d_h_two.astype(F32))
         d_mid = (d_out_img.astype(F32) + d_mid_ln).astype(BF16)
         mixed_late = after(mixed, sum_1)
@@ -277,23 +299,21 @@
         w_qkv_late = after(w_qkv, theirs_qkv)
         d_h_one = (dot(d_qkv[0], w_qkv_late[0], 1, 0) + dot(d_qkv[1], w_qkv_late[1], 1, 0)).astype(BF16)
         sum_qkv = dot(d_qkv[0], h_one, 0, 0) + swap(theirs_qkv)
+        d_in_ln, g_ln1_gain, g_ln1_bias = ln1_pull(d_h_one.astype(F32))
+        grad_x_img = (d_mid.astype(F32) + d_in_ln).astype(BF16)
+        grad_x = to_tokens(grad_x_img)
         sum_all = jnp.concatenate([sum_qkv.reshape(chips, qkv_cols, width), sum_o.reshape(chips, cols, width)], axis=1)
         g_all = scatter_rows(sum_all.reshape(chips * my_rows, width))
         grad_w_o = g_all[qkv_cols:].astype(BF16).reshape(my_heads, head_dim, width)
         g_qkv = g_all[:qkv_cols].reshape(3, cols, width)
         grad_w_q, grad_w_k, grad_w_v = (g_qkv[i].T.astype(BF16).reshape(width, my_heads, head_dim) for i in range(3))
-        d_in_ln, g_ln1_gain, g_ln1_bias = ln1_pull(d_h_one.astype(F32))
-        grad_x = to_tokens((d_mid.astype(F32) + d_in_ln).astype(BF16))
-
-        me = lax.axis_index('tp')
-        core, chip = lax.rem(me, 2), me // 2
 
         def halves(sums):
             first = jnp.where(core == 0, sums[0], sums[1])
             second = jnp.where(core == 0, sums[1], sums[0])
             return [first, second]
 
-        vecs = jnp.concatenate([g_ln1_gain, g_ln1_bias, token_sum(d_mid), g_ln2_gain, g_ln2_bias, token_sum(d_out_img)]
+        vecs = jnp.concatenate([g_ln1_gain, g_ln1_bias, token_sum(d_mid), g_ln2_gain, g_ln2_bias, d_out_sum]
                                + halves([token_sum(t) for t in d_qkv]) + halves(d_pre_sums))
         sums = sum_over_tp(vecs.reshape(-1, width), tp).reshape(-1)
         six = [sums[i * width:(i + 1) * width] for i in range(6)]

time: 546 us -> 552 us (1.011)
  the two profiles are of different devices: /device:TPU:112 before, /device:TPU:113 now
where the time goes in v5:
time: 552 us; the launch traced here: 543 us
  matrix products  165 us (30%)
  waiting for transfers between devices  154 us (28%)
  Pallas kernels  94.9 us (17%)
  local copies, waits for them, and re-layouts  49.6 us (9%)
  other arithmetic  37.6 us (7%)
  starting transfers between devices  26.3 us (5%)
  between operations  15 us (3%)
    dot_general x24, matrix products, dot(): lax.dot_general(a, b, (((ca,), (cb,)), ((), ())), preferred_element_type=...  165 us
    all_gather x2, waiting for transfers between devices, gather_rows(): lax.all_gather(rows, 'tp', axis=0, tiled=True, axis_index_groups=rings)  60.7 us
    all_to_all x2, waiting for transfers between devices, to_tokens(): lax.all_to_all(t.reshape(images, patches, width), 'tp', 1, 0, tiled=True)  46.3 us
    pallas_call x1, Pallas kernels, sum_over_tp(): pl.pallas_call(functools.partial(sum_kernel, n), out_shape=jax.ShapeDtype...  43.6 us
    pallas_call x2, Pallas kernels, attend_back(): pl.pallas_call(functools.partial(attend_back_kernel, group, heads, head_d...  34.8 us
    ppermute x3, waiting for transfers between devices, shift(): lax.ppermute(t, 'tp', [(i, (i + 2 * chip_steps) % tp) for i in range(tp)])  26.1 us
    pallas_call x2, Pallas kernels, attend(): pl.pallas_call(functools.partial(attend_kernel, group, heads, head_dim),...  16.5 us
    all_to_all x2, waiting for transfers between devices, to_images(): lax.all_to_all(t.reshape(tp, images, patches // tp, width), 'tp', 0, 0, t...  11.7 us
  transfers between devices with their start and end apart: 19, of which 10 were waited for; matrix products, arithmetic and copies ran while one was open for 41% of the time, Pallas kernels for 17%

profile of v5, /device:TPU:113, one launch (start us, length us, event | category | flops | bytes accessed | tf_op | source)
XLA Modules:
  0.0 542.6 jit_solution(2936299654796916034)
XLA Ops:
  9.5 2.2 pad_maximum_fusion.1
  11.8 6.0 %all-to-all-start = ((bf16[8,4,32,1024]{3,2,1,0:T(8,128)(2,1)}), bf16[8,4,32,1024]{3,2,1,0:T(8,128)(2,1)S(1)}, u32[]{:S(2)}, u32[]{:S(2)}) async-start(bf16[8,4,32,1024]{3,2,1,0:T(8,128)(2,1)} %bitcast.125), calls=%async_computation | async-start | bytes 4194304 | tf_op jit(solution)/shard_map/all_to_all | solution.py:198
  18.6 60.7 %all-gather.3.cloned.1.call-done = bf16[2112,1024]{1,0:T(8,128)(2,1)} async-done(((bf16[528,1024]{1,0:T(8,128)(2,1)}), bf16[2112,1024]{1,0:T(8,128)(2,1)}) %all-gather.3.cloned.1.call-update) | async-done | bytes 4325392 | tf_op jit(solution)/shard_map/all_gather | solution.py:177
  81.1 2.0 copy.39
  84.8 2.0 slice.133
  86.9 7.3 %add_convert_fusion.3.qkv_ref = bf16[1024,1536]{1,0:T(8,128)(2,1)} fusion(bf16[1536,1024]{1,0:T(8,128)(2,1)} %bitcast.121, f32[1536]{0:T(1024)S(1)} %reshape.270, bf16[1024,1024]{1,0:T(8,128)(2,1)S(1)} %bitcast.98, f32[1024]{0:T(1024)S(1)} %copy-done.36, f32[1024]{0:T(1024)S(1)} %copy-done.31, f32[1024]{0:T(1024)S(1)} %fusion.55, ...), kind=kOutput, calls=%fused_computation.57 | convolution fusion | flops 3230662656 | bytes 8411136 | tf_op jit(solution)/shard_map/dot_general | solution.py:32
  94.2 8.2 %attend.2 = bf16[1024,512]{1,0:T(8,128)(2,1)} custom-call(bf16[1024,1536]{1,0:T(8,128)(2,1)} %add_convert_fusion.3.qkv_ref), custom_call_target="tpu_custom_call" | custom-call | flops 2147483648 | bytes 4194304 | tf_op jit(solution)/shard_map/attend/pallas_call | solution.py:93
  102.4 4.4 fusion.69
  108.2 4.3 slice.136
  113.3 7.0 %add_convert_fusion.2.qkv_ref = bf16[1024,1536]{1,0:T(8,128)(2,1)} fusion(bf16[1536,1024]{1,0:T(8,128)(2,1)} %bitcast.123, f32[1536]{0:T(1024)S(1)} %reshape.271, bf16[1024,1024]{1,0:T(8,128)(2,1)S(1)} %bitcast.99, f32[1024]{0:T(1024)S(1)} %copy-done.36, f32[1024]{0:T(1024)S(1)} %copy-done.31, f32[1024]{0:T(1024)S(1)} %fusion.55, ...), kind=kOutput, calls=%fused_computation.56 | convolution fusion | flops 3230662656 | bytes 8411136 | tf_op jit(solution)/shard_map/dot_general | solution.py:32
  120.3 8.2 %attend.3 = bf16[1024,512]{1,0:T(8,128)(2,1)} custom-call(bf16[1024,1536]{1,0:T(8,128)(2,1)} %add_convert_fusion.2.qkv_ref), custom_call_target="tpu_custom_call" | custom-call | flops 2147483648 | bytes 4194304 | tf_op jit(solution)/shard_map/attend/pallas_call | solution.py:93
  128.5 4.7 convert_reduce_fusion.6
  133.4 4.7 all-to-all-start.1
  142.0 10.8 %fusion.13 = (bf16[1024,2048]{1,0:T(8,128)(2,1)}, bf16[1024,2048]{1,0:T(8,128)(2,1)}) fusion(f32[2048]{0:T(1024)S(1)} %bitcast.145, bf16[1024,1024]{1,0:T(8,128)(2,1)S(1)} %fusion.35, bf16[2048,1024]{0,1:T(8,128)(2,1)} %collective-permute-done.1), kind=kOutput, calls=%fused_computation.25 | convolution fusion | flops 4320133120 | bytes 14688256 | tf_op jit(solution)/shard_map/dot_general | solution.py:32
  152.8 11.7 %all-to-all-done.1 = bf16[8,4,32,1024]{3,2,1,0:T(8,128)(2,1)} async-done(((bf16[8,4,32,1024]{3,2,1,0:T(8,128)(2,1)}), bf16[8,4,32,1024]{3,2,1,0:T(8,128)(2,1)}, u32[]{:S(2)}, u32[]{:S(2)}) %all-to-all-start.1) | async-done | bytes 2097184 | tf_op jit(solution)/shard_map/all_to_all | solution.py:198
  164.5 2.0 copy.40
  167.3 6.7 %fusion.70 = f32[2048,1024]{1,0:T(8,128)} fusion(bf16[1024,2048]{1,0:T(8,128)(2,1)S(1)} %copy-done.40, bf16[1024,1024]{1,0:T(8,128)(2,1)S(1)} %bitcast.107), kind=kOutput, calls=%fused_computation.144 | convolution fusion | flops 4294967296 | bytes 14680064 | tf_op jit(solution)/shard_map/dot_general | solution.py:32
  175.9 2.7 collective-permute-start.3
  178.6 7.5 %add_convert_fusion = bf16[1024,2048]{1,0:T(8,128)(2,1)S(1)} fusion(f32[2048]{0:T(1024)S(1)} %bitcast.144, bf16[1024,1024]{1,0:T(8,128)(2,1)} %copy-done.15, bf16[2048,1024]{0,1:T(8,128)(2,1)} %all-gather.5.cloned.1.call-done), kind=kOutput, calls=%fused_computation.37 | convolution fusion | flops 4299161600 | bytes 10493952 | tf_op jit(solution)/shard_map/dot_general | solution.py:32
  186.0 2.1 collective-permute-done.5
  188.1 10.7 %convolution_add_fusion.2 = f32[2048,1024]{1,0:T(8,128)} fusion(f32[2048,1024]{1,0:T(8,128)} %collective-permute-done.5, bf16[1024,1024]{1,0:T(8,128)(2,1)S(1)} %bitcast.110, bf16[1024,2048]{1,0:T(8,128)(2,1)S(1)} %add_convert_fusion), kind=kOutput, calls=%fused_computation.94 | convolution fusion | flops 4318035968 | bytes 23068672 | tf_op jit(solution)/shard_map/dot_general | solution.py:32
  198.9 3.3 collective-permute-done.4
  202.2 20.9 %collective-permute-done.3 = bf16[512,1024]{1,0:T(8,128)(2,1)} collective-permute-done((bf16[512,1024]{1,0:T(8,128)(2,1)S(1)}, bf16[512,1024]{1,0:T(8,128)(2,1)}, u32[]{:S(2)}, u32[]{:S(2)}) %collective-permute-start.3) | collective-permute-done | bytes 1048608 | tf_op jit(solution)/shard_map/ppermute | solution.py:183
  223.1 1.9 collective-permute-done.2
  225.0 2.6 broadcast_in_dim.13
  228.6 2.3 constant_dynamic-update-slice_fusion.8
  231.0 2.3 constant_dynamic-update-slice_fusion.7
  233.2 2.3 constant_dynamic-update-slice_fusion.6
  236.1 13.3 %convert_reduce_fusion.1 = (f32[2048]{0:T(1024)}, bf16[1024,2048]{1,0:T(8,128)(2,1)S(1)}) fusion(bf16[1024,2048]{1,0:T(8,128)(2,1)} %copy-done.42, bf16[1024,1024]{1,0:T(8,128)(2,1)} %bitcast.108, bf16[2048,1024]{1,0:T(8,128)(2,1)} %constant_dynamic-update-slice_fusion.6), kind=kOutput, calls=%fused_computation.36 | convolution fusion | flops 4347394048 | bytes 14688256 | tf_op jit(solution)/shard_map/dot_general | solution.py:32
  249.5 13.0 %convert_reduce_fusion = (f32[2048]{0:T(1024)S(1)}, bf16[1024,2048]{1,0:T(8,128)(2,1)S(1)}) fusion(bf16[1024,2048]{1,0:T(8,128)(2,1)S(1)} %copy-done.44, bf16[1024,1024]{1,0:T(8,128)(2,1)S(1)} %bitcast.111, bf16[2048,1024]{1,0:T(8,128)(2,1)} %collective-permute-done.6), kind=kOutput, calls=%fused_computation.35 | convolution fusion | flops 4347394048 | bytes 14688256 | tf_op jit(solution)/shard_map/dot_general | solution.py:32
  262.5 4.6 fusion.71
  267.2 8.3 %fusion.72 = f32[1024,1024]{1,0:T(8,128)} fusion(bf16[1024,2048]{1,0:T(8,128)(2,1)S(1)} %get-tuple-element.130, bf16[2048,1024]{0,1:T(8,128)(2,1)} %collective-permute-done.1), kind=kOutput, calls=%fused_computation.146 | convolution fusion | flops 4294967296 | bytes 12582912 | tf_op jit(solution)/shard_map/dot_general | solution.py:32
  275.5 4.8 collective-permute-done.7
  280.3 7.1 %convolution_add_fusion.1 = f32[2048,1024]{1,0:T(8,128)} fusion(f32[2048,1024]{1,0:T(8,128)S(1)} %collective-permute-done.7, bf16[1024,2048]{1,0:T(8,128)(2,1)S(1)} %get-tuple-element.110, bf16[1024,1024]{1,0:T(8,128)(2,1)S(1)} %copy-done.16), kind=kOutput, calls=%fused_computation.93 | convolution fusion | flops 4297064448 | bytes 23068672 | tf_op jit(solution)/shard_map/dot_general | solution.py:32
  287.8 9.4 %add_convert_fusion.6 = bf16[1024,1024]{1,0:T(8,128)(2,1)S(1)} fusion(f32[1024,1024]{1,0:T(8,128)} %fusion.72, bf16[1024,2048]{1,0:T(8,128)(2,1)} %copy-done.39, bf16[2048,1024]{0,1:T(8,128)(2,1)} %all-gather.5.cloned.1.call-done), kind=kOutput, calls=%fused_computation.92 | convolution fusion | flops 4297064448 | bytes 14680064 | tf_op jit(solution)/shard_map/dot_general | solution.py:32
  297.3 7.7 %fusion.57 = f32[1024,1024]{1,0:T(8,128)S(1)} fusion(bf16[2048,1024]{1,0:T(8,128)(2,1)} %constant_dynamic-update-slice_fusion.6, bf16[1024,2048]{1,0:T(8,128)(2,1)S(1)} %copy-done.43), kind=kOutput, calls=%fused_computation.138 | convolution fusion | flops 4315938816 | bytes 12582912 | tf_op jit(solution)/shard_map/dot_general | solution.py:32
  305.0 8.5 %fusion.48 = bf16[1024,1024]{1,0:T(8,128)(2,1)} fusion(f32[1024,1024]{1,0:T(8,128)S(1)} %fusion.57, bf16[1024,1024]{1,0:T(8,128)(2,1)S(1)} %get-tuple-element.124, f32[1024]{0:T(1024)S(1)} %convert_element_type.213, bf16[1024,2048]{1,0:T(8,128)(2,1)S(1)} %copy-done.41, bf16[2048,1024]{1,0:T(8,128)(2,1)} %collective-permute-done.6), kind=kOutput, calls=%fused_computation.86 | convolution fusion | flops 4300210176 | bytes 16781312 | tf_op jit(solution)/shard_map/dot_general | solution.py:32
  314.9 2.7 fusion.49
  317.6 2.0 convert_reduce_fusion.8
  321.7 2.3 convolution_convert_fusion.1.da_ref
  325.3 2.6 convolution_add_fusion.3
  327.9 17.5 %attend_back.3 = bf16[1024,1536]{1,0:T(8,128)(2,1)} custom-call(bf16[1024,1536]{1,0:T(8,128)(2,1)} %add_convert_fusion.2.qkv_ref, bf16[1024,512]{1,0:T(8,128)(2,1)} %convolution_convert_fusion.1.da_ref), custom_call_target="tpu_custom_call" | custom-call | flops 4294967296 | bytes 7340032 | tf_op jit(solution)/shard_map/attend_back/pallas_call | solution.py:110
  345.4 7.8 %fusion.61 = f32[1536,1024]{1,0:T(8,128)} fusion(bf16[1024,1536]{1,0:T(8,128)(2,1)} %attend_back.3, bf16[1024,1024]{1,0:T(8,128)(2,1)S(1)} %bitcast.101, f32[1024]{0:T(1024)S(1)} %copy-done.37, f32[1024]{0:T(1024)S(1)} %copy-done.32, f32[1024]{0:T(1024)S(1)} %copy-done.29, f32[1024]{0:T(1024)S(1)} %copy-done.25), kind=kOutput, calls=%fused_computation.139 | convolution fusion | flops 3227516928 | bytes 11550720 | tf_op jit(solution)/shard_map/dot_general | solution.py:32
  353.3 2.3 convolution_convert_fusion.2.da_ref
  355.6 17.3 %attend_back.2 = bf16[1024,1536]{1,0:T(8,128)(2,1)} custom-call(bf16[1024,1536]{1,0:T(8,128)(2,1)} %add_convert_fusion.3.qkv_ref, bf16[1024,512]{1,0:T(8,128)(2,1)} %convolution_convert_fusion.2.da_ref), custom_call_target="tpu_custom_call" | custom-call | flops 4294967296 | bytes 7340032 | tf_op jit(solution)/shard_map/attend_back/pallas_call | solution.py:110
  372.9 7.9 %convolution_add_fusion = f32[1536,1024]{1,0:T(8,128)S(1)} fusion(f32[1536,1024]{1,0:T(8,128)} %collective-permute-done.9, bf16[1024,1536]{1,0:T(8,128)(2,1)} %attend_back.2, bf16[1024,1024]{1,0:T(8,128)(2,1)S(1)} %bitcast.102, f32[1024]{0:T(1024)S(1)} %copy-done.37, f32[1024]{0:T(1024)S(1)} %copy-done.32, f32[1024]{0:T(1024)S(1)} %copy-done.29, ...), kind=kOutput, calls=%fused_computation.71 | convolution fusion | flops 3229089792 | bytes 17842176 | tf_op jit(solution)/shard_map/dot_general | solution.py:32
  380.8 6.3 %pad_maximum_fusion = f32[4,512,1024]{2,1,0:T(8,128)} fusion(f32[4,128,1024]{2,1,0:T(8,128)} %bitcast.130, f32[4,384,1024]{2,1,0:T(8,128)S(1)} %bitcast.116), kind=kLoop, calls=%fused_computation.34 | loop fusion | flops 2097152 | bytes 16777216 | tf_op jit(solution)/shard_map/concatenate | solution.py:305
  387.1 4.6 copy.41
  391.7 5.0 all-to-all-start.2
  396.7 2.5 convert_reduce_fusion.9
  399.2 46.3 %all-to-all-done.2 = bf16[4,256,1024]{2,0,1:T(4,128)(2,1)} async-done(((bf16[4,256,1024]{2,0,1:T(4,128)(2,1)}), bf16[4,256,1024]{2,0,1:T(4,128)(2,1)}, u32[]{:S(2)}, u32[]{:S(2)}) %all-to-all-start.2) | async-done | bytes 2097184 | tf_op jit(solution)/shard_map/all_to_all | solution.py:204
  445.6 3.8 copy.42
  449.4 5.5 %fusion.74 = f32[1024,1024]{1,0:T(8,128)S(1)} fusion(bf16[1024,1536]{1,0:T(8,128)(2,1)} %attend_back.2, bf16[1536,1024]{1,0:T(8,128)(2,1)S(1)} %bitcast.122), kind=kOutput, calls=%fused_computation.148 | convolution fusion | flops 3221225472 | bytes 10485760 | tf_op jit(solution)/shard_map/dot_general | solution.py:32
  454.9 4.2 convert_reduce_fusion.4
  459.1 2.7 fusion.50
  461.9 2.0 fusion.38
  463.8 2.9 copy.43
  466.8 4.8 all-to-all-start.3
  471.6 2.6 convert_reduce_fusion.3
  475.6 43.6 %sum_over_tp.1 = f32[13,1024]{1,0:T(8,128)} custom-call(f32[13,1024]{1,0:T(8,128)} %reshape.261.vec_ref), custom_call_target="tpu_custom_call" | custom-call | tf_op jit(solution)/shard_map/sum_over_tp/pallas_call | solution.py:146
  525.0 2.0 copy.44
  527.1 2.7 convert_element_type.237
  529.8 1.7 convert_bitcast_fusion
  532.9 1.7 convert.14
  (172 shorter events, 31.9 us)
Async XLA Ops:
  7.2 72.1 %all-gather.3.cloned.1.call-start = ((), (), s32[]{:S(2)}) async-start(), calls=%async_computation.7 | async-start | bytes 5406720 | tf_op jit(solution)/shard_map/all_gather | solution.py:177
  9.4 70.3 %copy-start.34 = (bf16[1024]{0:T(1024)(128)(2,1)S(1)}, bf16[1024]{0:T(1024)(128)(2,1)}, u32[]{:S(2)}) copy-start(bf16[1024]{0:T(1024)(128)(2,1)} %param.27) | copy-start | bytes 6148
  11.8 68.0 %all-to-all-start = ((bf16[8,4,32,1024]{3,2,1,0:T(8,128)(2,1)}), bf16[8,4,32,1024]{3,2,1,0:T(8,128)(2,1)S(1)}, u32[]{:S(2)}, u32[]{:S(2)}) async-start(bf16[8,4,32,1024]{3,2,1,0:T(8,128)(2,1)} %bitcast.125), calls=%async_computation | async-start | bytes 4194304 | tf_op jit(solution)/shard_map/all_to_all | solution.py:198
  17.8 115.5 %all-gather.5.cloned.1.call-start = ((), (), s32[]{:S(2)}) async-start(), calls=%async_computation.8 | async-start | bytes 5242880 | tf_op jit(solution)/shard_map/all_gather | solution.py:177
  79.3 27.6 %collective-permute-start = (bf16[2112,1024]{1,0:T(8,128)(2,1)}, bf16[2112,1024]{1,0:T(8,128)(2,1)}, u32[]{:S(2)}, u32[]{:S(2)}) collective-permute-start(bf16[2112,1024]{1,0:T(8,128)(2,1)} %all-gather.3.cloned.1.call-done), channel_id=1, source_target_pairs={{0,1},{1,0},{2,3},{3,2},{4,5},{5,4},{6,7},{7,6},{8,9},{9,8},{10,11... | collective-permute-start | bytes 12976136 | tf_op jit(solution)/shard_map/ppermute | solution.py:186
  79.8 1.3 copy-start.9
  81.1 3.6 copy-start.10
  83.1 30.2 %copy-start = (bf16[4,8,32,1024]{3,2,1,0:T(8,128)(2,1)}, bf16[4,8,32,1024]{3,2,1,0:T(8,128)(2,1)S(1)}, u32[]{:S(2)}) copy-start(bf16[4,8,32,1024]{3,2,1,0:T(8,128)(2,1)S(1)} %copy.39) | copy-start | bytes 6291460
  83.4 29.8 %copy-start.24 = (f32[1024]{0:T(1024)}, f32[1024]{0:T(1024)S(1)}, u32[]{:S(2)}) copy-start(f32[1024]{0:T(1024)S(1)} %broadcast_multiply_fusion.1) | copy-start | bytes 12292
  84.1 0.6 copy-start.26
  84.7 28.5 %copy-start.28 = (f32[1024]{0:T(1024)}, f32[1024]{0:T(1024)S(1)}, u32[]{:S(2)}) copy-start(f32[1024]{0:T(1024)S(1)} %fusion.55) | copy-start | bytes 12292
  84.7 2.1 copy-start.31
  84.8 2.1 copy-start.36
  84.8 17.6 %copy-start.19 = (bf16[4,128,1024]{2,1,0:T(8,128)(2,1)}, bf16[4,128,1024]{2,1,0:T(8,128)(2,1)S(1)}, u32[]{:S(2)}) copy-start(bf16[4,128,1024]{2,1,0:T(8,128)(2,1)S(1)} %slice.135) | copy-start | bytes 3145732
  108.1 20.4 %copy-start.21 = (bf16[4,128,1024]{2,1,0:T(8,128)(2,1)}, bf16[4,128,1024]{2,1,0:T(8,128)(2,1)S(1)}, u32[]{:S(2)}) copy-start(bf16[4,128,1024]{2,1,0:T(8,128)(2,1)S(1)} %slice.138) | copy-start | bytes 3145732
  133.2 6.6 %copy-start.23 = (f32[1024]{0:T(1024)S(1)}, f32[1024]{0:T(1024)}, u32[]{:S(2)}) copy-start(f32[1024]{0:T(1024)} %param.28) | copy-start | bytes 12292
  133.2 6.6 %copy-start.33 = (f32[1024]{0:T(1024)S(1)}, f32[1024]{0:T(1024)}, u32[]{:S(2)}) copy-start(f32[1024]{0:T(1024)} %param.29) | copy-start | bytes 12292
  133.3 7.6 %collective-permute-start.1 = (bf16[2048,1024]{0,1:T(8,128)(2,1)}, bf16[2048,1024]{0,1:T(8,128)(2,1)}, u32[]{:S(2)}, u32[]{:S(2)}) collective-permute-start(bf16[2048,1024]{0,1:T(8,128)(2,1)} %all-gather.5.cloned.1.call-done), channel_id=1, source_target_pairs={{0,1},{1,0},{2,3},{3,2},{4,5},{5,4},{6,7},{7,6},{8,9},{9,8},{10,11... | collective-permute-start | bytes 12582920 | tf_op jit(solution)/shard_map/ppermute | solution.py:186
  133.4 31.1 %all-to-all-start.1 = ((bf16[8,4,32,1024]{3,2,1,0:T(8,128)(2,1)}), bf16[8,4,32,1024]{3,2,1,0:T(8,128)(2,1)}, u32[]{:S(2)}, u32[]{:S(2)}) async-start(bf16[8,4,32,1024]{3,2,1,0:T(8,128)(2,1)} %bitcast.126), calls=%async_computation.1 | async-start | bytes 4194304 | tf_op jit(solution)/shard_map/all_to_all | solution.py:198
  138.1 389.0 %reduce-scatter.8.cloned.1.call-start = ((), (), s32[]{:S(2)}) async-start(), calls=%async_computation.11 | async-start | bytes 10485760 | tf_op jit(solution)/shard_map/reduce_scatter | solution.py:180
  140.6 1.3 copy-start.15
  164.5 2.8 copy-start.40
  166.5 7.6 %copy-start.2 = (bf16[4,8,32,1024]{3,2,1,0:T(8,128)(2,1)}, bf16[4,8,32,1024]{3,2,1,0:T(8,128)(2,1)S(1)}, u32[]{:S(2)}) copy-start(bf16[4,8,32,1024]{3,2,1,0:T(8,128)(2,1)S(1)} %copy.40) | copy-start | bytes 6291460
  167.3 8.5 %copy-start.18 = (bf16[512,1024]{1,0:T(8,128)(2,1)S(1)}, bf16[512,1024]{1,0:T(8,128)(2,1)}, u32[]{:S(2)}) copy-start(bf16[512,1024]{1,0:T(8,128)(2,1)} %param.32) | copy-start | bytes 3145732
  174.1 14.1 %collective-permute-start.5 = (f32[2048,1024]{1,0:T(8,128)}, f32[2048,1024]{1,0:T(8,128)}, u32[]{:S(2)}, u32[]{:S(2)}) collective-permute-start(f32[2048,1024]{1,0:T(8,128)} %fusion.70), channel_id=1, source_target_pairs={{0,1},{1,0},{2,3},{3,2},{4,5},{5,4},{6,7},{7,6},{8,9},{9,8},{10,11... | collective-permute-start | bytes 25165832 | tf_op jit(solution)/shard_map/ppermute | solution.py:186
  175.8 26.4 %collective-permute-start.4 = (bf16[512,1024]{1,0:T(8,128)(2,1)S(1)}, bf16[512,1024]{1,0:T(8,128)(2,1)}, u32[]{:S(2)}, u32[]{:S(2)}) collective-permute-start(bf16[512,1024]{1,0:T(8,128)(2,1)S(1)} %copy-done.18), channel_id=1, source_target_pairs={{0,4},{1,5},{2,6},{3,7},{4,0},{5,1},{6,2},{7,3},{8,12},{9,13},{10,... | collective-permute-start | bytes 3145736 | tf_op jit(solution)/shard_map/ppermute | solution.py:183
  175.9 47.3 %collective-permute-start.3 = (bf16[512,1024]{1,0:T(8,128)(2,1)S(1)}, bf16[512,1024]{1,0:T(8,128)(2,1)}, u32[]{:S(2)}, u32[]{:S(2)}) collective-permute-start(bf16[512,1024]{1,0:T(8,128)(2,1)S(1)} %copy-done.18), channel_id=1, source_target_pairs={{0,6},{1,7},{2,0},{3,1},{4,2},{5,3},{6,4},{7,5},{8,14},{9,15},{10,... | collective-permute-start | bytes 3145736 | tf_op jit(solution)/shard_map/ppermute | solution.py:183
  178.6 46.4 %collective-permute-start.2 = (bf16[512,1024]{1,0:T(8,128)(2,1)S(1)}, bf16[512,1024]{1,0:T(8,128)(2,1)}, u32[]{:S(2)}, u32[]{:S(2)}) collective-permute-start(bf16[512,1024]{1,0:T(8,128)(2,1)S(1)} %copy-done.18), channel_id=1, source_target_pairs={{0,2},{1,3},{2,4},{3,5},{4,6},{5,7},{6,0},{7,1},{8,10},{9,11},{10,... | collective-permute-start | bytes 3145736 | tf_op jit(solution)/shard_map/ppermute | solution.py:183
  178.6 9.6 %copy-start.3 = (bf16[4,8,32,1024]{3,2,1,0:T(8,128)(2,1)S(1)}, bf16[4,8,32,1024]{3,2,1,0:T(8,128)(2,1)}, u32[]{:S(2)}) copy-start(bf16[4,8,32,1024]{3,2,1,0:T(8,128)(2,1)} %copy-done.2) | copy-start | bytes 6291460
  186.0 2.1 copy-start.42
  235.5 13.9 %collective-permute-start.6 = (bf16[2048,1024]{1,0:T(8,128)(2,1)}, bf16[2048,1024]{1,0:T(8,128)(2,1)}, u32[]{:S(2)}, u32[]{:S(2)}) collective-permute-start(bf16[2048,1024]{1,0:T(8,128)(2,1)} %constant_dynamic-update-slice_fusion.6), channel_id=1, source_target_pairs={{0,1},{1,0},{2,3},{3,2},{4,5},{5,4},{6,7},{7,6},{8,9},{9,8},{10,11... | collective-permute-start | bytes 12582920 | tf_op jit(solution)/shard_map/ppermute | solution.py:186
  236.1 293.7 %reduce-scatter.6.cloned.1.call-start = ((), (), s32[]{:S(2)}) async-start(), calls=%async_computation.10 | async-start | bytes 10485760 | tf_op jit(solution)/shard_map/reduce_scatter | solution.py:180
  236.1 13.3 %copy-start.4 = (bf16[4,8,32,1024]{3,2,1,0:T(8,128)(2,1)S(1)}, bf16[4,8,32,1024]{3,2,1,0:T(8,128)(2,1)}, u32[]{:S(2)}) copy-start(bf16[4,8,32,1024]{3,2,1,0:T(8,128)(2,1)} %copy-done.2) | copy-start | bytes 6291460
  236.1 13.3 %copy-start.44 = (bf16[1024,2048]{1,0:T(8,128)(2,1)S(1)}, bf16[1024,2048]{1,0:T(8,128)(2,1)}, u32[]{:S(2)}) copy-start(bf16[1024,2048]{1,0:T(8,128)(2,1)} %get-tuple-element.126) | copy-start | bytes 12582916
  249.4 30.9 %copy-start.39 = (bf16[1024,2048]{1,0:T(8,128)(2,1)}, bf16[1024,2048]{1,0:T(8,128)(2,1)S(1)}, u32[]{:S(2)}) copy-start(bf16[1024,2048]{1,0:T(8,128)(2,1)S(1)} %get-tuple-element.110) | copy-start | bytes 12582916
  249.4 13.0 %copy-start.16 = (bf16[1024,1024]{1,0:T(8,128)(2,1)S(1)}, bf16[1024,1024]{1,0:T(8,128)(2,1)}, u32[]{:S(2)}) copy-start(bf16[1024,1024]{1,0:T(8,128)(2,1)} %copy-done.15) | copy-start | bytes 6291460
  262.5 4.7 copy-start.35
  267.1 13.2 %collective-permute-start.7 = (f32[2048,1024]{1,0:T(8,128)S(1)}, f32[2048,1024]{1,0:T(8,128)S(1)}, u32[]{:S(2)}, u32[]{:S(2)}) collective-permute-start(f32[2048,1024]{1,0:T(8,128)S(1)} %fusion.71), channel_id=1, source_target_pairs={{0,1},{1,0},{2,3},{3,2},{4,5},{5,4},{6,7},{7,6},{8,9},{9,8},{10,11... | collective-permute-start | bytes 25165832 | tf_op jit(solution)/shard_map/ppermute | solution.py:186
  287.5 245.4 %reduce-scatter.4.cloned.1.call-start = ((), (), s32[]{:S(2)}) async-start(), calls=%async_computation.9 | async-start | bytes 10485760 | tf_op jit(solution)/shard_map/reduce_scatter | solution.py:180
  287.8 9.4 %copy-start.43 = (bf16[1024,2048]{1,0:T(8,128)(2,1)S(1)}, bf16[1024,2048]{1,0:T(8,128)(2,1)}, u32[]{:S(2)}) copy-start(bf16[1024,2048]{1,0:T(8,128)(2,1)} %copy-done.42) | copy-start | bytes 12582916
  297.2 7.7 %copy-start.41 = (bf16[1024,2048]{1,0:T(8,128)(2,1)S(1)}, bf16[1024,2048]{1,0:T(8,128)(2,1)}, u32[]{:S(2)}) copy-start(bf16[1024,2048]{1,0:T(8,128)(2,1)} %get-tuple-element.125) | copy-start | bytes 12582916
  313.5 4.1 copy-start.5
  317.6 2.1 copy-start.17
  319.7 5.6 %copy-start.6 = (bf16[1024,1024]{1,0:T(8,128)(2,1)}, bf16[1024,1024]{1,0:T(8,128)(2,1)S(1)}, u32[]{:S(2)}) copy-start(bf16[1024,1024]{1,0:T(8,128)(2,1)S(1)} %get-tuple-element.112) | copy-start | bytes 6291460
  319.7 2.0 copy-start.22
  321.0 4.2 copy-start.38
  321.0 4.2 collective-permute-start.8
  327.9 17.5 %copy-start.1 = (bf16[4,8,32,1024]{3,2,1,0:T(8,128)(2,1)S(1)}, bf16[4,8,32,1024]{3,2,1,0:T(8,128)(2,1)}, u32[]{:S(2)}) copy-start(bf16[4,8,32,1024]{3,2,1,0:T(8,128)(2,1)} %copy-done) | copy-start | bytes 6291460
  327.9 17.5 %copy-start.25 = (f32[1024]{0:T(1024)S(1)}, f32[1024]{0:T(1024)}, u32[]{:S(2)}) copy-start(f32[1024]{0:T(1024)} %copy-done.24) | copy-start | bytes 12292
  327.9 17.5 %copy-start.29 = (f32[1024]{0:T(1024)S(1)}, f32[1024]{0:T(1024)}, u32[]{:S(2)}) copy-start(f32[1024]{0:T(1024)} %copy-done.28) | copy-start | bytes 12292
  327.9 17.5 %copy-start.32 = (f32[1024]{0:T(1024)S(1)}, f32[1024]{0:T(1024)}, u32[]{:S(2)}) copy-start(f32[1024]{0:T(1024)} %param.19) | copy-start | bytes 12292
  327.9 17.5 %copy-start.37 = (f32[1024]{0:T(1024)S(1)}, f32[1024]{0:T(1024)}, u32[]{:S(2)}) copy-start(f32[1024]{0:T(1024)} %param.20) | copy-start | bytes 12292
  345.4 7.9 %copy-start.7 = (bf16[1024,1024]{1,0:T(8,128)(2,1)S(1)}, bf16[1024,1024]{1,0:T(8,128)(2,1)}, u32[]{:S(2)}) copy-start(bf16[1024,1024]{1,0:T(8,128)(2,1)} %copy-done.6) | copy-start | bytes 6291460
  345.4 7.9 %copy-start.20 = (bf16[4,128,1024]{2,1,0:T(8,128)(2,1)S(1)}, bf16[4,128,1024]{2,1,0:T(8,128)(2,1)}, u32[]{:S(2)}) copy-start(bf16[4,128,1024]{2,1,0:T(8,128)(2,1)} %copy-done.19) | copy-start | bytes 3145732
  353.2 19.6 %collective-permute-start.9 = (f32[1536,1024]{1,0:T(8,128)}, f32[1536,1024]{1,0:T(8,128)}, u32[]{:S(2)}, u32[]{:S(2)}) collective-permute-start(f32[1536,1024]{1,0:T(8,128)} %fusion.61), channel_id=1, source_target_pairs={{0,1},{1,0},{2,3},{3,2},{4,5},{5,4},{6,7},{7,6},{8,9},{9,8},{10,11... | collective-permute-start | bytes 18874376 | tf_op jit(solution)/shard_map/ppermute | solution.py:186
  391.7 53.9 %all-to-all-start.2 = ((bf16[4,256,1024]{2,0,1:T(4,128)(2,1)}), bf16[4,256,1024]{2,0,1:T(4,128)(2,1)}, u32[]{:S(2)}, u32[]{:S(2)}) async-start(bf16[4,256,1024]{2,0,1:T(4,128)(2,1)} %copy.41), calls=%async_computation.2 | async-start | bytes 4194304 | tf_op jit(solution)/shard_map/all_to_all | solution.py:204
  445.6 3.8 copy-start.11
  449.4 5.5 %copy-start.12 = (bf16[4,384,1024]{2,1,0:T(8,128)(2,1)S(1)}, bf16[4,384,1024]{2,1,0:T(8,128)(2,1)}, u32[]{:S(2)}) copy-start(bf16[4,384,1024]{2,1,0:T(8,128)(2,1)} %slice.136) | copy-start | bytes 9437188
  449.4 5.5 %copy-start.13 = (bf16[1024,1536]{1,0:T(8,128)(2,1)S(1)}, bf16[1024,1536]{1,0:T(8,128)(2,1)}, u32[]{:S(2)}) copy-start(bf16[1024,1536]{1,0:T(8,128)(2,1)} %attend_back.3) | copy-start | bytes 9437188
  454.9 4.2 copy-start.27
  459.1 2.8 copy-start.8
  466.8 58.3 %all-to-all-start.3 = ((bf16[4,256,1024]{2,0,1:T(4,128)(2,1)}), bf16[4,256,1024]{2,0,1:T(4,128)(2,1)S(1)}, u32[]{:S(2)}, u32[]{:S(2)}) async-start(bf16[4,256,1024]{2,0,1:T(4,128)(2,1)} %copy.43), calls=%async_computation.3 | async-start | bytes 4194304 | tf_op jit(solution)/shard_map/all_to_all | solution.py:204
  471.5 2.9 copy-start.14
  471.6 3.4 copy-start.30
Sparse Core Ops, SparseCore 0:
  11.9 67.3 all-gather.2
  80.8 44.2 all-gather.4
  236.2 75.9 reduce-scatter.7
  314.4 76.1 reduce-scatter.5
  392.8 124.0 reduce-scatter.3

commit v6 on v5

--- a/solution.py
+++ b/solution.py
@@ -179,9 +179,6 @@
     def scatter_rows(rows):
         return lax.psum_scatter(rows, 'tp', scatter_dimension=0, tiled=True, axis_index_groups=rings)
 
-    def shift(t, chip_steps):
-        return lax.ppermute(t, 'tp', [(i, (i + 2 * chip_steps) % tp) for i in range(tp)])
-
     def swap(t):
         return lax.ppermute(t, 'tp', pairs)
 
@@ -224,10 +221,8 @@
         qkv_rows = place([(t, i * cols) for i, t in enumerate(pieces)]
                          + [(jnp.broadcast_to(bias_row[None], (PAD, width)), my_rows)], my_rows + PAD)
         packed = both(gather_rows(qkv_rows))
-        me = lax.axis_index('tp')
-        core, chip = lax.rem(me, 2), me // 2
         x_img = lax.optimization_barrier(join_tokens(to_images(x)))
-        w1_mine = gather_rows(w_1.T)
+        w1_mine, w2_mine = gather_rows(w_1.T), gather_rows(w_2)
 
         w_qkv, wo, b_qkv, b_1_all = [], [], [], []
         for half in packed:
@@ -246,9 +241,6 @@
         qkv_theirs = (dot(h_one, w_qkv[1], 1, 1) + b_qkv[1]).astype(BF16)
         mixed_theirs = attend(qkv_theirs, images, my_heads, head_dim)
         qkv, mixed = [qkv_mine, qkv_theirs], [mixed_mine, mixed_theirs]
-        (w_2_late,) = after((w_2,), mixed_theirs)
-        steps = sorted(range(1, chips), key=lambda k: min(k, chips - k))
-        w2_pieces = [shift(w_2_late, k) for k in steps]
         x_mid = (x_f32 + dot(mixed[0], wo[0], 1, 0) + dot(mixed[1], wo[1], 1, 0) + b_o.astype(F32)).astype(BF16)
         w1 = both(w1_mine, x_mid)
         mid_f32 = x_mid.astype(F32)
@@ -267,12 +259,7 @@
         hidden = [gelus[0][0].astype(BF16), hidden_theirs]
         sum_2 = dot(hidden[0], d_out_img, 0, 0) + swap(theirs_2)
         grad_w_2 = scatter_rows(sum_2).astype(BF16)
-        (d_out_late,) = after((d_out_img,), sum_2)
-        d_out_sum = lax.optimization_barrier(token_sum(d_out_late))
-        w2_mine = jnp.zeros((chips * hid, width), BF16)
-        for k, piece in zip([0, *steps], after((w_2_late, *w2_pieces), sum_2)):
-            w2_mine = lax.dynamic_update_slice(w2_mine, piece, (lax.rem(chip + chips - k, chips) * hid, 0))
-        w2 = both(w2_mine)
+        w2 = both(w2_mine, sum_2)
         d_first = dot(d_out_img, after(w2[:1], sum_2)[0], 1, 1).astype(BF16)
         d_hidden = [d_first, dot(d_out_img, after(w2[1:], d_first)[0], 1, 1).astype(BF16)]
         d_pre = [g[1](d.astype(F32))[0].astype(BF16) for g, d in zip(gelus, d_hidden)]
@@ -302,18 +289,22 @@
         d_in_ln, g_ln1_gain, g_ln1_bias = ln1_pull(d_h_one.astype(F32))
         grad_x_img = (d_mid.astype(F32) + d_in_ln).astype(BF16)
         grad_x = to_tokens(grad_x_img)
+        sum_o, sum_qkv = after((sum_o, sum_qkv), grad_x_img)
         sum_all = jnp.concatenate([sum_qkv.reshape(chips, qkv_cols, width), sum_o.reshape(chips, cols, width)], axis=1)
         g_all = scatter_rows(sum_all.reshape(chips * my_rows, width))
         grad_w_o = g_all[qkv_cols:].astype(BF16).reshape(my_heads, head_dim, width)
         g_qkv = g_all[:qkv_cols].reshape(3, cols, width)
         grad_w_q, grad_w_k, grad_w_v = (g_qkv[i].T.astype(BF16).reshape(width, my_heads, head_dim) for i in range(3))
 
+        me = lax.axis_index('tp')
+        core, chip = lax.rem(me, 2), me // 2
+
         def halves(sums):
             first = jnp.where(core == 0, sums[0], sums[1])
             second = jnp.where(core == 0, sums[1], sums[0])
             return [first, second]
 
-        vecs = jnp.concatenate([g_ln1_gain, g_ln1_bias, token_sum(d_mid), g_ln2_gain, g_ln2_bias, d_out_sum]
+        vecs = jnp.concatenate([g_ln1_gain, g_ln1_bias, token_sum(d_mid), g_ln2_gain, g_ln2_bias, token_sum(d_out_img)]
                                + halves([token_sum(t) for t in d_qkv]) + halves(d_pre_sums))
         sums = sum_over_tp(vecs.reshape(-1, width), tp).reshape(-1)
         six = [sums[i * width:(i + 1) * width] for i in range(6)]

time: 552 us -> 545 us (0.987)
  local copies, waits for them, and re-layouts: 49.6 us -> 37.3 us
  Pallas kernels: 94.9 us -> 107 us
    ppermute x3 -> x0, waiting for transfers between devices: 26.1 us -> none  [shift(): lax.ppermute(t, 'tp', [(i, (i + 2 * chip_steps) % tp) for i in range(tp)])]
    all_gather x2 -> x3, waiting for transfers between devices: 60.7 us -> 80.8 us  [gather_rows(): lax.all_gather(rows, 'tp', axis=0, tiled=True, axis_index_groups=rings)]
    pallas_call x1, Pallas kernels: 43.6 us -> 55.3 us  [sum_over_tp(): pl.pallas_call(functools.partial(sum_kernel, n), out_shape=jax.ShapeDtype...]
    dynamic_update_slice x4 -> x0, local copies, waits for them, and re-layouts: 7.9 us -> none  [layer_body(): lax.dynamic_update_slice(w2_mine, piece, (lax.rem(chip + chips - k, chips...]
  transfers between devices with their start and end apart: 19 -> 17, of which waited for: 10 -> 8; matrix products, arithmetic and copies ran while one was open for 41% -> 40% of each run, Pallas kernels for 17% -> 20%
where the time goes in v6:
time: 545 us; the launch traced here: 535 us
  matrix products  163 us (30%)
  waiting for transfers between devices  154 us (28%)
  Pallas kernels  107 us (20%)
  local copies, waits for them, and re-layouts  37.3 us (7%)
  other arithmetic  36.3 us (7%)
  starting transfers between devices  23.2 us (4%)
  between operations  15.3 us (3%)
    dot_general x24, matrix products, dot(): lax.dot_general(a, b, (((ca,), (cb,)), ((), ())), preferred_element_type=...  163 us
    all_gather x3, waiting for transfers between devices, gather_rows(): lax.all_gather(rows, 'tp', axis=0, tiled=True, axis_index_groups=rings)  80.8 us
    pallas_call x1, Pallas kernels, sum_over_tp(): pl.pallas_call(functools.partial(sum_kernel, n), out_shape=jax.ShapeDtype...  55.3 us
    all_to_all x2, waiting for transfers between devices, to_tokens(): lax.all_to_all(t.reshape(images, patches, width), 'tp', 1, 0, tiled=True)  49.3 us
    pallas_call x2, Pallas kernels, attend_back(): pl.pallas_call(functools.partial(attend_back_kernel, group, heads, head_d...  34.9 us
    pallas_call x2, Pallas kernels, attend(): pl.pallas_call(functools.partial(attend_kernel, group, heads, head_dim),...  16.5 us
    all_to_all x2, waiting for transfers between devices, to_images(): lax.all_to_all(t.reshape(tp, images, patches // tp, width), 'tp', 0, 0, t...  11.7 us
    ppermute x7, waiting for transfers between devices, swap(): return lax.ppermute(t, 'tp', pairs)  11.1 us
  transfers between devices with their start and end apart: 17, of which 8 were waited for; matrix products, arithmetic and copies ran while one was open for 40% of the time, Pallas kernels for 20%

profile of v6, /device:TPU:113, one launch (start us, length us, event | category | flops | bytes accessed | tf_op | source)
XLA Modules:
  0.0 535.2 jit_solution(16743396940176658355)
XLA Ops:
  9.5 2.2 pad_maximum_fusion.1
  11.8 6.0 %all-to-all-start = ((bf16[8,4,32,1024]{3,2,1,0:T(8,128)(2,1)}), bf16[8,4,32,1024]{3,2,1,0:T(8,128)(2,1)S(1)}, u32[]{:S(2)}, u32[]{:S(2)}) async-start(bf16[8,4,32,1024]{3,2,1,0:T(8,128)(2,1)} %bitcast.125), calls=%async_computation | async-start | bytes 4194304 | tf_op jit(solution)/shard_map/all_to_all | solution.py:195
  18.6 60.7 %all-gather.4.cloned.1.call-done = bf16[2112,1024]{1,0:T(8,128)(2,1)} async-done(((bf16[528,1024]{1,0:T(8,128)(2,1)}), bf16[2112,1024]{1,0:T(8,128)(2,1)}) %all-gather.4.cloned.1.call-update) | async-done | bytes 4325392 | tf_op jit(solution)/shard_map/all_gather | solution.py:177
  79.8 1.3 copy-done.9
  81.1 2.0 copy.39
  84.8 2.0 slice.133
  86.9 7.2 %add_convert_fusion.3.qkv_ref = bf16[1024,1536]{1,0:T(8,128)(2,1)} fusion(bf16[1536,1024]{1,0:T(8,128)(2,1)} %bitcast.121, f32[1536]{0:T(1024)S(1)} %reshape.270, bf16[1024,1024]{1,0:T(8,128)(2,1)S(1)} %bitcast.98, f32[1024]{0:T(1024)S(1)} %copy-done.38, f32[1024]{0:T(1024)S(1)} %copy-done.32, f32[1024]{0:T(1024)S(1)} %fusion.56, ...), kind=kOutput, calls=%fused_computation.57 | convolution fusion | flops 3230662656 | bytes 8411136 | tf_op jit(solution)/shard_map/dot_general | solution.py:32
  94.1 8.2 %attend.2 = bf16[1024,512]{1,0:T(8,128)(2,1)} custom-call(bf16[1024,1536]{1,0:T(8,128)(2,1)} %add_convert_fusion.3.qkv_ref), custom_call_target="tpu_custom_call" | custom-call | flops 2147483648 | bytes 4194304 | tf_op jit(solution)/shard_map/attend/pallas_call | solution.py:93
  102.4 4.6 fusion.71
  106.9 1.3 slice.138
  108.2 4.4 slice.136
  113.4 7.0 %add_convert_fusion.2.qkv_ref = bf16[1024,1536]{1,0:T(8,128)(2,1)} fusion(bf16[1536,1024]{1,0:T(8,128)(2,1)} %bitcast.123, f32[1536]{0:T(1024)S(1)} %reshape.271, bf16[1024,1024]{1,0:T(8,128)(2,1)S(1)} %bitcast.99, f32[1024]{0:T(1024)S(1)} %copy-done.38, f32[1024]{0:T(1024)S(1)} %copy-done.32, f32[1024]{0:T(1024)S(1)} %fusion.56, ...), kind=kOutput, calls=%fused_computation.56 | convolution fusion | flops 3230662656 | bytes 8411136 | tf_op jit(solution)/shard_map/dot_general | solution.py:32
  120.5 8.2 %attend.3 = bf16[1024,512]{1,0:T(8,128)(2,1)} custom-call(bf16[1024,1536]{1,0:T(8,128)(2,1)} %add_convert_fusion.2.qkv_ref), custom_call_target="tpu_custom_call" | custom-call | flops 2147483648 | bytes 4194304 | tf_op jit(solution)/shard_map/attend/pallas_call | solution.py:93
  128.7 4.7 convert_reduce_fusion.6
  133.5 4.7 all-to-all-start.1
  142.1 10.9 %fusion.13 = (bf16[1024,2048]{1,0:T(8,128)(2,1)}, bf16[1024,2048]{1,0:T(8,128)(2,1)}) fusion(f32[2048]{0:T(1024)S(1)} %bitcast.144, bf16[1024,1024]{1,0:T(8,128)(2,1)S(1)} %fusion.35, bf16[2048,1024]{0,1:T(8,128)(2,1)} %collective-permute-done.1), kind=kOutput, calls=%fused_computation.25 | convolution fusion | flops 4320133120 | bytes 14688256 | tf_op jit(solution)/shard_map/dot_general | solution.py:32
  153.0 11.7 %all-to-all-done.1 = bf16[8,4,32,1024]{3,2,1,0:T(8,128)(2,1)} async-done(((bf16[8,4,32,1024]{3,2,1,0:T(8,128)(2,1)}), bf16[8,4,32,1024]{3,2,1,0:T(8,128)(2,1)}, u32[]{:S(2)}, u32[]{:S(2)}) %all-to-all-start.1) | async-done | bytes 2097184 | tf_op jit(solution)/shard_map/all_to_all | solution.py:195
  164.6 2.0 copy.40
  167.5 6.8 %fusion.72 = f32[2048,1024]{1,0:T(8,128)} fusion(bf16[1024,2048]{1,0:T(8,128)(2,1)S(1)} %copy-done.42, bf16[1024,1024]{1,0:T(8,128)(2,1)S(1)} %bitcast.107), kind=kOutput, calls=%fused_computation.141 | convolution fusion | flops 4294967296 | bytes 14680064 | tf_op jit(solution)/shard_map/dot_general | solution.py:32
  176.1 7.5 %add_convert_fusion = bf16[1024,2048]{1,0:T(8,128)(2,1)S(1)} fusion(f32[2048]{0:T(1024)S(1)} %bitcast.145, bf16[1024,1024]{1,0:T(8,128)(2,1)} %copy-done.17, bf16[2048,1024]{0,1:T(8,128)(2,1)} %all-gather.6.cloned.1.call-done), kind=kOutput, calls=%fused_computation.37 | convolution fusion | flops 4299161600 | bytes 10493952 | tf_op jit(solution)/shard_map/dot_general | solution.py:32
  183.6 4.7 collective-permute-done.2
  188.3 10.4 %convolution_add_fusion.2 = f32[2048,1024]{1,0:T(8,128)} fusion(f32[2048,1024]{1,0:T(8,128)} %collective-permute-done.2, bf16[1024,1024]{1,0:T(8,128)(2,1)S(1)} %bitcast.109, bf16[1024,2048]{1,0:T(8,128)(2,1)S(1)} %add_convert_fusion), kind=kOutput, calls=%fused_computation.95 | convolution fusion | flops 4318035968 | bytes 23068672 | tf_op jit(solution)/shard_map/dot_general | solution.py:32
  198.8 20.1 %all-gather.8.cloned.1.call-done = bf16[2048,1024]{1,0:T(8,128)(2,1)} async-done(((bf16[512,1024]{1,0:T(8,128)(2,1)}), bf16[2048,1024]{1,0:T(8,128)(2,1)}) %all-gather.8.cloned.1.call-update) | async-done | bytes 4194320 | tf_op jit(solution)/shard_map/all_gather | solution.py:177
  220.2 13.3 %convert_reduce_fusion.1 = (f32[2048]{0:T(1024)}, bf16[1024,2048]{1,0:T(8,128)(2,1)S(1)}) fusion(bf16[1024,2048]{1,0:T(8,128)(2,1)} %copy-done.44, bf16[1024,1024]{1,0:T(8,128)(2,1)} %bitcast.108, bf16[2048,1024]{1,0:T(8,128)(2,1)} %all-gather.8.cloned.1.call-done), kind=kOutput, calls=%fused_computation.36 | convolution fusion | flops 4347394048 | bytes 14688256 | tf_op jit(solution)/shard_map/dot_general | solution.py:32
  233.5 13.0 %convert_reduce_fusion = (f32[2048]{0:T(1024)S(1)}, bf16[1024,2048]{1,0:T(8,128)(2,1)S(1)}) fusion(bf16[1024,2048]{1,0:T(8,128)(2,1)S(1)} %copy-done.46, bf16[1024,1024]{1,0:T(8,128)(2,1)S(1)} %bitcast.110, bf16[2048,1024]{1,0:T(8,128)(2,1)} %collective-permute-done.3), kind=kOutput, calls=%fused_computation.35 | convolution fusion | flops 4347394048 | bytes 14688256 | tf_op jit(solution)/shard_map/dot_general | solution.py:32
  246.5 4.6 fusion.73
  251.3 8.3 %fusion.74 = f32[1024,1024]{1,0:T(8,128)} fusion(bf16[1024,2048]{1,0:T(8,128)(2,1)S(1)} %get-tuple-element.123, bf16[2048,1024]{0,1:T(8,128)(2,1)} %collective-permute-done.1), kind=kOutput, calls=%fused_computation.143 | convolution fusion | flops 4294967296 | bytes 12582912 | tf_op jit(solution)/shard_map/dot_general | solution.py:32
  259.5 4.8 collective-permute-done.4
  264.4 7.2 %convolution_add_fusion.1 = f32[2048,1024]{1,0:T(8,128)} fusion(f32[2048,1024]{1,0:T(8,128)S(1)} %collective-permute-done.4, bf16[1024,2048]{1,0:T(8,128)(2,1)S(1)} %get-tuple-element.102, bf16[1024,1024]{1,0:T(8,128)(2,1)S(1)} %copy-done.18), kind=kOutput, calls=%fused_computation.94 | convolution fusion | flops 4297064448 | bytes 23068672 | tf_op jit(solution)/shard_map/dot_general | solution.py:32
  271.9 9.5 %add_convert_fusion.5 = bf16[1024,1024]{1,0:T(8,128)(2,1)S(1)} fusion(f32[1024,1024]{1,0:T(8,128)} %fusion.74, bf16[1024,2048]{1,0:T(8,128)(2,1)} %copy-done.41, bf16[2048,1024]{0,1:T(8,128)(2,1)} %all-gather.6.cloned.1.call-done), kind=kOutput, calls=%fused_computation.93 | convolution fusion | flops 4297064448 | bytes 14680064 | tf_op jit(solution)/shard_map/dot_general | solution.py:32
  281.4 5.3 fusion.58
  286.8 8.4 %fusion.49 = bf16[1024,1024]{1,0:T(8,128)(2,1)} fusion(f32[1024,1024]{1,0:T(8,128)S(1)} %fusion.58, bf16[1024,1024]{1,0:T(8,128)(2,1)S(1)} %get-tuple-element.117, f32[1024]{0:T(1024)S(1)} %convert_element_type.211, bf16[1024,2048]{1,0:T(8,128)(2,1)S(1)} %copy-done.43, bf16[2048,1024]{1,0:T(8,128)(2,1)} %collective-permute-done.3), kind=kOutput, calls=%fused_computation.89 | convolution fusion | flops 4300210176 | bytes 16781312 | tf_op jit(solution)/shard_map/dot_general | solution.py:32
  295.2 1.3 convert_reduce_fusion.5
  296.5 2.7 fusion.50
  299.3 2.3 convert_reduce_fusion.8
  301.7 1.3 fusion.75
  303.6 2.3 convolution_convert_fusion.1.da_ref
  305.9 1.3 collective-permute-done.5
  307.2 2.6 convolution_add_fusion.3
  309.8 17.6 %attend_back.3 = bf16[1024,1536]{1,0:T(8,128)(2,1)} custom-call(bf16[1024,1536]{1,0:T(8,128)(2,1)} %add_convert_fusion.2.qkv_ref, bf16[1024,512]{1,0:T(8,128)(2,1)} %convolution_convert_fusion.1.da_ref), custom_call_target="tpu_custom_call" | custom-call | flops 4294967296 | bytes 7340032 | tf_op jit(solution)/shard_map/attend_back/pallas_call | solution.py:110
  327.5 7.8 %fusion.62 = f32[1536,1024]{1,0:T(8,128)} fusion(bf16[1024,1536]{1,0:T(8,128)(2,1)} %attend_back.3, bf16[1024,1024]{1,0:T(8,128)(2,1)S(1)} %bitcast.101, f32[1024]{0:T(1024)S(1)} %copy-done.39, f32[1024]{0:T(1024)S(1)} %copy-done.33, f32[1024]{0:T(1024)S(1)} %copy-done.30, f32[1024]{0:T(1024)S(1)} %copy-done.25), kind=kOutput, calls=%fused_computation.136 | convolution fusion | flops 3227516928 | bytes 11550720 | tf_op jit(solution)/shard_map/dot_general | solution.py:32
  335.3 2.3 convolution_convert_fusion.2.da_ref
  337.6 17.3 %attend_back.2 = bf16[1024,1536]{1,0:T(8,128)(2,1)} custom-call(bf16[1024,1536]{1,0:T(8,128)(2,1)} %add_convert_fusion.3.qkv_ref, bf16[1024,512]{1,0:T(8,128)(2,1)} %convolution_convert_fusion.2.da_ref), custom_call_target="tpu_custom_call" | custom-call | flops 4294967296 | bytes 7340032 | tf_op jit(solution)/shard_map/attend_back/pallas_call | solution.py:110
  354.8 6.5 %fusion.76 = f32[1024,1024]{1,0:T(8,128)S(1)} fusion(bf16[1024,1536]{1,0:T(8,128)(2,1)} %attend_back.2, bf16[1536,1024]{1,0:T(8,128)(2,1)} %bitcast.122), kind=kOutput, calls=%fused_computation.145 | convolution fusion | flops 3221225472 | bytes 10485760 | tf_op jit(solution)/shard_map/dot_general | solution.py:32
  361.4 4.4 convert_reduce_fusion.4
  365.8 2.7 fusion.51
  368.5 3.0 fusion.39
  371.5 6.9 %convolution_add_fusion = f32[1536,1024]{1,0:T(8,128)S(1)} fusion(f32[1536,1024]{1,0:T(8,128)} %collective-permute-done.6, bf16[1024,1536]{1,0:T(8,128)(2,1)S(1)} %copy-done.15, bf16[1024,1024]{1,0:T(8,128)(2,1)S(1)} %bitcast.105, f32[1024]{0:T(1024)S(1)} %copy-done.39, f32[1024]{0:T(1024)S(1)} %copy-done.33, f32[1024]{0:T(1024)S(1)} %copy-done.30, ...), kind=kOutput, calls=%fused_computation.73 | convolution fusion | flops 3229089792 | bytes 17842176 | tf_op jit(solution)/shard_map/dot_general | solution.py:32
  378.4 6.2 %pad_maximum_fusion = f32[4,512,1024]{2,1,0:T(8,128)} fusion(f32[4,128,1024]{2,1,0:T(8,128)} %bitcast.130, f32[4,384,1024]{2,1,0:T(8,128)S(1)} %bitcast.116), kind=kLoop, calls=%fused_computation.34 | loop fusion | flops 2097152 | bytes 16777216 | tf_op jit(solution)/shard_map/concatenate | solution.py:293
  384.7 1.5 copy-done.16
  386.2 2.9 copy.41
  389.1 4.0 all-to-all-start.2
  393.1 49.3 %all-to-all-done.2 = bf16[4,256,1024]{2,0,1:T(4,128)(2,1)S(1)} async-done(((bf16[4,256,1024]{2,0,1:T(4,128)(2,1)}), bf16[4,256,1024]{2,0,1:T(4,128)(2,1)S(1)}, u32[]{:S(2)}, u32[]{:S(2)}) %all-to-all-start.2) | async-done | bytes 2097184 | tf_op jit(solution)/shard_map/all_to_all | solution.py:201
  442.4 2.0 copy.42
  444.4 2.9 copy.43
  447.4 4.7 all-to-all-start.3
  452.2 2.6 convert_reduce_fusion.3
  456.2 55.3 %sum_over_tp.1 = f32[13,1024]{1,0:T(8,128)} custom-call(f32[13,1024]{1,0:T(8,128)} %reshape.261.vec_ref), custom_call_target="tpu_custom_call" | custom-call | tf_op jit(solution)/shard_map/sum_over_tp/pallas_call | solution.py:146
  515.9 1.5 fusion.69
  517.4 2.0 copy.44
  519.4 2.7 convert_element_type.234
  522.1 1.7 convert_bitcast_fusion
  523.9 1.3 copy.45
  525.2 1.7 convert.14
  (168 shorter events, 22.1 us)
Async XLA Ops:
  7.2 72.1 %all-gather.4.cloned.1.call-start = ((), (), s32[]{:S(2)}) async-start(), calls=%async_computation.7 | async-start | bytes 5406720 | tf_op jit(solution)/shard_map/all_gather | solution.py:177
  9.4 70.3 %copy-start.35 = (bf16[1024]{0:T(1024)(128)(2,1)S(1)}, bf16[1024]{0:T(1024)(128)(2,1)}, u32[]{:S(2)}) copy-start(bf16[1024]{0:T(1024)(128)(2,1)} %param.27) | copy-start | bytes 6148
  11.8 68.0 %all-to-all-start = ((bf16[8,4,32,1024]{3,2,1,0:T(8,128)(2,1)}), bf16[8,4,32,1024]{3,2,1,0:T(8,128)(2,1)S(1)}, u32[]{:S(2)}, u32[]{:S(2)}) async-start(bf16[8,4,32,1024]{3,2,1,0:T(8,128)(2,1)} %bitcast.125), calls=%async_computation | async-start | bytes 4194304 | tf_op jit(solution)/shard_map/all_to_all | solution.py:195
  17.8 115.6 %all-gather.6.cloned.1.call-start = ((), (), s32[]{:S(2)}) async-start(), calls=%async_computation.8 | async-start | bytes 5242880 | tf_op jit(solution)/shard_map/all_gather | solution.py:177
  79.3 27.7 %collective-permute-start = (bf16[2112,1024]{1,0:T(8,128)(2,1)}, bf16[2112,1024]{1,0:T(8,128)(2,1)}, u32[]{:S(2)}, u32[]{:S(2)}) collective-permute-start(bf16[2112,1024]{1,0:T(8,128)(2,1)} %all-gather.4.cloned.1.call-done), channel_id=1, source_target_pairs={{0,1},{1,0},{2,3},{3,2},{4,5},{5,4},{6,7},{7,6},{8,9},{9,8},{10,11... | collective-permute-start | bytes 12976136 | tf_op jit(solution)/shard_map/ppermute | solution.py:183
  79.8 1.3 copy-start.9
  81.1 3.6 copy-start.11
  83.1 30.3 %copy-start = (bf16[4,8,32,1024]{3,2,1,0:T(8,128)(2,1)}, bf16[4,8,32,1024]{3,2,1,0:T(8,128)(2,1)S(1)}, u32[]{:S(2)}) copy-start(bf16[4,8,32,1024]{3,2,1,0:T(8,128)(2,1)S(1)} %copy.39) | copy-start | bytes 6291460
  83.4 30.0 %copy-start.24 = (f32[1024]{0:T(1024)}, f32[1024]{0:T(1024)S(1)}, u32[]{:S(2)}) copy-start(f32[1024]{0:T(1024)S(1)} %broadcast_multiply_fusion.1) | copy-start | bytes 12292
  84.1 0.6 copy-start.27
  84.7 28.7 %copy-start.29 = (f32[1024]{0:T(1024)}, f32[1024]{0:T(1024)S(1)}, u32[]{:S(2)}) copy-start(f32[1024]{0:T(1024)S(1)} %fusion.56) | copy-start | bytes 12292
  84.7 2.1 copy-start.32
  84.8 2.1 copy-start.38
  84.8 17.5 %copy-start.20 = (bf16[4,128,1024]{2,1,0:T(8,128)(2,1)}, bf16[4,128,1024]{2,1,0:T(8,128)(2,1)S(1)}, u32[]{:S(2)}) copy-start(bf16[4,128,1024]{2,1,0:T(8,128)(2,1)S(1)} %slice.135) | copy-start | bytes 3145732
  108.2 20.5 %copy-start.22 = (bf16[4,128,1024]{2,1,0:T(8,128)(2,1)}, bf16[4,128,1024]{2,1,0:T(8,128)(2,1)S(1)}, u32[]{:S(2)}) copy-start(bf16[4,128,1024]{2,1,0:T(8,128)(2,1)S(1)} %slice.138) | copy-start | bytes 3145732
  133.4 6.6 %copy-start.26 = (f32[1024]{0:T(1024)S(1)}, f32[1024]{0:T(1024)}, u32[]{:S(2)}) copy-start(f32[1024]{0:T(1024)} %param.28) | copy-start | bytes 12292
  133.4 6.6 %copy-start.34 = (f32[1024]{0:T(1024)S(1)}, f32[1024]{0:T(1024)}, u32[]{:S(2)}) copy-start(f32[1024]{0:T(1024)} %param.29) | copy-start | bytes 12292
  133.4 7.6 %collective-permute-start.1 = (bf16[2048,1024]{0,1:T(8,128)(2,1)}, bf16[2048,1024]{0,1:T(8,128)(2,1)}, u32[]{:S(2)}, u32[]{:S(2)}) collective-permute-start(bf16[2048,1024]{0,1:T(8,128)(2,1)} %all-gather.6.cloned.1.call-done), channel_id=1, source_target_pairs={{0,1},{1,0},{2,3},{3,2},{4,5},{5,4},{6,7},{7,6},{8,9},{9,8},{10,11... | collective-permute-start | bytes 12582920 | tf_op jit(solution)/shard_map/ppermute | solution.py:183
  133.5 31.1 %all-to-all-start.1 = ((bf16[8,4,32,1024]{3,2,1,0:T(8,128)(2,1)}), bf16[8,4,32,1024]{3,2,1,0:T(8,128)(2,1)}, u32[]{:S(2)}, u32[]{:S(2)}) async-start(bf16[8,4,32,1024]{3,2,1,0:T(8,128)(2,1)} %bitcast.126), calls=%async_computation.1 | async-start | bytes 4194304 | tf_op jit(solution)/shard_map/all_to_all | solution.py:195
  138.2 80.6 %all-gather.8.cloned.1.call-start = ((), (), s32[]{:S(2)}) async-start(), calls=%async_computation.9 | async-start | bytes 5242880 | tf_op jit(solution)/shard_map/all_gather | solution.py:177
  140.8 1.3 copy-start.17
  164.6 2.8 copy-start.42
  166.6 7.6 %copy-start.5 = (bf16[4,8,32,1024]{3,2,1,0:T(8,128)(2,1)}, bf16[4,8,32,1024]{3,2,1,0:T(8,128)(2,1)S(1)}, u32[]{:S(2)}) copy-start(bf16[4,8,32,1024]{3,2,1,0:T(8,128)(2,1)S(1)} %copy.40) | copy-start | bytes 6291460
  174.2 14.1 %collective-permute-start.2 = (f32[2048,1024]{1,0:T(8,128)}, f32[2048,1024]{1,0:T(8,128)}, u32[]{:S(2)}, u32[]{:S(2)}) collective-permute-start(f32[2048,1024]{1,0:T(8,128)} %fusion.72), channel_id=1, source_target_pairs={{0,1},{1,0},{2,3},{3,2},{4,5},{5,4},{6,7},{7,6},{8,9},{9,8},{10,11... | collective-permute-start | bytes 25165832 | tf_op jit(solution)/shard_map/ppermute | solution.py:183
  175.3 344.1 %reduce-scatter.8.cloned.1.call-start = ((), (), s32[]{:S(2)}) async-start(), calls=%async_computation.12 | async-start | bytes 10485760 | tf_op jit(solution)/shard_map/reduce_scatter | solution.py:180
  176.1 12.2 %copy-start.6 = (bf16[4,8,32,1024]{3,2,1,0:T(8,128)(2,1)S(1)}, bf16[4,8,32,1024]{3,2,1,0:T(8,128)(2,1)}, u32[]{:S(2)}) copy-start(bf16[4,8,32,1024]{3,2,1,0:T(8,128)(2,1)} %copy-done.5) | copy-start | bytes 6291460
  183.6 4.8 copy-start.44
  218.8 14.7 %collective-permute-start.3 = (bf16[2048,1024]{1,0:T(8,128)(2,1)}, bf16[2048,1024]{1,0:T(8,128)(2,1)}, u32[]{:S(2)}, u32[]{:S(2)}) collective-permute-start(bf16[2048,1024]{1,0:T(8,128)(2,1)} %all-gather.8.cloned.1.call-done), channel_id=1, source_target_pairs={{0,1},{1,0},{2,3},{3,2},{4,5},{5,4},{6,7},{7,6},{8,9},{9,8},{10,11... | collective-permute-start | bytes 12582920 | tf_op jit(solution)/shard_map/ppermute | solution.py:183
  219.7 302.4 %reduce-scatter.6.cloned.1.call-start = ((), (), s32[]{:S(2)}) async-start(), calls=%async_computation.11 | async-start | bytes 10485760 | tf_op jit(solution)/shard_map/reduce_scatter | solution.py:180
  220.2 13.3 %copy-start.7 = (bf16[4,8,32,1024]{3,2,1,0:T(8,128)(2,1)S(1)}, bf16[4,8,32,1024]{3,2,1,0:T(8,128)(2,1)}, u32[]{:S(2)}) copy-start(bf16[4,8,32,1024]{3,2,1,0:T(8,128)(2,1)} %copy-done.5) | copy-start | bytes 6291460
  220.2 13.3 %copy-start.46 = (bf16[1024,2048]{1,0:T(8,128)(2,1)S(1)}, bf16[1024,2048]{1,0:T(8,128)(2,1)}, u32[]{:S(2)}) copy-start(bf16[1024,2048]{1,0:T(8,128)(2,1)} %get-tuple-element.119) | copy-start | bytes 12582916
  233.5 30.9 %copy-start.41 = (bf16[1024,2048]{1,0:T(8,128)(2,1)}, bf16[1024,2048]{1,0:T(8,128)(2,1)S(1)}, u32[]{:S(2)}) copy-start(bf16[1024,2048]{1,0:T(8,128)(2,1)S(1)} %get-tuple-element.102) | copy-start | bytes 12582916
  233.5 13.0 %copy-start.18 = (bf16[1024,1024]{1,0:T(8,128)(2,1)S(1)}, bf16[1024,1024]{1,0:T(8,128)(2,1)}, u32[]{:S(2)}) copy-start(bf16[1024,1024]{1,0:T(8,128)(2,1)} %copy-done.17) | copy-start | bytes 6291460
  246.5 4.7 copy-start.36
  251.2 13.2 %collective-permute-start.4 = (f32[2048,1024]{1,0:T(8,128)S(1)}, f32[2048,1024]{1,0:T(8,128)S(1)}, u32[]{:S(2)}, u32[]{:S(2)}) collective-permute-start(f32[2048,1024]{1,0:T(8,128)S(1)} %fusion.73), channel_id=1, source_target_pairs={{0,1},{1,0},{2,3},{3,2},{4,5},{5,4},{6,7},{7,6},{8,9},{9,8},{10,11... | collective-permute-start | bytes 25165832 | tf_op jit(solution)/shard_map/ppermute | solution.py:183
  271.6 253.6 %reduce-scatter.4.cloned.1.call-start = ((), (), s32[]{:S(2)}) async-start(), calls=%async_computation.10 | async-start | bytes 10485760 | tf_op jit(solution)/shard_map/reduce_scatter | solution.py:180
  271.9 9.5 %copy-start.37 = (bf16[2048,1024]{1,0:T(8,128)(2,1)S(1)}, bf16[2048,1024]{1,0:T(8,128)(2,1)}, u32[]{:S(2)}) copy-start(bf16[2048,1024]{1,0:T(8,128)(2,1)} %all-gather.8.cloned.1.call-done) | copy-start | bytes 12582916
  271.9 9.5 %copy-start.45 = (bf16[1024,2048]{1,0:T(8,128)(2,1)S(1)}, bf16[1024,2048]{1,0:T(8,128)(2,1)}, u32[]{:S(2)}) copy-start(bf16[1024,2048]{1,0:T(8,128)(2,1)} %copy-done.44) | copy-start | bytes 12582916
  281.4 5.3 copy-start.43
  295.2 4.1 copy-start.8
  299.3 2.4 copy-start.19
  301.6 5.5 %copy-start.2 = (bf16[1024,1024]{1,0:T(8,128)(2,1)}, bf16[1024,1024]{1,0:T(8,128)(2,1)S(1)}, u32[]{:S(2)}) copy-start(bf16[1024,1024]{1,0:T(8,128)(2,1)S(1)} %get-tuple-element.104) | copy-start | bytes 6291460
  301.7 2.0 copy-start.23
  302.9 4.2 copy-start.40
  303.0 4.2 collective-permute-start.5
  309.8 17.6 %copy-start.1 = (bf16[4,8,32,1024]{3,2,1,0:T(8,128)(2,1)S(1)}, bf16[4,8,32,1024]{3,2,1,0:T(8,128)(2,1)}, u32[]{:S(2)}) copy-start(bf16[4,8,32,1024]{3,2,1,0:T(8,128)(2,1)} %copy-done) | copy-start | bytes 6291460
  309.8 17.6 %copy-start.25 = (f32[1024]{0:T(1024)S(1)}, f32[1024]{0:T(1024)}, u32[]{:S(2)}) copy-start(f32[1024]{0:T(1024)} %copy-done.24) | copy-start | bytes 12292
  309.8 17.6 %copy-start.30 = (f32[1024]{0:T(1024)S(1)}, f32[1024]{0:T(1024)}, u32[]{:S(2)}) copy-start(f32[1024]{0:T(1024)} %copy-done.29) | copy-start | bytes 12292
  309.8 17.6 %copy-start.33 = (f32[1024]{0:T(1024)S(1)}, f32[1024]{0:T(1024)}, u32[]{:S(2)}) copy-start(f32[1024]{0:T(1024)} %param.19) | copy-start | bytes 12292
  309.8 17.6 %copy-start.39 = (f32[1024]{0:T(1024)S(1)}, f32[1024]{0:T(1024)}, u32[]{:S(2)}) copy-start(f32[1024]{0:T(1024)} %param.20) | copy-start | bytes 12292
  327.4 7.9 %copy-start.3 = (bf16[1024,1024]{1,0:T(8,128)(2,1)S(1)}, bf16[1024,1024]{1,0:T(8,128)(2,1)}, u32[]{:S(2)}) copy-start(bf16[1024,1024]{1,0:T(8,128)(2,1)} %copy-done.2) | copy-start | bytes 6291460
  327.4 7.9 %copy-start.21 = (bf16[4,128,1024]{2,1,0:T(8,128)(2,1)S(1)}, bf16[4,128,1024]{2,1,0:T(8,128)(2,1)}, u32[]{:S(2)}) copy-start(bf16[4,128,1024]{2,1,0:T(8,128)(2,1)} %copy-done.20) | copy-start | bytes 3145732
  335.2 36.3 %collective-permute-start.6 = (f32[1536,1024]{1,0:T(8,128)}, f32[1536,1024]{1,0:T(8,128)}, u32[]{:S(2)}, u32[]{:S(2)}) collective-permute-start(f32[1536,1024]{1,0:T(8,128)} %fusion.62), channel_id=1, source_target_pairs={{0,1},{1,0},{2,3},{3,2},{4,5},{5,4},{6,7},{7,6},{8,9},{9,8},{10,11... | collective-permute-start | bytes 18874376 | tf_op jit(solution)/shard_map/ppermute | solution.py:183
  354.8 6.5 %copy-start.12 = (bf16[4,384,1024]{2,1,0:T(8,128)(2,1)S(1)}, bf16[4,384,1024]{2,1,0:T(8,128)(2,1)}, u32[]{:S(2)}) copy-start(bf16[4,384,1024]{2,1,0:T(8,128)(2,1)} %slice.136) | copy-start | bytes 9437188
  354.8 6.5 %copy-start.13 = (bf16[1024,1536]{1,0:T(8,128)(2,1)S(1)}, bf16[1024,1536]{1,0:T(8,128)(2,1)}, u32[]{:S(2)}) copy-start(bf16[1024,1536]{1,0:T(8,128)(2,1)} %attend_back.3) | copy-start | bytes 9437188
  361.3 4.4 copy-start.28
  365.8 2.8 copy-start.4
  368.5 3.0 copy-start.15
  384.6 1.6 copy-start.16
  389.1 53.3 %all-to-all-start.2 = ((bf16[4,256,1024]{2,0,1:T(4,128)(2,1)}), bf16[4,256,1024]{2,0,1:T(4,128)(2,1)S(1)}, u32[]{:S(2)}, u32[]{:S(2)}) async-start(bf16[4,256,1024]{2,0,1:T(4,128)(2,1)} %copy.41), calls=%async_computation.2 | async-start | bytes 4194304 | tf_op jit(solution)/shard_map/all_to_all | solution.py:201
  442.4 2.0 copy-start.10
  447.4 70.0 %all-to-all-start.3 = ((bf16[4,256,1024]{2,0,1:T(4,128)(2,1)}), bf16[4,256,1024]{2,0,1:T(4,128)(2,1)S(1)}, u32[]{:S(2)}, u32[]{:S(2)}) async-start(bf16[4,256,1024]{2,0,1:T(4,128)(2,1)} %copy.43), calls=%async_computation.3 | async-start | bytes 4194304 | tf_op jit(solution)/shard_map/all_to_all | solution.py:201
  452.1 2.9 copy-start.14
  452.1 3.4 copy-start.31
Sparse Core Ops, SparseCore 0:
  11.9 67.3 all-gather.3
  80.8 44.0 all-gather.5
  175.4 43.3 all-gather.7
  221.0 76.8 reduce-scatter.7
  300.1 76.1 reduce-scatter.5
  384.8 124.6 reduce-scatter.3
